TPU v7x, 256 devices: a whole 4x4x8 slice. The times are simulated.
256 devices in a mesh: dp: 2 (over y_hi), tm: 32 (over z, y_lo, core), rows: 4 (over x).
Axes of the slice: x: 4, y: 4 (y_hi: 2, y_lo: 2; y = y_hi * 2 + y_lo), z: 8, core: 2. Of those that a mesh axis runs over, the one named last changes fastest.
Arguments:
- clips: bfloat16 [2, 64, 4, 128, 256], P('dp', 'tm', 'rows'), may hold values from -12 to 12
- weight: bfloat16 [3, 3, 3, 256, 256], replicated, may hold values from -0.078125 to 0.078125
- bias: float32 [256], replicated, may hold values from -1 to 1
- head: float32 [256], replicated, may hold values from -4 to 4
Outputs:
- grad_weight: float32 [3, 3, 3, 256, 256], replicated
- grad_bias: float32 [256], replicated
- grad_head: float32 [256], replicated
All inputs are finite; a program needn't handle non-finite values.
Results may differ from a plain program's by a relative error of at most 0.0003.
Values may be sent and summed in bfloat16 or wider, within the bound.
No kernel may reach another device: no remote copies, remote signals or barrier semaphores. Data moves between devices by JAX's collectives and lax.ppermute only.
A program may use at most 128 MiB of HBM per device.

v0:
```python
import jax
import jax.numpy as jnp
from jax import lax
from jax.sharding import PartitionSpec as P

penalty_weight = 0.01


def padded_2(value, sides, width):
    for axis, dim in sides:
        count, length = (lax.axis_size(axis), value.shape[dim])
        up = [(i, (i + 1) % count) for i in range(count - 1)]
        down = [(j, i) for i, j in up]
        last = lax.slice_in_dim(value, length - width, length, axis=dim)
        initial = lax.slice_in_dim(value, 0, width, axis=dim)
        before = lax.ppermute(last, axis, up)
        after = lax.ppermute(initial, axis, down)
        value = jnp.concatenate([before, value, after], axis=dim)
    return value


def conv_offsets(padded, weight, transpose):
    nclip, tpad, rpad, wpad, chans = padded.shape
    frames, rowsn, cols = (tpad - 2, rpad - 2, wpad - 2)
    total = jnp.zeros((nclip * frames * rowsn * cols, weight.shape[4]), jnp.float32)
    for a in range(3):
        for b in range(3):
            for d in range(3):
                if transpose:
                    piece = padded[
                        :, 2 - a : 2 - a + frames, 2 - b : 2 - b + rowsn, 2 - d : 2 - d + cols
                    ]
                    total = total + lax.dot_general(
                        piece.reshape(-1, chans),
                        weight[a, b, d],
                        (((1,), (1,)), ((), ())),
                        preferred_element_type=jnp.float32,
                    )
                else:
                    piece = padded[:, a : a + frames, b : b + rowsn, d : d + cols]
                    total = total + jnp.dot(
                        piece.reshape(-1, chans),
                        weight[a, b, d],
                        preferred_element_type=jnp.float32,
                    )
    return total.reshape(nclip, frames, rowsn, cols, -1)


def correlate(padded, right):
    nclip, tpad, rpad, wpad, chans = padded.shape
    frames, rowsn, cols = (tpad - 2, rpad - 2, wpad - 2)
    right_rows = right.reshape(-1, right.shape[-1])
    blocks = []
    for a in range(3):
        for b in range(3):
            for d in range(3):
                piece = padded[:, a : a + frames, b : b + rowsn, d : d + cols].reshape(-1, chans)
                blocks.append(
                    lax.dot_general(
                        piece,
                        right_rows,
                        (((0,), (0,)), ((), ())),
                        preferred_element_type=jnp.float32,
                    )
                )
    return jnp.stack(blocks).reshape(3, 3, 3, chans, right.shape[-1])


def pad_columns(field):
    return jnp.pad(field, ((0, 0), (0, 0), (0, 0), (1, 1), (0, 0)))


def per_device(clips, weight, bias, head):
    clip_pad = pad_columns(padded_2(clips, (("tm", 1), ("rows", 2)), 1))
    pre = conv_offsets(clip_pad, weight, False) + bias
    sig = jax.nn.sigmoid(pre)
    slope = sig * (1.0 + pre * (1.0 - sig))
    curve = sig * (1.0 - sig) * (2.0 + pre * (1.0 - 2.0 * sig))
    score_grad = (head * slope).astype(jnp.bfloat16)
    score_pad = pad_columns(padded_2(score_grad, (("tm", 1), ("rows", 2)), 1))
    input_grad = conv_offsets(score_pad, weight, True).astype(jnp.bfloat16)
    grad_pad = pad_columns(padded_2(input_grad, (("tm", 1), ("rows", 2)), 1))
    back_grad = penalty_weight * conv_offsets(grad_pad, weight, False)
    pre_grad = back_grad * head * curve
    pre_grad_b = pre_grad.astype(jnp.bfloat16)
    local_weight = penalty_weight * correlate(grad_pad, score_grad) + correlate(
        clip_pad, pre_grad_b
    )
    local_bias = jnp.sum(pre_grad, axis=(0, 1, 2, 3))
    local_head = jnp.sum(back_grad * slope, axis=(0, 1, 2, 3))
    grad_weight, grad_bias, grad_head = lax.psum(
        (local_weight, local_bias, local_head), ("dp", "tm", "rows")
    )
    return (grad_weight, grad_bias, grad_head)


def solution(mesh):
    return jax.shard_map(
        per_device,
        mesh=mesh,
        in_specs=(P("dp", "tm", "rows", None, None), P(), P(), P()),
        out_specs=(P(), P(), P()),
        check_vma=False,
    )
```

profile of v0, /device:TPU:1, one launch (start us, length us, event | category | flops | bytes accessed | tf_op | source)
XLA Modules:
  0.0 534.8 jit_solution(14304096221612865775)
XLA Ops:
  8.3 4.6 collective-permute-start
  12.8 1.9 collective-permute-start.1
  14.8 3.6 collective-permute-done.1
  18.5 3.1 collective-permute-start.2
  25.7 4.1 collective-permute-done.3
  33.3 2.0 fusion.385
  37.0 1.7 copy.24
  38.6 1.8 fusion.392
  40.4 1.7 copy.23
  42.1 1.8 fusion.251
  43.9 1.8 fusion.245
  45.7 1.7 copy.25
  49.0 1.7 copy.29
  52.3 1.8 fusion.221
  54.1 1.8 fusion.391
  60.9 1.8 fusion.209
  64.3 1.7 copy.35
  67.6 1.7 copy.37
  71.0 1.8 fusion.188
  74.4 1.7 copy.40
  77.7 1.8 fusion.176
  81.2 1.7 copy.43
  82.8 1.7 copy.46
  84.5 1.7 copy.47
  87.8 1.8 fusion.154
  89.6 1.7 copy.48
  101.1 3.4 collective-permute-start.4
  104.5 1.9 collective-permute-start.5
  106.4 3.6 collective-permute-done.5
  110.1 3.1 collective-permute-start.6
  114.6 2.8 collective-permute-done.6
  117.4 4.1 collective-permute-done.7
  128.5 3.5 collective-permute-start.8
  132.0 1.9 collective-permute-start.9
  133.9 4.3 collective-permute-done.9
  138.3 2.8 collective-permute-start.10
  144.6 4.1 collective-permute-done.11
  150.3 2.0 fusion.384
  157.9 3.0 copy-done.5
  160.9 1.8 copy.55
  162.7 1.9 fusion.247
  164.6 1.7 copy.57
  166.2 1.8 fusion.388
  169.7 1.8 fusion.242
  171.5 1.7 copy.58
  176.5 1.7 copy.63
  178.2 1.9 fusion.217
  180.0 1.8 fusion.387
  186.8 1.8 fusion.205
  199.5 1.7 copy.68
  201.2 1.7 copy.69
  204.5 1.8 fusion.184
  206.3 1.7 copy.70
  208.0 1.7 copy.72
  209.7 1.7 copy.74
  211.3 1.8 fusion.172
  216.4 1.7 copy.77
  218.1 1.7 copy.78
  221.4 1.8 fusion.150
  223.2 1.7 copy.79
  237.8 4.1 multiply_add_fusion
  241.9 82.1 %all-reduce.3 = (f32[256]{0:T(256)}, f32[256]{0:T(256)}) all-reduce(f32[256]{0:T(256)S(1)} %get-tuple-element.5, f32[256]{0:T(256)S(1)} %get-tuple-element.61), channel_id=1, replica_groups=mesh['dp'=2,'tm'=32,'rows'=4] {'dp','tm','rows'}, use_global_device_ids=true, to_apply=%region_2.3 | all-reduce | flops 512 | bytes 4096 | tf_op jit(solution)/shard_map/psum | solution.py:91
  324.0 197.2 %all-reduce.6.cloned.1.call-done = f32[3,3,3,256,256]{4,3,2,1,0:T(8,128)} async-done(((f32[3,3,3,256,256]{4,3,2,1,0:T(8,128)}), f32[3,3,3,256,256]{4,3,2,1,0:T(8,128)}) %all-reduce.6.cloned.1.call-update) | async-done | bytes 7077904 | tf_op jit(solution)/shard_map/psum | solution.py:91
  521.2 6.7 %copy.139 = f32[3,3,3,256,256]{4,3,2,1,0:T(8,128)} copy(f32[3,3,3,256,256]{4,3,2,1,0:T(8,128)} %all-reduce.6.cloned.1.call-done) | data formatting | bytes 14155776
  (295 shorter events, 97.9 us)
Async XLA Ops:
  7.2 514.0 %all-reduce.6.cloned.1.call-start = ((), (), s32[]{:S(2)}) async-start(), calls=%async_computation | async-start | bytes 14155776 | tf_op jit(solution)/shard_map/psum | solution.py:91
  8.3 6.5 %collective-permute-start = (bf16[1,1,1,128,256]{3,4,1,2,0:T(8,128)(2,1)S(1)}, bf16[1,1,1,128,256]{3,4,1,2,0:T(8,128)(2,1)S(1)}, u32[]{:S(2)}, u32[]{:S(2)}) collective-permute-start(bf16[1,1,1,128,256]{3,4,1,2,0:T(8,128)(2,1)S(1)} %get-tuple-element.90), channel_id=1, source_target_pairs={{0,4},{4,8},{8,12},{12,16},{16,20},{20,24},{24,28},{28,32},{32,36}... | collective-permute-start | bytes 196616 | tf_op jit(solution)/shard_map/ppermute | solution.py:16
  12.8 5.6 %collective-permute-start.1 = (bf16[1,1,1,128,256]{3,4,1,2,0:T(8,128)(2,1)S(1)}, bf16[1,1,1,128,256]{3,4,1,2,0:T(8,128)(2,1)S(1)}, u32[]{:S(2)}, u32[]{:S(2)}) collective-permute-start(bf16[1,1,1,128,256]{3,4,1,2,0:T(8,128)(2,1)S(1)} %get-tuple-element.91), channel_id=1, source_target_pairs={{4,0},{8,4},{12,8},{16,12},{20,16},{24,20},{28,24},{32,28},{36,32}... | collective-permute-start | bytes 196616 | tf_op jit(solution)/shard_map/ppermute | solution.py:17
  18.5 7.3 %collective-permute-start.2 = (bf16[1,4,1,128,256]{3,4,1,2,0:T(8,128)(2,1)S(1)}, bf16[1,4,1,128,256]{3,4,1,2,0:T(8,128)(2,1)S(1)}, u32[]{:S(2)}, u32[]{:S(2)}) collective-permute-start(bf16[1,4,1,128,256]{3,4,1,2,0:T(8,128)(2,1)S(1)} %pad_maximum_fusion), channel_id=1, source_target_pairs={{0,1},{1,2},{2,3},{4,5},{5,6},{6,7},{8,9},{9,10},{10,11},{12,13},{... | collective-permute-start | bytes 786440 | tf_op jit(solution)/shard_map/ppermute | solution.py:16
  21.6 8.2 %collective-permute-start.3 = (bf16[1,4,1,128,256]{3,4,1,2,0:T(8,128)(2,1)S(1)}, bf16[1,4,1,128,256]{3,4,1,2,0:T(8,128)(2,1)S(1)}, u32[]{:S(2)}, u32[]{:S(2)}) collective-permute-start(bf16[1,4,1,128,256]{3,4,1,2,0:T(8,128)(2,1)S(1)} %pad_maximum_fusion), channel_id=1, source_target_pairs={{1,0},{2,1},{3,2},{5,4},{6,5},{7,6},{9,8},{10,9},{11,10},{13,12},{... | collective-permute-start | bytes 786440 | tf_op jit(solution)/shard_map/ppermute | solution.py:17
  22.9 6.9 %copy-start.16 = (bf16[1,2,1,128,256]{3,4,1,2,0:T(8,128)(2,1)}, bf16[1,2,1,128,256]{3,4,1,2,0:T(8,128)(2,1)S(1)}, u32[]{:S(2)}) copy-start(bf16[1,2,1,128,256]{3,4,1,2,0:T(8,128)(2,1)S(1)} %get-tuple-element.88) | copy-start | bytes 393220
  23.0 6.9 %copy-start.18 = (bf16[1,2,1,128,256]{3,4,1,2,0:T(8,128)(2,1)}, bf16[1,2,1,128,256]{3,4,1,2,0:T(8,128)(2,1)S(1)}, u32[]{:S(2)}) copy-start(bf16[1,2,1,128,256]{3,4,1,2,0:T(8,128)(2,1)S(1)} %get-tuple-element.89) | copy-start | bytes 393220
  25.7 4.1 copy-start.8
  33.3 8.8 %copy-start = (bf16[3,3,3,256,256]{4,3,2,1,0:T(8,128)(2,1)S(1)}, bf16[3,3,3,256,256]{4,3,2,1,0:T(8,128)(2,1)}, u32[]{:S(2)}) copy-start(bf16[3,3,3,256,256]{4,3,2,1,0:T(8,128)(2,1)} %param.5) | copy-start | bytes 10616836
  91.3 6.0 %copy-start.20 = (f32[256,256]{1,0:T(8,128)S(1)}, f32[256,256]{1,0:T(8,128)}, u32[]{:S(2)}) copy-start(f32[256,256]{1,0:T(8,128)} %fusion.221) | copy-start | bytes 786436
  91.3 6.0 %copy-start.43 = (bf16[1,2,1,128,256]{4,3,1,2,0:T(8,128)(2,1)S(1)}, bf16[1,2,1,128,256]{4,3,1,2,0:T(8,128)(2,1)}, u32[]{:S(2)}) copy-start(bf16[1,2,1,128,256]{4,3,1,2,0:T(8,128)(2,1)} %copy.30) | copy-start | bytes 393220
  91.3 6.2 %copy-start.34 = (bf16[1,2,1,128,256]{4,3,1,2,0:T(8,128)(2,1)S(1)}, bf16[1,2,1,128,256]{4,3,1,2,0:T(8,128)(2,1)}, u32[]{:S(2)}) copy-start(bf16[1,2,1,128,256]{4,3,1,2,0:T(8,128)(2,1)} %copy.32) | copy-start | bytes 393220
  91.3 6.4 %copy-start.23 = (f32[256,256]{1,0:T(8,128)S(1)}, f32[256,256]{1,0:T(8,128)}, u32[]{:S(2)}) copy-start(f32[256,256]{1,0:T(8,128)} %fusion.209) | copy-start | bytes 786436
  91.3 6.5 %copy-start.45 = (bf16[1,2,1,128,256]{4,3,1,2,0:T(8,128)(2,1)S(1)}, bf16[1,2,1,128,256]{4,3,1,2,0:T(8,128)(2,1)}, u32[]{:S(2)}) copy-start(bf16[1,2,1,128,256]{4,3,1,2,0:T(8,128)(2,1)} %copy.33) | copy-start | bytes 393220
  91.3 6.7 %copy-start.36 = (bf16[1,2,1,128,256]{4,3,1,2,0:T(8,128)(2,1)S(1)}, bf16[1,2,1,128,256]{4,3,1,2,0:T(8,128)(2,1)}, u32[]{:S(2)}) copy-start(bf16[1,2,1,128,256]{4,3,1,2,0:T(8,128)(2,1)} %copy.35) | copy-start | bytes 393220
  92.7 5.5 %copy-start.14 = (bf16[1,2,1,128,256]{4,3,2,1,0:T(8,128)(2,1)S(1)}, bf16[1,2,1,128,256]{4,3,2,1,0:T(8,128)(2,1)}, u32[]{:S(2)}) copy-start(bf16[1,2,1,128,256]{4,3,2,1,0:T(8,128)(2,1)} %param.4) | copy-start | bytes 393220
  93.8 4.6 copy-start.32
  95.0 3.7 copy-start.31
  96.1 2.8 copy-start.21
  96.1 2.8 copy-start.42
  97.3 1.8 copy-start.33
  97.5 1.8 copy-start.22
  98.6 2.0 copy-start.1
  98.6 2.0 copy-start.50
  98.6 2.1 copy-start.52
  98.6 2.1 copy-start.54
  98.6 2.0 copy-start.55
  101.0 5.5 %copy-start.48 = (f32[256,256]{1,0:T(8,128)}, f32[256,256]{1,0:T(8,128)S(1)}, u32[]{:S(2)}) copy-start(f32[256,256]{1,0:T(8,128)S(1)} %get-tuple-element.93) | copy-start | bytes 786436
  101.1 5.3 collective-permute-start.4
  104.5 5.6 %collective-permute-start.5 = (bf16[1,1,1,128,256]{4,3,1,2,0:T(8,128)(2,1)S(1)}, bf16[1,1,1,128,256]{4,3,1,2,0:T(8,128)(2,1)S(1)}, u32[]{:S(2)}, u32[]{:S(2)}) collective-permute-start(bf16[1,1,1,128,256]{4,3,1,2,0:T(8,128)(2,1)S(1)} %get-tuple-element.87), channel_id=1, source_target_pairs={{4,0},{8,4},{12,8},{16,12},{20,16},{24,20},{28,24},{32,28},{36,32}... | collective-permute-start | bytes 196616 | tf_op jit(solution)/shard_map/ppermute | solution.py:17
  110.1 7.3 %collective-permute-start.6 = (bf16[1,4,1,128,256]{4,3,1,2,0:T(8,128)(2,1)S(1)}, bf16[1,4,1,128,256]{4,3,1,2,0:T(8,128)(2,1)S(1)}, u32[]{:S(2)}, u32[]{:S(2)}) collective-permute-start(bf16[1,4,1,128,256]{4,3,1,2,0:T(8,128)(2,1)S(1)} %pad_maximum_fusion.1), channel_id=1, source_target_pairs={{0,1},{1,2},{2,3},{4,5},{5,6},{6,7},{8,9},{9,10},{10,11},{12,13},{... | collective-permute-start | bytes 786440 | tf_op jit(solution)/shard_map/ppermute | solution.py:16
  113.3 8.2 %collective-permute-start.7 = (bf16[1,4,1,128,256]{4,3,1,2,0:T(8,128)(2,1)S(1)}, bf16[1,4,1,128,256]{4,3,1,2,0:T(8,128)(2,1)S(1)}, u32[]{:S(2)}, u32[]{:S(2)}) collective-permute-start(bf16[1,4,1,128,256]{4,3,1,2,0:T(8,128)(2,1)S(1)} %pad_maximum_fusion.1), channel_id=1, source_target_pairs={{1,0},{2,1},{3,2},{5,4},{6,5},{7,6},{9,8},{10,9},{11,10},{13,12},{... | collective-permute-start | bytes 786440 | tf_op jit(solution)/shard_map/ppermute | solution.py:17
  128.3 26.6 %copy-start.12 = (bf16[256,256]{1,0:T(8,128)(2,1)}, bf16[256,256]{1,0:T(8,128)(2,1)S(1)}, u32[]{:S(2)}) copy-start(bf16[256,256]{1,0:T(8,128)(2,1)S(1)} %fusion.87) | copy-start | bytes 393220
  128.5 5.4 %collective-permute-start.8 = (bf16[1,1,1,128,256]{3,4,1,2,0:T(8,128)(2,1)S(1)}, bf16[1,1,1,128,256]{3,4,1,2,0:T(8,128)(2,1)S(1)}, u32[]{:S(2)}, u32[]{:S(2)}) collective-permute-start(bf16[1,1,1,128,256]{3,4,1,2,0:T(8,128)(2,1)S(1)} %get-tuple-element.82), channel_id=1, source_target_pairs={{0,4},{4,8},{8,12},{12,16},{16,20},{20,24},{24,28},{28,32},{32,36}... | collective-permute-start | bytes 196616 | tf_op jit(solution)/shard_map/ppermute | solution.py:16
  132.0 6.3 %collective-permute-start.9 = (bf16[1,1,1,128,256]{3,4,1,2,0:T(8,128)(2,1)S(1)}, bf16[1,1,1,128,256]{3,4,1,2,0:T(8,128)(2,1)S(1)}, u32[]{:S(2)}, u32[]{:S(2)}) collective-permute-start(bf16[1,1,1,128,256]{3,4,1,2,0:T(8,128)(2,1)S(1)} %get-tuple-element.83), channel_id=1, source_target_pairs={{4,0},{8,4},{12,8},{16,12},{20,16},{24,20},{28,24},{32,28},{36,32}... | collective-permute-start | bytes 196616 | tf_op jit(solution)/shard_map/ppermute | solution.py:17
  138.3 6.3 %collective-permute-start.10 = (bf16[1,4,1,128,256]{3,4,1,2,0:T(8,128)(2,1)S(1)}, bf16[1,4,1,128,256]{3,4,1,2,0:T(8,128)(2,1)S(1)}, u32[]{:S(2)}, u32[]{:S(2)}) collective-permute-start(bf16[1,4,1,128,256]{3,4,1,2,0:T(8,128)(2,1)S(1)} %pad_maximum_fusion.2), channel_id=1, source_target_pairs={{0,1},{1,2},{2,3},{4,5},{5,6},{6,7},{8,9},{9,10},{10,11},{12,13},{... | collective-permute-start | bytes 786440 | tf_op jit(solution)/shard_map/ppermute | solution.py:16
  141.1 7.6 %collective-permute-start.11 = (bf16[1,4,1,128,256]{3,4,1,2,0:T(8,128)(2,1)S(1)}, bf16[1,4,1,128,256]{3,4,1,2,0:T(8,128)(2,1)S(1)}, u32[]{:S(2)}, u32[]{:S(2)}) collective-permute-start(bf16[1,4,1,128,256]{3,4,1,2,0:T(8,128)(2,1)S(1)} %pad_maximum_fusion.2), channel_id=1, source_target_pairs={{1,0},{2,1},{3,2},{5,4},{6,5},{7,6},{9,8},{10,9},{11,10},{13,12},{... | collective-permute-start | bytes 786440 | tf_op jit(solution)/shard_map/ppermute | solution.py:17
  144.6 11.7 %copy-start.11 = (bf16[1,4,1,128,256]{3,4,1,2,0:T(8,128)(2,1)}, bf16[1,4,1,128,256]{3,4,1,2,0:T(8,128)(2,1)S(1)}, u32[]{:S(2)}) copy-start(bf16[1,4,1,128,256]{3,4,1,2,0:T(8,128)(2,1)S(1)} %collective-permute-done.10) | copy-start | bytes 786436
  148.7 8.8 %copy-start.10 = (bf16[1,4,1,128,256]{3,4,1,2,0:T(8,128)(2,1)}, bf16[1,4,1,128,256]{3,4,1,2,0:T(8,128)(2,1)S(1)}, u32[]{:S(2)}) copy-start(bf16[1,4,1,128,256]{3,4,1,2,0:T(8,128)(2,1)S(1)} %collective-permute-done.11) | copy-start | bytes 786436
  157.9 3.0 copy-start.5
  160.9 31.1 %copy-start.2 = (bf16[3,3,3,256,256]{4,3,2,1,0:T(8,128)(2,1)S(1)}, bf16[3,3,3,256,256]{4,3,2,1,0:T(8,128)(2,1)}, u32[]{:S(2)}) copy-start(bf16[3,3,3,256,256]{4,3,2,1,0:T(8,128)(2,1)} %param.5) | copy-start | bytes 10616836
  192.0 5.8 %copy-start.24 = (f32[256,256]{1,0:T(8,128)S(1)}, f32[256,256]{1,0:T(8,128)}, u32[]{:S(2)}) copy-start(f32[256,256]{1,0:T(8,128)} %fusion.217) | copy-start | bytes 786436
  192.0 5.9 %copy-start.46 = (bf16[1,2,1,128,256]{4,3,1,2,0:T(8,128)(2,1)S(1)}, bf16[1,2,1,128,256]{4,3,1,2,0:T(8,128)(2,1)}, u32[]{:S(2)}) copy-start(bf16[1,2,1,128,256]{4,3,1,2,0:T(8,128)(2,1)} %copy.62) | copy-start | bytes 393220
  192.0 6.1 %copy-start.40 = (bf16[1,2,1,128,256]{4,3,1,2,0:T(8,128)(2,1)S(1)}, bf16[1,2,1,128,256]{4,3,1,2,0:T(8,128)(2,1)}, u32[]{:S(2)}) copy-start(bf16[1,2,1,128,256]{4,3,1,2,0:T(8,128)(2,1)} %copy.64) | copy-start | bytes 393220
  192.0 6.3 %copy-start.26 = (f32[256,256]{1,0:T(8,128)S(1)}, f32[256,256]{1,0:T(8,128)}, u32[]{:S(2)}) copy-start(f32[256,256]{1,0:T(8,128)} %fusion.205) | copy-start | bytes 786436
  192.0 6.3 %copy-start.47 = (bf16[1,2,1,128,256]{4,3,1,2,0:T(8,128)(2,1)S(1)}, bf16[1,2,1,128,256]{4,3,1,2,0:T(8,128)(2,1)}, u32[]{:S(2)}) copy-start(bf16[1,2,1,128,256]{4,3,1,2,0:T(8,128)(2,1)} %copy.65) | copy-start | bytes 393220
  192.0 6.5 %copy-start.41 = (bf16[1,2,1,128,256]{4,3,1,2,0:T(8,128)(2,1)S(1)}, bf16[1,2,1,128,256]{4,3,1,2,0:T(8,128)(2,1)}, u32[]{:S(2)}) copy-start(bf16[1,2,1,128,256]{4,3,1,2,0:T(8,128)(2,1)} %copy.67) | copy-start | bytes 393220
  193.4 5.3 copy-start.13
  224.9 4.8 copy-start.25
  224.9 6.1 %copy-start.39 = (bf16[1,2,1,128,256]{4,3,1,2,0:T(8,128)(2,1)S(1)}, bf16[1,2,1,128,256]{4,3,1,2,0:T(8,128)(2,1)}, u32[]{:S(2)}) copy-start(bf16[1,2,1,128,256]{4,3,1,2,0:T(8,128)(2,1)} %copy.75) | copy-start | bytes 393220
  224.9 6.3 %copy-start.27 = (bf16[1,2,1,128,256]{4,3,1,2,0:T(8,128)(2,1)S(1)}, bf16[1,2,1,128,256]{4,3,1,2,0:T(8,128)(2,1)}, u32[]{:S(2)}) copy-start(bf16[1,2,1,128,256]{4,3,1,2,0:T(8,128)(2,1)} %copy.76) | copy-start | bytes 393220
  224.9 6.5 %copy-start.38 = (bf16[1,2,1,128,256]{4,3,1,2,0:T(8,128)(2,1)S(1)}, bf16[1,2,1,128,256]{4,3,1,2,0:T(8,128)(2,1)}, u32[]{:S(2)}) copy-start(bf16[1,2,1,128,256]{4,3,1,2,0:T(8,128)(2,1)} %copy.77) | copy-start | bytes 393220
  224.9 6.7 %copy-start.37 = (bf16[1,2,1,128,256]{4,3,1,2,0:T(8,128)(2,1)S(1)}, bf16[1,2,1,128,256]{4,3,1,2,0:T(8,128)(2,1)}, u32[]{:S(2)}) copy-start(bf16[1,2,1,128,256]{4,3,1,2,0:T(8,128)(2,1)} %copy.78) | copy-start | bytes 393220
  226.2 5.6 %copy-start.49 = (f32[256,256]{1,0:T(8,128)S(1)}, f32[256,256]{1,0:T(8,128)}, u32[]{:S(2)}) copy-start(f32[256,256]{1,0:T(8,128)} %copy-done.48) | copy-start | bytes 786436
  226.2 5.6 %copy-start.51 = (f32[256,256]{1,0:T(8,128)S(1)}, f32[256,256]{1,0:T(8,128)}, u32[]{:S(2)}) copy-start(f32[256,256]{1,0:T(8,128)} %fusion.150) | copy-start | bytes 786436
  226.2 5.6 %copy-start.53 = (bf16[1,2,1,128,256]{4,3,1,2,0:T(8,128)(2,1)S(1)}, bf16[1,2,1,128,256]{4,3,1,2,0:T(8,128)(2,1)}, u32[]{:S(2)}) copy-start(bf16[1,2,1,128,256]{4,3,1,2,0:T(8,128)(2,1)} %copy.79) | copy-start | bytes 393220
  229.7 2.5 copy-start.4
  229.7 2.7 copy-start.9
  231.1 1.8 copy-start.19
  231.5 2.0 copy-start.7
  231.8 6.0 %slice-start = ((s8[7077888]{0:T(1024)(128)(4,1)}), s8[4194304]{0:T(1024)(128)(4,1)S(1)}, s32[]{:S(2)}) async-start(s8[7077888]{0:T(1024)(128)(4,1)} %bitcast.898), calls=%async_computation.1 | async-start | bytes 8388608
  232.1 2.7 copy-start.15
  234.0 2.7 copy-start.17
  234.4 3.4 slice-start.1
  (7 other events, 10.7 us)
Sparse Core Ops, SparseCore 0:
  242.1 279.1 all-reduce.5
where the time goes:
time: 538 us; the launch traced here: 535 us
  waiting for transfers between devices  226 us (42%)
  local copies, waits for them, and re-layouts  108 us (20%)
  blocking collectives  82.1 us (15%)
  matrix products  65.3 us (12%)
  starting transfers between devices  30.4 us (6%)
  between operations  15.9 us (3%)
  other arithmetic  7.71 us (1%)
    psum x1, waiting for transfers between devices, per_device(): lax.psum((local_weight, local_bias, local_head), ('dp', 'tm', 'rows'))  197 us
    psum x1, blocking collectives, per_device(): lax.psum((local_weight, local_bias, local_head), ('dp', 'tm', 'rows'))  82.1 us
    dot_general x54, matrix products, conv_offsets(): jnp.dot(piece.reshape(-1, chans), weight[a, b, d], preferred_element_type...  48.5 us
    slice x29, local copies, waits for them, and re-layouts, correlate(): piece = padded[:, a:a + frames, b:b + rowsn, d:d + cols].reshape(-1, chans)  47.1 us
    slice x29, local copies, waits for them, and re-layouts, conv_offsets(): piece = padded[:, a:a + frames, b:b + rowsn, d:d + cols]  46.9 us
    ppermute x6, waiting for transfers between devices, padded_2(): after = lax.ppermute(initial, axis, down)  23.9 us
    ppermute x6, starting transfers between devices, padded_2(): before = lax.ppermute(last, axis, up)  20.6 us
    unnamed x118, local copies, waits for them, and re-layouts  13.2 us
  transfers between devices with their start and end apart: 13, of which 10 were waited for; matrix products, arithmetic and copies ran while one was open for 1% of the time, Pallas kernels for 0%

commit v1 on v0

v1 whole, which is shorter than its diff:
```python
import functools

import jax
import jax.numpy as jnp
from jax import lax
from jax.experimental import pallas as pl
from jax.experimental.pallas import tpu as pltpu
from jax.sharding import Mesh, PartitionSpec as P

PENALTY = 0.01
F32 = jnp.float32
BF16 = jnp.bfloat16
ROWS = 4
COLS = 128
CH = 256
PART = CH // ROWS
TILES = 27 * PART // 8
PIECE = 7
PIECES = 32
ALL = ("yh", "z", "yl", "c", "x")
PLANE = ("yh", "z", "yl")
CHAIN = ("z", "yl", "c")


def moved(fn):
    pairs = []
    for yh in range(2):
        for z in range(8):
            for yl in range(2):
                for c in range(2):
                    for x in range(4):
                        y2, z2, c2, x2 = fn(yh * 2 + yl, z, c, x)
                        y2, z2, x2 = y2 % 4, z2 % 8, x2 % 4
                        src = (((yh * 8 + z) * 2 + yl) * 2 + c) * 4 + x
                        dst = ((((y2 // 2) * 8 + z2) * 2 + y2 % 2) * 2 + c2) * 4 + x2
                        pairs.append((src, dst))
    return pairs


def permute(value, fn):
    return lax.ppermute(value, ALL, moved(fn))


def along_x(step):
    return lambda y, z, c, x: (y, z, c, x + step)


def swap_core(y, z, c, x):
    return (y, z, 1 - c, x)


def split_first(step):
    return lambda y, z, c, x: (y, z, c, x + step) if c else (y + step, z, c, x)


def split_second(step):
    return lambda y, z, c, x: (y + step, z, c, x) if c else (y, z, c, x + step)


def chain(value, step):
    count = 32
    pairs = [(i, i + step) for i in range(count) if 0 <= i + step < count]
    return lax.ppermute(value, CHAIN, pairs)


VMEM = pl.BlockSpec(memory_space=pltpu.VMEM)
SMEM = pl.BlockSpec(memory_space=pltpu.SMEM)
ANY = pl.BlockSpec(memory_space=pl.ANY)


def params(limit=60 << 20):
    return pltpu.CompilerParams(vmem_limit_bytes=limit)


def cost(flops, nbytes):
    return pl.CostEstimate(flops=int(flops), bytes_accessed=int(nbytes), transcendentals=0)


def gather_rows_kernel(pos_ref, own, below, above, across, first, second):
    x = pos_ref[0]
    for shift, ref in ((0, own), (3, below), (1, above), (2, across)):
        row = lax.rem(x + shift, 4)
        first[row] = ref[0]
        second[row] = ref[1]


def gather_rows(pos, own, below, above, across):
    out = jax.ShapeDtypeStruct((ROWS, COLS, CH), BF16)
    return pl.pallas_call(
        gather_rows_kernel,
        out_shape=(out, out),
        in_specs=[SMEM] + [VMEM] * 4,
        out_specs=(VMEM, VMEM),
        compiler_params=params(),
        cost_estimate=cost(1e6, 1 << 20),
        name="gather_rows",
    )(pos, own, below, above, across)


def spread_columns(frames, spread):
    row = lax.broadcasted_iota(jnp.int32, (COLS, CH), 0)
    for f, ref in enumerate(frames):
        for r in range(ROWS):
            slab = ref[r]
            wide = slab.astype(F32)
            left = jnp.where(row == 0, 0.0, pltpu.roll(wide, 1, axis=0))
            right = jnp.where(row == COLS - 1, 0.0, pltpu.roll(wide, COLS - 1, axis=0))
            spread[f, r, :, 0:CH] = left.astype(BF16)
            spread[f, r, :, CH : 2 * CH] = slab
            spread[f, r, :, 2 * CH : 3 * CH] = right.astype(BF16)


TAPS = [(1, 1), (0, 1), (2, 1), (0, 0), (1, 0), (2, 0), (0, 2), (1, 2), (2, 2)]


def start_weights(w_hbm, w_buf, sems):
    for n, (a, b) in enumerate(TAPS):
        pltpu.make_async_copy(w_hbm.at[a, b], w_buf.at[n], sems.at[n]).start()


def convolve(spread, w_hbm, w_buf, sems, acc):
    for n, (a, b) in enumerate(TAPS):
        pltpu.make_async_copy(w_hbm.at[a, b], w_buf.at[n], sems.at[n]).wait()
        rows = ROWS if b == 1 else ROWS - 1
        src = 1 if b == 2 else 0
        dst = 1 if b == 0 else 0
        piece = spread[a : a + 2, src : src + rows].reshape(2 * rows * COLS, 3 * CH)
        term = jnp.dot(piece, w_buf[n], preferred_element_type=F32)
        term = term.reshape(2, rows, COLS, CH)
        if n == 0:
            acc[...] = term
        else:
            acc[:, dst : dst + rows] += term


def forward_kernel(prev, first, second, follow, w_hbm, bias, head, pre, g0, g1, spread, w_buf, sems):
    start_weights(w_hbm, w_buf, sems)
    spread_columns((prev, first, second, follow), spread)
    convolve(spread, w_hbm, w_buf, sems, pre)
    for f, out in ((0, g0), (1, g1)):
        for r in range(ROWS):
            value = pre[f, r] + bias[...]
            pre[f, r] = value
            sig = jax.nn.sigmoid(value)
            slope = sig * (1.0 + value * (1.0 - sig))
            out[r] = (head[...] * slope).astype(BF16)


def transpose_kernel(prev, first, second, follow, w_hbm, g0, g1, spread, acc, w_buf, sems):
    start_weights(w_hbm, w_buf, sems)
    spread_columns((prev, first, second, follow), spread)
    convolve(spread, w_hbm, w_buf, sems, acc)
    for f, out in ((0, g0), (1, g1)):
        out[...] = acc[f].astype(BF16)


def conv_scratch():
    return dict(
        spread=pltpu.VMEM((4, ROWS, COLS, 3 * CH), BF16),
        acc=pltpu.VMEM((2, ROWS, COLS, CH), F32),
        w_buf=pltpu.VMEM((9, 3 * CH, CH), BF16),
        sems=pltpu.SemaphoreType.DMA((9,)),
    )


FRAME = jax.ShapeDtypeStruct((ROWS, COLS, CH), BF16)
CONV_FLOPS = 2 * 1024 * 27 * CH * CH


def forward(frames, w9, bias, head):
    s = conv_scratch()
    return pl.pallas_call(
        forward_kernel,
        out_shape=(jax.ShapeDtypeStruct((2, ROWS, COLS, CH), F32), FRAME, FRAME),
        in_specs=[VMEM] * 4 + [ANY, VMEM, VMEM],
        out_specs=(VMEM, VMEM, VMEM),
        scratch_shapes=[s["spread"], s["w_buf"], s["sems"]],
        compiler_params=params(),
        cost_estimate=cost(CONV_FLOPS, 6 << 20),
        name="forward",
    )(*frames, w9, bias, head)


def transposed(frames, w9):
    s = conv_scratch()
    return pl.pallas_call(
        transpose_kernel,
        out_shape=(FRAME, FRAME),
        in_specs=[VMEM] * 4 + [ANY],
        out_specs=(VMEM, VMEM),
        scratch_shapes=[s["spread"], s["acc"], s["w_buf"], s["sems"]],
        compiler_params=params(),
        cost_estimate=cost(CONV_FLOPS, 5 << 20),
        name="transposed",
    )(*frames, w9)


def part_transposed(frames, x, turned):
    chan = lax.broadcasted_iota(jnp.int32, (PART, CH), 1)
    want = lax.broadcasted_iota(jnp.int32, (PART, CH), 0) + x * PART
    pick = jnp.where(chan == want, 1.0, 0.0).astype(BF16)
    width = ROWS * COLS
    lane = lax.rem(lax.broadcasted_iota(jnp.int32, (PART, width), 1), COLS)
    for f, ref in enumerate(frames):
        flat = ref[...].reshape(width, CH)
        mid = lax.dot_general(pick, flat, (((1,), (1,)), ((), ())), preferred_element_type=F32)
        left = jnp.where(lane == 0, 0.0, pltpu.roll(mid, 1, axis=1))
        right = jnp.where(lane == COLS - 1, 0.0, pltpu.roll(mid, width - 1, axis=1))
        at = slice(f * width, (f + 1) * width)
        turned[0:PART, at] = left.astype(BF16)
        turned[PART : 2 * PART, at] = mid.astype(BF16)
        turned[2 * PART : 3 * PART, at] = right.astype(BF16)


def correlate(turned, grads, b):
    width = ROWS * COLS
    rows = ROWS if b == 1 else ROWS - 1
    src = 1 if b == 2 else 0
    dst = 1 if b == 0 else 0
    left = []
    for a in range(3):
        parts = []
        for f in range(2):
            at = (a + f) * width + src * COLS
            parts.append(turned[:, at : at + rows * COLS])
        left.append(jnp.concatenate(parts, axis=1))
    left = jnp.concatenate(left, axis=0)
    right = [g[dst : dst + rows].reshape(rows * COLS, CH) for g in grads]
    return jnp.dot(left, jnp.concatenate(right, axis=0), preferred_element_type=F32)


def backward_kernel(
    pos, i0, i1, i2, i3, c0, c1, c2, c3, s0, s1, pre, w_hbm, head, out,
    spread, acc, w_buf, turn_i, turn_c, pgb, sems,
):
    x = pos[0]
    core = pos[1]
    start_weights(w_hbm, w_buf, sems)
    grads = (i0, i1, i2, i3)
    spread_columns(grads, spread)
    part_transposed(grads, x, turn_i)
    part_transposed((c0, c1, c2, c3), x, turn_c)
    convolve(spread, w_hbm, w_buf, sems, acc)
    sum_bias = jnp.zeros((8, CH), F32)
    sum_head = jnp.zeros((8, CH), F32)
    for f in range(2):
        for r in range(ROWS):
            back = PENALTY * acc[f, r]
            value = pre[f, r]
            sig = jax.nn.sigmoid(value)
            slope = sig * (1.0 + value * (1.0 - sig))
            curve = sig * (1.0 - sig) * (2.0 + value * (1.0 - 2.0 * sig))
            grad = back * head[...] * curve
            pgb[f, r] = grad.astype(BF16)
            sum_bias = sum_bias + jnp.sum(grad.reshape(COLS // 8, 8, CH), axis=0)
            sum_head = sum_head + jnp.sum((back * slope).reshape(COLS // 8, 8, CH), axis=0)
    total_bias = jnp.sum(sum_bias, axis=0, keepdims=True)
    total_head = jnp.sum(sum_head, axis=0, keepdims=True)
    row = lax.broadcasted_iota(jnp.int32, (8, CH), 0)
    small = jnp.where(row == 0, total_bias, jnp.where(row == 1, total_head, 0.0))
    slots = [jnp.where(core == h, 1, 0) for h in range(2)]
    for b in range(3):
        block = PENALTY * correlate(turn_i, (s0, s1), b) + correlate(turn_c, (pgb.at[0], pgb.at[1]), b)
        for a in range(3):
            for d in range(3):
                k = (a * 3 + b) * 3 + d
                tap = block[(a * 3 + d) * PART : (a * 3 + d + 1) * PART]
                for h in range(2):
                    half = tap[:, h * 128 : (h + 1) * 128].reshape(PART // 8, 8, 128)
                    out[slots[h], k * 8 : (k + 1) * 8] = half
    for h in range(2):
        out[slots[h], TILES] = small[:, h * 128 : (h + 1) * 128]
        out[slots[h], TILES + 1 :] = jnp.zeros((PIECE * PIECES - TILES - 1, 8, 128), F32)


def backward(pos, grads, clips, score, pre, w9, head):
    s = conv_scratch()
    return pl.pallas_call(
        backward_kernel,
        out_shape=jax.ShapeDtypeStruct((2, PIECE * PIECES, 8, 128), F32),
        in_specs=[SMEM] + [VMEM] * 11 + [ANY, VMEM],
        out_specs=VMEM,
        scratch_shapes=[
            s["spread"],
            s["acc"],
            s["w_buf"],
            pltpu.VMEM((3 * PART, 4 * ROWS * COLS), BF16),
            pltpu.VMEM((3 * PART, 4 * ROWS * COLS), BF16),
            pltpu.VMEM((2, ROWS, COLS, CH), BF16),
            s["sems"],
        ],
        compiler_params=params(),
        cost_estimate=cost(CONV_FLOPS * 1.6, 10 << 20),
        name="backward",
    )(pos, *grads, *clips, *score, pre, w9, head)


def relative(distance):
    return jnp.where(distance == 0, 0, jnp.where(distance == 3, 1, distance + 1))


def assemble_kernel(pos, mine, other, out, small):
    x, core, y = pos[0], pos[1], pos[2]
    part = pl.program_id(0)
    at_x = relative(lax.rem(part - x + 4, 4))
    for ref, held in ((mine, core), (other, 1 - core)):
        lane = pl.ds(pl.multiple_of(held * 128, 128), 128)
        for row in range(4):
            at_y = relative(lax.rem(row - y + 4, 4))
            place = jnp.where(held == 0, at_x * 4 + at_y, at_y * 4 + at_x)
            for z in range(8):
                piece = ((row // 2) * 8 + z) * 2 + row % 2
                for j in range(PIECE):
                    tile = piece * PIECE + j
                    if tile < TILES:
                        out[tile // 8, 0, tile % 8, :, lane] = ref[place, z, j]
                    elif tile == TILES:
                        small[:, lane] = ref[place, z, j]


def assemble(pos, mine, other):
    whole = pl.BlockSpec((16, 8, PIECE, 8, 128), lambda i: (0, 0, 0, 0, 0))
    return pl.pallas_call(
        assemble_kernel,
        grid=(ROWS,),
        out_shape=(
            jax.ShapeDtypeStruct((27, ROWS, 8, 8, CH), F32),
            jax.ShapeDtypeStruct((8, CH), F32),
        ),
        in_specs=[SMEM, VMEM, VMEM],
        out_specs=(
            pl.BlockSpec((27, 1, 8, 8, CH), lambda i: (0, i, 0, 0, 0)),
            pl.BlockSpec((8, CH), lambda i: (0, 0)),
        ),
        compiler_params=params(),
        cost_estimate=cost(1e6, 15 << 20),
        name="assemble",
    )(pos, mine, other)


def ring_gather(value, plan):
    below = permute(value, plan(1))
    above = permute(value, plan(-1))
    half = value.shape[0] // 2
    across_low = permute(below[:half], plan(1))
    across_high = permute(above[half:], plan(-1))
    across = jnp.concatenate([across_low, across_high], axis=0)
    return jnp.stack([value, below, above, across])


def per_device(clips, weight, bias, head):
    x = lax.axis_index("x")
    core = lax.axis_index("c")
    y = lax.axis_index("yh") * 2 + lax.axis_index("yl")
    pos = jnp.stack([x, core, y]).astype(jnp.int32)
    own = clips.reshape(2, COLS, CH)
    below = permute(own, along_x(1))
    above = permute(own, along_x(-1))
    across = permute(own, along_x(2))
    w9 = weight.reshape(3, 3, 3 * CH, CH)
    turned = weight[::-1, ::-1, ::-1].swapaxes(3, 4).reshape(3, 3, 3 * CH, CH)
    bias = bias.reshape(1, CH)
    head = head.reshape(1, CH)

    def with_halo(first, second):
        return (chain(second, 1), first, second, chain(first, -1))

    clip_frames = with_halo(*gather_rows(pos, own, below, above, across))
    pre, s0, s1 = forward(clip_frames, w9, bias, head)
    grad_frames = with_halo(*transposed(with_halo(s0, s1), turned))
    terms = backward(pos, grad_frames, clip_frames, (s0, s1), pre, w9, head)
    half = terms[1] + permute(terms[0], swap_core)
    pieces = lax.all_to_all(half.reshape(PIECES, PIECE, 8, 128), PLANE, 0, 0, tiled=True)
    piece = jnp.sum(pieces, axis=0)
    line = jnp.broadcast_to(piece[None], (8, PIECE, 8, 128))
    line = lax.all_to_all(line, "z", 0, 0, tiled=True)
    block = ring_gather(line, split_first)
    mine = ring_gather(block.reshape(32, PIECE, 8, 128), split_second)
    mine = mine.reshape(16, 8, PIECE, 8, 128)
    other = permute(mine, swap_core)
    grad_weight, small = assemble(pos, mine, other)
    return grad_weight.reshape(3, 3, 3, CH, CH), small[0], small[1]


def solution(mesh):
    fine = Mesh(mesh.devices.reshape(2, 8, 2, 2, 4), ALL)
    return jax.shard_map(
        per_device,
        mesh=fine,
        in_specs=(P("yh", CHAIN, "x", None, None), P(), P(), P()),
        out_specs=(P(), P(), P()),
        check_vma=False,
    )
```

time: 538 us -> 204 us (0.38)
  waiting for transfers between devices: 226 us -> 54.2 us
  local copies, waits for them, and re-layouts: 108 us -> 10.8 us
  matrix products: 65.3 us -> 0 us
  Pallas kernels: 0 us -> 42.7 us
  blocking collectives: 82.1 us -> 52.8 us
  between operations: 15.9 us -> 0.82 us
  starting transfers between devices: 30.4 us -> 39.8 us
  other arithmetic: 7.71 us -> 2.33 us
    psum x1 -> x0, waiting for transfers between devices: 197 us -> none  [per_device(): lax.psum((local_weight, local_bias, local_head), ('dp', 'tm', 'rows'))]
    slice x64 -> x5, local copies, waits for them, and re-layouts: 94.5 us -> 1.42 us  [the longest x1 1.34 us: per_device(): return (grad_weight.reshape(3, 3, 3, CH, CH), small[0], small[1])]
    psum x1 -> x0, blocking collectives: 82.1 us -> none  [per_device(): lax.psum((local_weight, local_bias, local_head), ('dp', 'tm', 'rows'))]
    dot_general x135 -> x0, matrix products: 65.3 us -> none  [the longest x54 48.5 us: conv_offsets(): jnp.dot(piece.reshape(-1, chans), weight[a, b, d], preferred_element_type...]
    all_to_all x0 -> x2, blocking collectives: none -> 52.8 us  [the longest x1 40.7 us: per_device(): lax.all_to_all(half.reshape(PIECES, PIECE, 8, 128), PLANE, 0, 0, tiled=True)]
    pallas_call x0 -> x5, Pallas kernels: none -> 42.7 us  [the longest x1 14.2 us: backward(): pl.pallas_call(backward_kernel, out_shape=jax.ShapeDtypeStruct((2, PIECE...]
    ppermute x12 -> x19, waiting for transfers between devices: 28.4 us -> 54.2 us  [the longest x13 42.4 us: permute(): return lax.ppermute(value, ALL, moved(fn))]
    unnamed x118 -> x16, local copies, waits for them, and re-layouts: 13.2 us -> 2.08 us
  transfers between devices with their start and end apart: 13 -> 19, of which waited for: 10 -> 15; matrix products, arithmetic and copies ran while one was open for 1% -> 3% of each run, Pallas kernels for 0% -> 0%
where the time goes in v1:
time: 204 us; the launch traced here: 203 us
  waiting for transfers between devices  54.2 us (27%)
  blocking collectives  52.8 us (26%)
  Pallas kernels  42.7 us (21%)
  starting transfers between devices  39.8 us (20%)
  local copies, waits for them, and re-layouts  10.8 us (5%)
  other arithmetic  2.33 us (1%)
    ppermute x13, waiting for transfers between devices, permute(): return lax.ppermute(value, ALL, moved(fn))  42.4 us
    all_to_all x1, blocking collectives, per_device(): lax.all_to_all(half.reshape(PIECES, PIECE, 8, 128), PLANE, 0, 0, tiled=True)  40.7 us
    ppermute x13, starting transfers between devices, permute(): return lax.ppermute(value, ALL, moved(fn))  24.1 us
    ppermute x6, starting transfers between devices, chain(): return lax.ppermute(value, CHAIN, pairs)  15.7 us
    pallas_call x1, Pallas kernels, backward(): pl.pallas_call(backward_kernel, out_shape=jax.ShapeDtypeStruct((2, PIECE...  14.2 us
    all_to_all x1, blocking collectives, per_device(): line = lax.all_to_all(line, 'z', 0, 0, tiled=True)  12.2 us
    ppermute x6, waiting for transfers between devices, chain(): return lax.ppermute(value, CHAIN, pairs)  11.8 us
    pallas_call x1, Pallas kernels, forward(): pl.pallas_call(forward_kernel, out_shape=(jax.ShapeDtypeStruct((2, ROWS,...  10.3 us
  transfers between devices with their start and end apart: 19, of which 15 were waited for; matrix products, arithmetic and copies ran while one was open for 3% of the time, Pallas kernels for 0%

profile of v1, /device:TPU:1, one launch (start us, length us, event | category | flops | bytes accessed | tf_op | source)
XLA Modules:
  0.0 203.4 jit_solution(13839668633243874130)
XLA Ops:
  0.6 3.6 %collective-permute-start.2 = (bf16[2,128,256]{2,1,0:T(8,128)(2,1)}, bf16[2,128,256]{2,1,0:T(8,128)(2,1)S(1)}, u32[]{:S(2)}, u32[]{:S(2)}) collective-permute-start(bf16[2,128,256]{2,1,0:T(8,128)(2,1)} %bitcast.46), channel_id=1, source_target_pairs={{0,2},{1,3},{2,0},{3,1},{4,6},{5,7},{6,4},{7,5},{8,10},{9,11},{10,... | collective-permute-start | bytes 393224 | tf_op jit(solution)/shard_map/ppermute | solution.py:41
  4.3 0.9 collective-permute-start.1
  5.1 0.6 collective-permute-start
  5.7 0.6 pad_add_fusion.pos_ref.pos
  6.4 0.5 collective-permute-done.2.across
  6.9 3.7 %collective-permute-done.1.above = bf16[2,128,256]{2,1,0:T(8,128)(2,1)S(1)} collective-permute-done((bf16[2,128,256]{2,1,0:T(8,128)(2,1)}, bf16[2,128,256]{2,1,0:T(8,128)(2,1)S(1)}, u32[]{:S(2)}, u32[]{:S(2)}) %collective-permute-start.1) | collective-permute-done | bytes 131104 | tf_op jit(solution)/shard_map/ppermute | solution.py:41
  10.5 2.2 %collective-permute-done.below = bf16[2,128,256]{2,1,0:T(8,128)(2,1)S(1)} collective-permute-done((bf16[2,128,256]{2,1,0:T(8,128)(2,1)}, bf16[2,128,256]{2,1,0:T(8,128)(2,1)S(1)}, u32[]{:S(2)}, u32[]{:S(2)}) %collective-permute-start) | collective-permute-done | bytes 131104 | tf_op jit(solution)/shard_map/ppermute | solution.py:41
  12.7 0.0 copy-done.1
  12.7 0.0 copy-done.2
  12.7 0.7 copy-done.3
  13.4 1.9 gather_rows.1
  15.3 3.1 %collective-permute-start.3 = (bf16[4,128,256]{2,1,0:T(8,128)(2,1)}, bf16[4,128,256]{2,1,0:T(8,128)(2,1)S(1)}, u32[]{:S(2)}, u32[]{:S(2)}) collective-permute-start(bf16[4,128,256]{2,1,0:T(8,128)(2,1)} %get-tuple-element.12.second.c2), channel_id=1, source_target_pairs={{0,4},{4,8},{8,12},{12,16},{16,20},{20,24},{24,28},{28,32},{32,36}... | collective-permute-start | bytes 786440 | tf_op jit(solution)/shard_map/ppermute | solution.py:63
  18.5 1.9 collective-permute-start.4
  20.4 1.7 collective-permute-done.3.prev.c0
  22.1 4.3 %collective-permute-done.4.follow.c3 = bf16[4,128,256]{2,1,0:T(8,128)(2,1)S(1)} collective-permute-done((bf16[4,128,256]{2,1,0:T(8,128)(2,1)}, bf16[4,128,256]{2,1,0:T(8,128)(2,1)S(1)}, u32[]{:S(2)}, u32[]{:S(2)}) %collective-permute-start.4) | collective-permute-done | bytes 262176 | tf_op jit(solution)/shard_map/ppermute | solution.py:63
  26.4 0.0 copy-done.4
  26.4 0.7 copy-done.5
  27.1 10.3 %forward.1 = (f32[2,4,128,256]{3,2,1,0:T(8,128)}, bf16[4,128,256]{2,1,0:T(8,128)(2,1)}, bf16[4,128,256]{2,1,0:T(8,128)(2,1)}) custom-call(bf16[4,128,256]{2,1,0:T(8,128)(2,1)} %copy-done.4, bf16[4,128,256]{2,1,0:T(8,128)(2,1)} %get-tuple-element.13.first.c1, bf16[4,128,256]{2,1,0:T(8,128)(2,1)} %get-tuple-element.12.second.c2, ...), custom_call_target="tpu_custom_call" | custom-call | flops 3623878656 | bytes 6291456 | tf_op jit(solution)/shard_map/forward/pallas_call | solution.py:172
  37.3 1.9 collective-permute-start.5
  39.3 3.1 %collective-permute-start.6 = (bf16[4,128,256]{2,1,0:T(8,128)(2,1)}, bf16[4,128,256]{2,1,0:T(8,128)(2,1)}, u32[]{:S(2)}, u32[]{:S(2)}) collective-permute-start(bf16[4,128,256]{2,1,0:T(8,128)(2,1)} %get-tuple-element.15.first.s0), channel_id=1, source_target_pairs={{4,0},{8,4},{12,8},{16,12},{20,16},{24,20},{28,24},{32,28},{36,32}... | collective-permute-start | bytes 786440 | tf_op jit(solution)/shard_map/ppermute | solution.py:63
  42.4 2.2 %reverse_bitcast_fusion = bf16[3,3,3,256,256]{3,4,2,1,0:T(8,128)(2,1)S(1)} fusion(bf16[3,3,3,256,256]{4,3,2,1,0:T(8,128)(2,1)} %param.5), kind=kLoop, calls=%fused_computation.1 | loop fusion | bytes 7077888 | tf_op jit(solution)/shard_map/transpose | solution.py:361
  44.6 3.8 %copy.7 = bf16[3,3,3,256,256]{4,3,2,1,0:T(8,128)(2,1)} copy(bf16[3,3,3,256,256]{3,4,2,1,0:T(8,128)(2,1)S(1)} %reverse_bitcast_fusion) | data formatting | bytes 7077888 | tf_op jit(solution)/shard_map/transpose | solution.py:361
  48.5 0.0 collective-permute-done.5.prev
  48.5 0.0 collective-permute-done.6.follow
  48.5 9.7 %transposed.1 = (bf16[4,128,256]{2,1,0:T(8,128)(2,1)}, bf16[4,128,256]{2,1,0:T(8,128)(2,1)}) custom-call(bf16[4,128,256]{2,1,0:T(8,128)(2,1)} %collective-permute-done.5.prev, bf16[4,128,256]{2,1,0:T(8,128)(2,1)} %get-tuple-element.15.first.s0, bf16[4,128,256]{2,1,0:T(8,128)(2,1)} %get-tuple-element.14.second.s1, ...), custom_call_target="tpu_custom_call" | custom-call | flops 3623878656 | bytes 5242880 | tf_op jit(solution)/shard_map/transposed/pallas_call | solution.py:186
  58.2 3.5 %collective-permute-start.7 = (bf16[4,128,256]{2,1,0:T(8,128)(2,1)}, bf16[4,128,256]{2,1,0:T(8,128)(2,1)S(1)}, u32[]{:S(2)}, u32[]{:S(2)}) collective-permute-start(bf16[4,128,256]{2,1,0:T(8,128)(2,1)} %get-tuple-element.16.i2), channel_id=1, source_target_pairs={{0,4},{4,8},{8,12},{12,16},{16,20},{20,24},{24,28},{28,32},{32,36}... | collective-permute-start | bytes 786440 | tf_op jit(solution)/shard_map/ppermute | solution.py:63
  61.8 2.1 %collective-permute-start.8 = (bf16[4,128,256]{2,1,0:T(8,128)(2,1)}, bf16[4,128,256]{2,1,0:T(8,128)(2,1)S(1)}, u32[]{:S(2)}, u32[]{:S(2)}) collective-permute-start(bf16[4,128,256]{2,1,0:T(8,128)(2,1)} %get-tuple-element.17.i1), channel_id=1, source_target_pairs={{4,0},{8,4},{12,8},{16,12},{20,16},{24,20},{28,24},{32,28},{36,32}... | collective-permute-start | bytes 786440 | tf_op jit(solution)/shard_map/ppermute | solution.py:63
  63.9 1.5 collective-permute-done.7.i0
  65.4 4.3 %collective-permute-done.8.i3 = bf16[4,128,256]{2,1,0:T(8,128)(2,1)S(1)} collective-permute-done((bf16[4,128,256]{2,1,0:T(8,128)(2,1)}, bf16[4,128,256]{2,1,0:T(8,128)(2,1)S(1)}, u32[]{:S(2)}, u32[]{:S(2)}) %collective-permute-start.8) | collective-permute-done | bytes 262176 | tf_op jit(solution)/shard_map/ppermute | solution.py:63
  69.7 0.0 copy-done.6
  69.7 0.7 copy-done.7
  70.4 14.2 %backward.1 = f32[2,224,8,128]{3,2,1,0:T(8,128)} custom-call(s32[3]{0:T(128)} %pad_add_fusion.pos_ref.pos, bf16[4,128,256]{2,1,0:T(8,128)(2,1)} %copy-done.6, bf16[4,128,256]{2,1,0:T(8,128)(2,1)} %get-tuple-element.17.i1, bf16[4,128,256]{2,1,0:T(8,128)(2,1)} %get-tuple-element.16.i2, bf16[4,128,256]{2,1,0:T(8,128)(2,1)} %copy-done.7, ...), custom_call_target="tpu_custom_call" | custom-call | flops 5798205952 | bytes 10485760 | tf_op jit(solution)/shard_map/backward/pallas_call | solution.py:278
  84.6 1.2 slice_bitcast_fusion
  85.8 0.1 collective-permute-start.9
  85.9 2.5 %collective-permute-done.9 = f32[224,8,128]{2,1,0:T(8,128)S(1)} collective-permute-done((f32[224,8,128]{2,1,0:T(8,128)S(1)}, f32[224,8,128]{2,1,0:T(8,128)S(1)}, u32[]{:S(2)}, u32[]{:S(2)}) %collective-permute-start.9) | collective-permute-done | bytes 917536 | tf_op jit(solution)/shard_map/ppermute | solution.py:41
  88.4 1.3 fusion
  89.7 40.7 %all_to_all.10 = f32[32,7,8,128]{3,2,1,0:T(8,128)S(1)} all-to-all(f32[32,7,8,128]{3,2,1,0:T(8,128)S(1)} %bitcast.37), channel_id=1, replica_groups=mesh['yh'=2,'z'=8,'yl'=2,'c'=2,'x'=4] {'yh','z','yl'}, dimensions={0} | all-to-all | bytes 1835008 | tf_op jit(solution)/shard_map/all_to_all | solution.py:373
  130.3 0.1 reduce_sum.9
  130.4 12.2 %all_to_all.11 = f32[8,7,8,128]{3,2,1,0:T(8,128)S(1)} all-to-all(f32[8,7,8,128]{3,2,1,0:T(8,128)S(1)} %broadcast_in_dim.2), channel_id=1, replica_groups=mesh['yh'=2,'z'=8,'yl'=2,'c'=2,'x'=4] {'z'}, dimensions={0} | all-to-all | bytes 458752 | tf_op jit(solution)/shard_map/all_to_all | solution.py:376
  142.6 2.3 %collective-permute-start.11 = (f32[8,7,8,128]{3,2,1,0:T(8,128)S(1)}, f32[8,7,8,128]{3,2,1,0:T(8,128)S(1)}, u32[]{:S(2)}, u32[]{:S(2)}) collective-permute-start(f32[8,7,8,128]{3,2,1,0:T(8,128)S(1)} %all_to_all.11), channel_id=1, source_target_pairs={{0,136},{1,137},{2,138},{3,139},{4,7},{5,4},{6,5},{7,6},{8,0},{9,1... | collective-permute-start | bytes 688136 | tf_op jit(solution)/shard_map/ppermute | solution.py:41
  144.9 0.0 collective-permute-start.10
  144.9 3.0 %collective-permute-done.11 = f32[8,7,8,128]{3,2,1,0:T(8,128)S(1)} collective-permute-done((f32[8,7,8,128]{3,2,1,0:T(8,128)S(1)}, f32[8,7,8,128]{3,2,1,0:T(8,128)S(1)}, u32[]{:S(2)}, u32[]{:S(2)}) %collective-permute-start.11) | collective-permute-done | bytes 229408 | tf_op jit(solution)/shard_map/ppermute | solution.py:41
  147.9 3.2 %collective-permute-start.13 = (f32[4,7,8,128]{3,2,1,0:T(8,128)S(1)}, f32[4,7,8,128]{3,2,1,0:T(8,128)S(1)}, u32[]{:S(2)}, u32[]{:S(2)}) collective-permute-start(f32[4,7,8,128]{3,2,1,0:T(8,128)S(1)} %slice.35), channel_id=1, source_target_pairs={{0,136},{1,137},{2,138},{3,139},{4,7},{5,4},{6,5},{7,6},{8,0},{9,1... | collective-permute-start | bytes 344072 | tf_op jit(solution)/shard_map/ppermute | solution.py:41
  151.1 0.0 collective-permute-done.10
  151.1 0.1 collective-permute-start.12
  151.2 1.7 collective-permute-done.13
  152.9 3.2 %collective-permute-done.12 = f32[4,7,8,128]{3,2,1,0:T(8,128)S(1)} collective-permute-done((f32[4,7,8,128]{3,2,1,0:T(8,128)S(1)}, f32[4,7,8,128]{3,2,1,0:T(8,128)S(1)}, u32[]{:S(2)}, u32[]{:S(2)}) %collective-permute-start.12) | collective-permute-done | bytes 114720 | tf_op jit(solution)/shard_map/ppermute | solution.py:41
  156.1 0.1 pad_maximum_fusion.1
  156.1 1.2 collective-permute-start.15
  157.3 0.3 collective-permute-start.14
  157.7 11.1 %collective-permute-done.15 = f32[32,7,8,128]{3,2,1,0:T(8,128)S(1)} collective-permute-done((f32[32,7,8,128]{3,2,1,0:T(8,128)S(1)}, f32[32,7,8,128]{3,2,1,0:T(8,128)S(1)}, u32[]{:S(2)}, u32[]{:S(2)}) %collective-permute-start.15) | collective-permute-done | bytes 917536 | tf_op jit(solution)/shard_map/ppermute | solution.py:41
  168.8 2.4 %collective-permute-start.17 = (f32[16,7,8,128]{3,2,1,0:T(8,128)S(1)}, f32[16,7,8,128]{3,2,1,0:T(8,128)S(1)}, u32[]{:S(2)}, u32[]{:S(2)}) collective-permute-start(f32[16,7,8,128]{3,2,1,0:T(8,128)S(1)} %slice.37), channel_id=1, source_target_pairs={{0,3},{1,0},{2,1},{3,2},{4,140},{5,141},{6,142},{7,143},{8,11},{9,... | collective-permute-start | bytes 1376264 | tf_op jit(solution)/shard_map/ppermute | solution.py:41
  171.2 0.0 collective-permute-done.14
  171.2 0.1 collective-permute-start.16
  171.3 5.3 %collective-permute-done.17 = f32[16,7,8,128]{3,2,1,0:T(8,128)S(1)} collective-permute-done((f32[16,7,8,128]{3,2,1,0:T(8,128)S(1)}, f32[16,7,8,128]{3,2,1,0:T(8,128)S(1)}, u32[]{:S(2)}, u32[]{:S(2)}) %collective-permute-start.17) | collective-permute-done | bytes 458784 | tf_op jit(solution)/shard_map/ppermute | solution.py:41
  176.6 3.2 %collective-permute-done.16 = f32[16,7,8,128]{3,2,1,0:T(8,128)S(1)} collective-permute-done((f32[16,7,8,128]{3,2,1,0:T(8,128)S(1)}, f32[16,7,8,128]{3,2,1,0:T(8,128)S(1)}, u32[]{:S(2)}, u32[]{:S(2)}) %collective-permute-start.16) | collective-permute-done | bytes 458784 | tf_op jit(solution)/shard_map/ppermute | solution.py:41
  179.9 0.1 maximum_bitcast_fusion
  179.9 0.2 pad_maximum_fusion
  180.2 0.0 copy-start
  180.2 9.3 %collective-permute-start.18 = (f32[16,8,7,8,128]{4,3,2,1,0:T(8,128)S(1)}, f32[16,8,7,8,128]{4,3,2,1,0:T(8,128)}, u32[]{:S(2)}, u32[]{:S(2)}) collective-permute-start(f32[16,8,7,8,128]{4,3,2,1,0:T(8,128)S(1)} %bitcast.32), channel_id=1, source_target_pairs={{0,4},{1,5},{2,6},{3,7},{4,0},{5,1},{6,2},{7,3},{8,12},{9,13},{10,... | collective-permute-start | bytes 11010056 | tf_op jit(solution)/shard_map/ppermute | solution.py:41
  189.4 6.2 %collective-permute-done.18.other = f32[16,8,7,8,128]{4,3,2,1,0:T(8,128)} collective-permute-done((f32[16,8,7,8,128]{4,3,2,1,0:T(8,128)S(1)}, f32[16,8,7,8,128]{4,3,2,1,0:T(8,128)}, u32[]{:S(2)}, u32[]{:S(2)}) %collective-permute-start.18) | collective-permute-done | bytes 3670048 | tf_op jit(solution)/shard_map/ppermute | solution.py:41
  195.6 0.0 copy-done
  195.6 6.5 %assemble.1 = (f32[27,4,8,8,256]{4,3,2,1,0:T(8,128)}, f32[8,256]{1,0:T(8,128)}) custom-call(s32[3]{0:T(128)} %pad_add_fusion.pos_ref.pos, f32[16,8,7,8,128]{4,3,2,1,0:T(8,128)} %bitcast.33, f32[16,8,7,8,128]{4,3,2,1,0:T(8,128)} %collective-permute-done.18.other), custom_call_target="tpu_custom_call" | custom-call | flops 1000000 | bytes 15728640 | tf_op jit(solution)/shard_map/assemble/pallas_call | solution.py:323
  202.1 1.3 fusion.1
  (13 shorter events, 0.1 us)
Async XLA Ops:
  0.6 6.2 %collective-permute-start.2 = (bf16[2,128,256]{2,1,0:T(8,128)(2,1)}, bf16[2,128,256]{2,1,0:T(8,128)(2,1)S(1)}, u32[]{:S(2)}, u32[]{:S(2)}) collective-permute-start(bf16[2,128,256]{2,1,0:T(8,128)(2,1)} %bitcast.46), channel_id=1, source_target_pairs={{0,2},{1,3},{2,0},{3,1},{4,6},{5,7},{6,4},{7,5},{8,10},{9,11},{10,... | collective-permute-start | bytes 393224 | tf_op jit(solution)/shard_map/ppermute | solution.py:41
  4.3 6.2 %collective-permute-start.1 = (bf16[2,128,256]{2,1,0:T(8,128)(2,1)}, bf16[2,128,256]{2,1,0:T(8,128)(2,1)S(1)}, u32[]{:S(2)}, u32[]{:S(2)}) collective-permute-start(bf16[2,128,256]{2,1,0:T(8,128)(2,1)} %bitcast.47), channel_id=1, source_target_pairs={{0,3},{1,0},{2,1},{3,2},{4,7},{5,4},{6,5},{7,6},{8,11},{9,8},{10,9... | collective-permute-start | bytes 393224 | tf_op jit(solution)/shard_map/ppermute | solution.py:41
  5.1 7.6 %collective-permute-start = (bf16[2,128,256]{2,1,0:T(8,128)(2,1)}, bf16[2,128,256]{2,1,0:T(8,128)(2,1)S(1)}, u32[]{:S(2)}, u32[]{:S(2)}) collective-permute-start(bf16[2,128,256]{2,1,0:T(8,128)(2,1)} %bitcast.48), channel_id=1, source_target_pairs={{0,1},{1,2},{2,3},{3,0},{4,5},{5,6},{6,7},{7,4},{8,9},{9,10},{10,1... | collective-permute-start | bytes 393224 | tf_op jit(solution)/shard_map/ppermute | solution.py:41
  6.8 5.9 %copy-start.1 = (bf16[2,128,256]{2,1,0:T(8,128)(2,1)}, bf16[2,128,256]{2,1,0:T(8,128)(2,1)S(1)}, u32[]{:S(2)}) copy-start(bf16[2,128,256]{2,1,0:T(8,128)(2,1)S(1)} %collective-permute-done.2.across) | copy-start | bytes 393220
  10.5 2.2 %copy-start.2 = (bf16[2,128,256]{2,1,0:T(8,128)(2,1)}, bf16[2,128,256]{2,1,0:T(8,128)(2,1)S(1)}, u32[]{:S(2)}) copy-start(bf16[2,128,256]{2,1,0:T(8,128)(2,1)S(1)} %collective-permute-done.1.above) | copy-start | bytes 393220
  12.7 0.7 copy-start.3
  15.3 6.7 %collective-permute-start.3 = (bf16[4,128,256]{2,1,0:T(8,128)(2,1)}, bf16[4,128,256]{2,1,0:T(8,128)(2,1)S(1)}, u32[]{:S(2)}, u32[]{:S(2)}) collective-permute-start(bf16[4,128,256]{2,1,0:T(8,128)(2,1)} %get-tuple-element.12.second.c2), channel_id=1, source_target_pairs={{0,4},{4,8},{8,12},{12,16},{16,20},{20,24},{24,28},{28,32},{32,36}... | collective-permute-start | bytes 786440 | tf_op jit(solution)/shard_map/ppermute | solution.py:63
  18.5 7.9 %collective-permute-start.4 = (bf16[4,128,256]{2,1,0:T(8,128)(2,1)}, bf16[4,128,256]{2,1,0:T(8,128)(2,1)S(1)}, u32[]{:S(2)}, u32[]{:S(2)}) collective-permute-start(bf16[4,128,256]{2,1,0:T(8,128)(2,1)} %get-tuple-element.13.first.c1), channel_id=1, source_target_pairs={{4,0},{8,4},{12,8},{16,12},{20,16},{24,20},{28,24},{32,28},{36,32}... | collective-permute-start | bytes 786440 | tf_op jit(solution)/shard_map/ppermute | solution.py:63
  22.1 4.3 %copy-start.4 = (bf16[4,128,256]{2,1,0:T(8,128)(2,1)}, bf16[4,128,256]{2,1,0:T(8,128)(2,1)S(1)}, u32[]{:S(2)}) copy-start(bf16[4,128,256]{2,1,0:T(8,128)(2,1)S(1)} %collective-permute-done.3.prev.c0) | copy-start | bytes 786436
  26.4 0.7 copy-start.5
  37.3 11.1 %collective-permute-start.5 = (bf16[4,128,256]{2,1,0:T(8,128)(2,1)}, bf16[4,128,256]{2,1,0:T(8,128)(2,1)}, u32[]{:S(2)}, u32[]{:S(2)}) collective-permute-start(bf16[4,128,256]{2,1,0:T(8,128)(2,1)} %get-tuple-element.14.second.s1), channel_id=1, source_target_pairs={{0,4},{4,8},{8,12},{12,16},{16,20},{20,24},{24,28},{28,32},{32,36}... | collective-permute-start | bytes 786440 | tf_op jit(solution)/shard_map/ppermute | solution.py:63
  39.3 9.2 %collective-permute-start.6 = (bf16[4,128,256]{2,1,0:T(8,128)(2,1)}, bf16[4,128,256]{2,1,0:T(8,128)(2,1)}, u32[]{:S(2)}, u32[]{:S(2)}) collective-permute-start(bf16[4,128,256]{2,1,0:T(8,128)(2,1)} %get-tuple-element.15.first.s0), channel_id=1, source_target_pairs={{4,0},{8,4},{12,8},{16,12},{20,16},{24,20},{28,24},{32,28},{36,32}... | collective-permute-start | bytes 786440 | tf_op jit(solution)/shard_map/ppermute | solution.py:63
  58.2 7.2 %collective-permute-start.7 = (bf16[4,128,256]{2,1,0:T(8,128)(2,1)}, bf16[4,128,256]{2,1,0:T(8,128)(2,1)S(1)}, u32[]{:S(2)}, u32[]{:S(2)}) collective-permute-start(bf16[4,128,256]{2,1,0:T(8,128)(2,1)} %get-tuple-element.16.i2), channel_id=1, source_target_pairs={{0,4},{4,8},{8,12},{12,16},{16,20},{20,24},{24,28},{28,32},{32,36}... | collective-permute-start | bytes 786440 | tf_op jit(solution)/shard_map/ppermute | solution.py:63
  61.8 7.9 %collective-permute-start.8 = (bf16[4,128,256]{2,1,0:T(8,128)(2,1)}, bf16[4,128,256]{2,1,0:T(8,128)(2,1)S(1)}, u32[]{:S(2)}, u32[]{:S(2)}) collective-permute-start(bf16[4,128,256]{2,1,0:T(8,128)(2,1)} %get-tuple-element.17.i1), channel_id=1, source_target_pairs={{4,0},{8,4},{12,8},{16,12},{20,16},{24,20},{28,24},{32,28},{36,32}... | collective-permute-start | bytes 786440 | tf_op jit(solution)/shard_map/ppermute | solution.py:63
  65.4 4.3 %copy-start.6 = (bf16[4,128,256]{2,1,0:T(8,128)(2,1)}, bf16[4,128,256]{2,1,0:T(8,128)(2,1)S(1)}, u32[]{:S(2)}) copy-start(bf16[4,128,256]{2,1,0:T(8,128)(2,1)S(1)} %collective-permute-done.7.i0) | copy-start | bytes 786436
  69.7 0.7 copy-start.7
  85.8 2.6 %collective-permute-start.9 = (f32[224,8,128]{2,1,0:T(8,128)S(1)}, f32[224,8,128]{2,1,0:T(8,128)S(1)}, u32[]{:S(2)}, u32[]{:S(2)}) collective-permute-start(f32[224,8,128]{2,1,0:T(8,128)S(1)} %slice_bitcast_fusion), channel_id=1, source_target_pairs={{0,4},{1,5},{2,6},{3,7},{4,0},{5,1},{6,2},{7,3},{8,12},{9,13},{10,... | collective-permute-start | bytes 2752520 | tf_op jit(solution)/shard_map/ppermute | solution.py:41
  142.6 5.3 %collective-permute-start.11 = (f32[8,7,8,128]{3,2,1,0:T(8,128)S(1)}, f32[8,7,8,128]{3,2,1,0:T(8,128)S(1)}, u32[]{:S(2)}, u32[]{:S(2)}) collective-permute-start(f32[8,7,8,128]{3,2,1,0:T(8,128)S(1)} %all_to_all.11), channel_id=1, source_target_pairs={{0,136},{1,137},{2,138},{3,139},{4,7},{5,4},{6,5},{7,6},{8,0},{9,1... | collective-permute-start | bytes 688136 | tf_op jit(solution)/shard_map/ppermute | solution.py:41
  144.9 6.2 %collective-permute-start.10 = (f32[8,7,8,128]{3,2,1,0:T(8,128)S(1)}, f32[8,7,8,128]{3,2,1,0:T(8,128)S(1)}, u32[]{:S(2)}, u32[]{:S(2)}) collective-permute-start(f32[8,7,8,128]{3,2,1,0:T(8,128)S(1)} %all_to_all.11), channel_id=1, source_target_pairs={{0,8},{1,9},{2,10},{3,11},{4,5},{5,6},{6,7},{7,4},{8,128},{9,129},... | collective-permute-start | bytes 688136 | tf_op jit(solution)/shard_map/ppermute | solution.py:41
  147.9 5.0 %collective-permute-start.13 = (f32[4,7,8,128]{3,2,1,0:T(8,128)S(1)}, f32[4,7,8,128]{3,2,1,0:T(8,128)S(1)}, u32[]{:S(2)}, u32[]{:S(2)}) collective-permute-start(f32[4,7,8,128]{3,2,1,0:T(8,128)S(1)} %slice.35), channel_id=1, source_target_pairs={{0,136},{1,137},{2,138},{3,139},{4,7},{5,4},{6,5},{7,6},{8,0},{9,1... | collective-permute-start | bytes 344072 | tf_op jit(solution)/shard_map/ppermute | solution.py:41
  151.1 4.9 %collective-permute-start.12 = (f32[4,7,8,128]{3,2,1,0:T(8,128)S(1)}, f32[4,7,8,128]{3,2,1,0:T(8,128)S(1)}, u32[]{:S(2)}, u32[]{:S(2)}) collective-permute-start(f32[4,7,8,128]{3,2,1,0:T(8,128)S(1)} %slice.34), channel_id=1, source_target_pairs={{0,8},{1,9},{2,10},{3,11},{4,5},{5,6},{6,7},{7,4},{8,128},{9,129},... | collective-permute-start | bytes 344072 | tf_op jit(solution)/shard_map/ppermute | solution.py:41
  156.1 12.6 %collective-permute-start.15 = (f32[32,7,8,128]{3,2,1,0:T(8,128)S(1)}, f32[32,7,8,128]{3,2,1,0:T(8,128)S(1)}, u32[]{:S(2)}, u32[]{:S(2)}) collective-permute-start(f32[32,7,8,128]{3,2,1,0:T(8,128)S(1)} %bitcast.34), channel_id=1, source_target_pairs={{0,3},{1,0},{2,1},{3,2},{4,140},{5,141},{6,142},{7,143},{8,11},{9,... | collective-permute-start | bytes 2752520 | tf_op jit(solution)/shard_map/ppermute | solution.py:41
  157.3 13.9 %collective-permute-start.14 = (f32[32,7,8,128]{3,2,1,0:T(8,128)S(1)}, f32[32,7,8,128]{3,2,1,0:T(8,128)S(1)}, u32[]{:S(2)}, u32[]{:S(2)}) collective-permute-start(f32[32,7,8,128]{3,2,1,0:T(8,128)S(1)} %bitcast.35), channel_id=1, source_target_pairs={{0,1},{1,2},{2,3},{3,0},{4,12},{5,13},{6,14},{7,15},{8,9},{9,10},{... | collective-permute-start | bytes 2752520 | tf_op jit(solution)/shard_map/ppermute | solution.py:41
  168.8 7.8 %collective-permute-start.17 = (f32[16,7,8,128]{3,2,1,0:T(8,128)S(1)}, f32[16,7,8,128]{3,2,1,0:T(8,128)S(1)}, u32[]{:S(2)}, u32[]{:S(2)}) collective-permute-start(f32[16,7,8,128]{3,2,1,0:T(8,128)S(1)} %slice.37), channel_id=1, source_target_pairs={{0,3},{1,0},{2,1},{3,2},{4,140},{5,141},{6,142},{7,143},{8,11},{9,... | collective-permute-start | bytes 1376264 | tf_op jit(solution)/shard_map/ppermute | solution.py:41
  171.2 8.6 %collective-permute-start.16 = (f32[16,7,8,128]{3,2,1,0:T(8,128)S(1)}, f32[16,7,8,128]{3,2,1,0:T(8,128)S(1)}, u32[]{:S(2)}, u32[]{:S(2)}) collective-permute-start(f32[16,7,8,128]{3,2,1,0:T(8,128)S(1)} %slice.36), channel_id=1, source_target_pairs={{0,1},{1,2},{2,3},{3,0},{4,12},{5,13},{6,14},{7,15},{8,9},{9,10},{... | collective-permute-start | bytes 1376264 | tf_op jit(solution)/shard_map/ppermute | solution.py:41
  180.2 15.4 %copy-start = (f32[4,32,7,8,128]{4,3,2,1,0:T(8,128)}, f32[4,32,7,8,128]{4,3,2,1,0:T(8,128)S(1)}, u32[]{:S(2)}) copy-start(f32[4,32,7,8,128]{4,3,2,1,0:T(8,128)S(1)} %pad_maximum_fusion) | copy-start | bytes 11010052
  180.2 15.4 %collective-permute-start.18 = (f32[16,8,7,8,128]{4,3,2,1,0:T(8,128)S(1)}, f32[16,8,7,8,128]{4,3,2,1,0:T(8,128)}, u32[]{:S(2)}, u32[]{:S(2)}) collective-permute-start(f32[16,8,7,8,128]{4,3,2,1,0:T(8,128)S(1)} %bitcast.32), channel_id=1, source_target_pairs={{0,4},{1,5},{2,6},{3,7},{4,0},{5,1},{6,2},{7,3},{8,12},{9,13},{10,... | collective-permute-start | bytes 11010056 | tf_op jit(solution)/shard_map/ppermute | solution.py:41

commit v2 on v1

--- a/solution.py
+++ b/solution.py
@@ -18,7 +18,6 @@
 PIECE = 7
 PIECES = 32
 ALL = ("yh", "z", "yl", "c", "x")
-PLANE = ("yh", "z", "yl")
 CHAIN = ("z", "yl", "c")
 
 
@@ -65,10 +64,9 @@
 
 VMEM = pl.BlockSpec(memory_space=pltpu.VMEM)
 SMEM = pl.BlockSpec(memory_space=pltpu.SMEM)
-ANY = pl.BlockSpec(memory_space=pl.ANY)
-
-
-def params(limit=60 << 20):
+
+
+def params(limit=24 << 20):
     return pltpu.CompilerParams(vmem_limit_bytes=limit)
 
 
@@ -113,19 +111,13 @@
 TAPS = [(1, 1), (0, 1), (2, 1), (0, 0), (1, 0), (2, 0), (0, 2), (1, 2), (2, 2)]
 
 
-def start_weights(w_hbm, w_buf, sems):
+def convolve(spread, weight, acc):
     for n, (a, b) in enumerate(TAPS):
-        pltpu.make_async_copy(w_hbm.at[a, b], w_buf.at[n], sems.at[n]).start()
-
-
-def convolve(spread, w_hbm, w_buf, sems, acc):
-    for n, (a, b) in enumerate(TAPS):
-        pltpu.make_async_copy(w_hbm.at[a, b], w_buf.at[n], sems.at[n]).wait()
         rows = ROWS if b == 1 else ROWS - 1
         src = 1 if b == 2 else 0
         dst = 1 if b == 0 else 0
         piece = spread[a : a + 2, src : src + rows].reshape(2 * rows * COLS, 3 * CH)
-        term = jnp.dot(piece, w_buf[n], preferred_element_type=F32)
+        term = jnp.dot(piece, weight[a, b], preferred_element_type=F32)
         term = term.reshape(2, rows, COLS, CH)
         if n == 0:
             acc[...] = term
@@ -133,10 +125,9 @@
             acc[:, dst : dst + rows] += term
 
 
-def forward_kernel(prev, first, second, follow, w_hbm, bias, head, pre, g0, g1, spread, w_buf, sems):
-    start_weights(w_hbm, w_buf, sems)
+def forward_kernel(prev, first, second, follow, weight, bias, head, pre, g0, g1, spread):
     spread_columns((prev, first, second, follow), spread)
-    convolve(spread, w_hbm, w_buf, sems, pre)
+    convolve(spread, weight, pre)
     for f, out in ((0, g0), (1, g1)):
         for r in range(ROWS):
             value = pre[f, r] + bias[...]
@@ -146,10 +137,9 @@
             out[r] = (head[...] * slope).astype(BF16)
 
 
-def transpose_kernel(prev, first, second, follow, w_hbm, g0, g1, spread, acc, w_buf, sems):
-    start_weights(w_hbm, w_buf, sems)
+def transpose_kernel(prev, first, second, follow, weight, g0, g1, spread, acc):
     spread_columns((prev, first, second, follow), spread)
-    convolve(spread, w_hbm, w_buf, sems, acc)
+    convolve(spread, weight, acc)
     for f, out in ((0, g0), (1, g1)):
         out[...] = acc[f].astype(BF16)
 
@@ -158,9 +148,25 @@
     return dict(
         spread=pltpu.VMEM((4, ROWS, COLS, 3 * CH), BF16),
         acc=pltpu.VMEM((2, ROWS, COLS, CH), F32),
-        w_buf=pltpu.VMEM((9, 3 * CH, CH), BF16),
-        sems=pltpu.SemaphoreType.DMA((9,)),
     )
+
+
+def turn_kernel(weight, out):
+    for d in range(3):
+        out[0, 0, 2 - d] = weight[0, 0, d].T
+
+
+def turn_weights(weight):
+    return pl.pallas_call(
+        turn_kernel,
+        grid=(9,),
+        out_shape=jax.ShapeDtypeStruct((3, 3, 3, CH, CH), BF16),
+        in_specs=[pl.BlockSpec((1, 1, 3, CH, CH), lambda n: (n // 3, n % 3, 0, 0, 0))],
+        out_specs=pl.BlockSpec((1, 1, 3, CH, CH), lambda n: (2 - n // 3, 2 - n % 3, 0, 0, 0)),
+        compiler_params=params(8 << 20),
+        cost_estimate=cost(2e9, 8 << 20),
+        name="turn_weights",
+    )(weight)
 
 
 FRAME = jax.ShapeDtypeStruct((ROWS, COLS, CH), BF16)
@@ -172,9 +178,9 @@
     return pl.pallas_call(
         forward_kernel,
         out_shape=(jax.ShapeDtypeStruct((2, ROWS, COLS, CH), F32), FRAME, FRAME),
-        in_specs=[VMEM] * 4 + [ANY, VMEM, VMEM],
+        in_specs=[VMEM] * 7,
         out_specs=(VMEM, VMEM, VMEM),
-        scratch_shapes=[s["spread"], s["w_buf"], s["sems"]],
+        scratch_shapes=[s["spread"]],
         compiler_params=params(),
         cost_estimate=cost(CONV_FLOPS, 6 << 20),
         name="forward",
@@ -186,9 +192,9 @@
     return pl.pallas_call(
         transpose_kernel,
         out_shape=(FRAME, FRAME),
-        in_specs=[VMEM] * 4 + [ANY],
+        in_specs=[VMEM] * 5,
         out_specs=(VMEM, VMEM),
-        scratch_shapes=[s["spread"], s["acc"], s["w_buf"], s["sems"]],
+        scratch_shapes=[s["spread"], s["acc"]],
         compiler_params=params(),
         cost_estimate=cost(CONV_FLOPS, 5 << 20),
         name="transposed",
@@ -230,17 +236,16 @@
 
 
 def backward_kernel(
-    pos, i0, i1, i2, i3, c0, c1, c2, c3, s0, s1, pre, w_hbm, head, out,
-    spread, acc, w_buf, turn_i, turn_c, pgb, sems,
+    pos, i0, i1, i2, i3, c0, c1, c2, c3, s0, s1, pre, weight, head, sent, kept,
+    spread, acc, turn_i, turn_c, pgb, total,
 ):
     x = pos[0]
     core = pos[1]
-    start_weights(w_hbm, w_buf, sems)
     grads = (i0, i1, i2, i3)
     spread_columns(grads, spread)
     part_transposed(grads, x, turn_i)
     part_transposed((c0, c1, c2, c3), x, turn_c)
-    convolve(spread, w_hbm, w_buf, sems, acc)
+    convolve(spread, weight, acc)
     sum_bias = jnp.zeros((8, CH), F32)
     sum_head = jnp.zeros((8, CH), F32)
     for f in range(2):
@@ -258,36 +263,47 @@
     total_head = jnp.sum(sum_head, axis=0, keepdims=True)
     row = lax.broadcasted_iota(jnp.int32, (8, CH), 0)
     small = jnp.where(row == 0, total_bias, jnp.where(row == 1, total_head, 0.0))
-    slots = [jnp.where(core == h, 1, 0) for h in range(2)]
+    blocks = []
     for b in range(3):
         block = PENALTY * correlate(turn_i, (s0, s1), b) + correlate(turn_c, (pgb.at[0], pgb.at[1]), b)
-        for a in range(3):
-            for d in range(3):
-                k = (a * 3 + b) * 3 + d
-                tap = block[(a * 3 + d) * PART : (a * 3 + d + 1) * PART]
-                for h in range(2):
-                    half = tap[:, h * 128 : (h + 1) * 128].reshape(PART // 8, 8, 128)
-                    out[slots[h], k * 8 : (k + 1) * 8] = half
-    for h in range(2):
-        out[slots[h], TILES] = small[:, h * 128 : (h + 1) * 128]
-        out[slots[h], TILES + 1 :] = jnp.zeros((PIECE * PIECES - TILES - 1, 8, 128), F32)
+        blocks.append(block)
+    for b, block in enumerate(blocks):
+        total[b * 9 * PART : (b + 1) * 9 * PART] = block
+
+    def store(out, h):
+        lanes = slice(h * 128, (h + 1) * 128)
+        for k in range(27):
+            a, b, d = k // 9, (k // 3) % 3, k % 3
+            at = ((b * 3 + a) * 3 + d) * PART
+            out[k * 8 : (k + 1) * 8] = total[at : at + PART, lanes].reshape(PART // 8, 8, 128)
+        out[TILES] = small[:, lanes]
+        out[TILES + 1 :] = jnp.zeros((PIECE * PIECES - TILES - 1, 8, 128), F32)
+
+    @pl.when(core == 0)
+    def _():
+        store(kept, 0)
+        store(sent, 1)
+
+    @pl.when(core == 1)
+    def _():
+        store(kept, 1)
+        store(sent, 0)
 
 
 def backward(pos, grads, clips, score, pre, w9, head):
     s = conv_scratch()
     return pl.pallas_call(
         backward_kernel,
-        out_shape=jax.ShapeDtypeStruct((2, PIECE * PIECES, 8, 128), F32),
-        in_specs=[SMEM] + [VMEM] * 11 + [ANY, VMEM],
-        out_specs=VMEM,
+        out_shape=(jax.ShapeDtypeStruct((PIECE * PIECES, 8, 128), F32),) * 2,
+        in_specs=[SMEM] + [VMEM] * 13,
+        out_specs=(VMEM, VMEM),
         scratch_shapes=[
             s["spread"],
             s["acc"],
-            s["w_buf"],
             pltpu.VMEM((3 * PART, 4 * ROWS * COLS), BF16),
             pltpu.VMEM((3 * PART, 4 * ROWS * COLS), BF16),
             pltpu.VMEM((2, ROWS, COLS, CH), BF16),
-            s["sems"],
+            pltpu.VMEM((27 * PART, CH), F32),
         ],
         compiler_params=params(),
         cost_estimate=cost(CONV_FLOPS * 1.6, 10 << 20),
@@ -309,7 +325,7 @@
             at_y = relative(lax.rem(row - y + 4, 4))
             place = jnp.where(held == 0, at_x * 4 + at_y, at_y * 4 + at_x)
             for z in range(8):
-                piece = ((row // 2) * 8 + z) * 2 + row % 2
+                piece = row * 8 + z
                 for j in range(PIECE):
                     tile = piece * PIECE + j
                     if tile < TILES:
@@ -358,7 +374,7 @@
     above = permute(own, along_x(-1))
     across = permute(own, along_x(2))
     w9 = weight.reshape(3, 3, 3 * CH, CH)
-    turned = weight[::-1, ::-1, ::-1].swapaxes(3, 4).reshape(3, 3, 3 * CH, CH)
+    turned = turn_weights(weight).reshape(3, 3, 3 * CH, CH)
     bias = bias.reshape(1, CH)
     head = head.reshape(1, CH)
 
@@ -368,9 +384,11 @@
     clip_frames = with_halo(*gather_rows(pos, own, below, above, across))
     pre, s0, s1 = forward(clip_frames, w9, bias, head)
     grad_frames = with_halo(*transposed(with_halo(s0, s1), turned))
-    terms = backward(pos, grad_frames, clip_frames, (s0, s1), pre, w9, head)
-    half = terms[1] + permute(terms[0], swap_core)
-    pieces = lax.all_to_all(half.reshape(PIECES, PIECE, 8, 128), PLANE, 0, 0, tiled=True)
+    sent, kept = backward(pos, grad_frames, clip_frames, (s0, s1), pre, w9, head)
+    half = kept + permute(sent, swap_core)
+    lines = lax.all_to_all(half.reshape(4, 8, PIECE, 8, 128), ("yh", "yl"), 0, 0, tiled=True)
+    line = jnp.sum(lines, axis=0)
+    pieces = lax.all_to_all(line, "z", 0, 0, tiled=True)
     piece = jnp.sum(pieces, axis=0)
     line = jnp.broadcast_to(piece[None], (8, PIECE, 8, 128))
     line = lax.all_to_all(line, "z", 0, 0, tiled=True)

time: 204 us -> 175 us (0.86)
  Pallas kernels: 42.7 us -> 21.5 us
  local copies, waits for them, and re-layouts: 10.8 us -> 4.93 us
  waiting for transfers between devices: 54.2 us -> 59.7 us
  blocking collectives: 52.8 us -> 49.5 us
  starting transfers between devices: 39.8 us -> 37.5 us
    pallas_call x1, Pallas kernels: 10.3 us -> 3.36 us  [forward(): pl.pallas_call(forward_kernel, out_shape=(jax.ShapeDtypeStruct((2, ROWS,...]
    pallas_call x1, Pallas kernels: 9.73 us -> 3.24 us  [transposed(): pl.pallas_call(transpose_kernel, out_shape=(FRAME, FRAME), in_specs=[VMEM...]
    transpose x2 -> x0, local copies, waits for them, and re-layouts: 6.08 us -> none  [per_device(): turned = weight[::-1, ::-1, ::-1].swapaxes(3, 4).reshape(3, 3, 3 * CH, CH)]
    ppermute x6, waiting for transfers between devices: 11.8 us -> 16.5 us  [chain(): return lax.ppermute(value, CHAIN, pairs)]
    pallas_call x1 -> x2, Pallas kernels: 14.2 us -> 10.5 us  [the longest x1 8.91 us: backward(): pl.pallas_call(backward_kernel, out_shape=(jax.ShapeDtypeStruct((PIECE *...]
    all_to_all x1 -> x2, blocking collectives: 40.7 us -> 37.9 us  [the longest x1 19.5 us: per_device(): pieces = lax.all_to_all(line, 'z', 0, 0, tiled=True)]
    pallas_call x1, Pallas kernels: 6.49 us -> 3.85 us  [assemble(): pl.pallas_call(assemble_kernel, grid=(ROWS,), out_shape=(jax.ShapeDtypeSt...]
    unnamed x16 -> x12, local copies, waits for them, and re-layouts: 2.08 us -> 4.27 us
  transfers between devices with their start and end apart: 19 -> 19, of which waited for: 15 -> 17; matrix products, arithmetic and copies ran while one was open for 3% -> 0% of each run, Pallas kernels for 0% -> 1%
where the time goes in v2:
time: 175 us
  waiting for transfers between devices  59.7 us (34%)
  blocking collectives  49.5 us (28%)
  starting transfers between devices  37.5 us (21%)
  Pallas kernels  21.5 us (12%)
  local copies, waits for them, and re-layouts  4.93 us (3%)
    ppermute x13, waiting for transfers between devices, permute(): return lax.ppermute(value, ALL, moved(fn))  43.2 us
    ppermute x13, starting transfers between devices, permute(): return lax.ppermute(value, ALL, moved(fn))  23.6 us
    all_to_all x1, blocking collectives, per_device(): pieces = lax.all_to_all(line, 'z', 0, 0, tiled=True)  19.5 us
    all_to_all x1, blocking collectives, per_device(): lax.all_to_all(half.reshape(4, 8, PIECE, 8, 128), ('yh', 'yl'), 0, 0, til...  18.4 us
    ppermute x6, waiting for transfers between devices, chain(): return lax.ppermute(value, CHAIN, pairs)  16.5 us
    ppermute x6, starting transfers between devices, chain(): return lax.ppermute(value, CHAIN, pairs)  13.9 us
    all_to_all x1, blocking collectives, per_device(): line = lax.all_to_all(line, 'z', 0, 0, tiled=True)  11.6 us
    pallas_call x1, Pallas kernels, backward(): pl.pallas_call(backward_kernel, out_shape=(jax.ShapeDtypeStruct((PIECE *...  8.91 us
  transfers between devices with their start and end apart: 19, of which 17 were waited for; matrix products, arithmetic and copies ran while one was open for 0% of the time, Pallas kernels for 1%

profile of v2, /device:TPU:1, one launch (start us, length us, event | category | flops | bytes accessed | tf_op | source)
XLA Modules:
  0.0 174.7 jit_solution(8310923732601998716)
XLA Ops:
  0.6 3.6 %collective-permute-start.2 = (bf16[2,128,256]{2,1,0:T(8,128)(2,1)}, bf16[2,128,256]{2,1,0:T(8,128)(2,1)S(1)}, u32[]{:S(2)}, u32[]{:S(2)}) collective-permute-start(bf16[2,128,256]{2,1,0:T(8,128)(2,1)} %bitcast.26), channel_id=1, source_target_pairs={{0,2},{1,3},{2,0},{3,1},{4,6},{5,7},{6,4},{7,5},{8,10},{9,11},{10,... | collective-permute-start | bytes 393224 | tf_op jit(solution)/shard_map/ppermute | solution.py:40
  4.3 0.9 collective-permute-start.1
  5.1 0.6 collective-permute-start
  5.7 0.1 pad_add_fusion.pos_ref.pos
  5.8 1.0 collective-permute-done.2.across
  6.8 3.7 %collective-permute-done.1.above = bf16[2,128,256]{2,1,0:T(8,128)(2,1)S(1)} collective-permute-done((bf16[2,128,256]{2,1,0:T(8,128)(2,1)}, bf16[2,128,256]{2,1,0:T(8,128)(2,1)S(1)}, u32[]{:S(2)}, u32[]{:S(2)}) %collective-permute-start.1) | collective-permute-done | bytes 131104 | tf_op jit(solution)/shard_map/ppermute | solution.py:40
  10.5 2.2 %collective-permute-done.below = bf16[2,128,256]{2,1,0:T(8,128)(2,1)S(1)} collective-permute-done((bf16[2,128,256]{2,1,0:T(8,128)(2,1)}, bf16[2,128,256]{2,1,0:T(8,128)(2,1)S(1)}, u32[]{:S(2)}, u32[]{:S(2)}) %collective-permute-start) | collective-permute-done | bytes 131104 | tf_op jit(solution)/shard_map/ppermute | solution.py:40
  12.7 0.0 copy-start
  12.7 0.9 copy-done
  13.6 0.6 gather_rows.1
  14.2 3.1 %collective-permute-start.3 = (bf16[4,128,256]{2,1,0:T(8,128)(2,1)S(1)}, bf16[4,128,256]{2,1,0:T(8,128)(2,1)S(1)}, u32[]{:S(2)}, u32[]{:S(2)}) collective-permute-start(bf16[4,128,256]{2,1,0:T(8,128)(2,1)S(1)} %get-tuple-element.14.second.c2), channel_id=1, source_target_pairs={{0,4},{4,8},{8,12},{12,16},{16,20},{20,24},{24,28},{28,32},{32,36}... | collective-permute-start | bytes 786440 | tf_op jit(solution)/shard_map/ppermute | solution.py:62
  17.4 1.9 %collective-permute-start.4 = (bf16[4,128,256]{2,1,0:T(8,128)(2,1)S(1)}, bf16[4,128,256]{2,1,0:T(8,128)(2,1)S(1)}, u32[]{:S(2)}, u32[]{:S(2)}) collective-permute-start(bf16[4,128,256]{2,1,0:T(8,128)(2,1)S(1)} %get-tuple-element.15.first.c1), channel_id=1, source_target_pairs={{4,0},{8,4},{12,8},{16,12},{20,16},{24,20},{28,24},{32,28},{36,32}... | collective-permute-start | bytes 786440 | tf_op jit(solution)/shard_map/ppermute | solution.py:62
  19.3 1.4 collective-permute-done.3.prev.c0
  20.6 4.4 %collective-permute-done.4.follow.c3 = bf16[4,128,256]{2,1,0:T(8,128)(2,1)S(1)} collective-permute-done((bf16[4,128,256]{2,1,0:T(8,128)(2,1)S(1)}, bf16[4,128,256]{2,1,0:T(8,128)(2,1)S(1)}, u32[]{:S(2)}, u32[]{:S(2)}) %collective-permute-start.4) | collective-permute-done | bytes 262176 | tf_op jit(solution)/shard_map/ppermute | solution.py:62
  25.0 0.0 copy-start.1
  25.0 2.0 %copy-done.1 = bf16[3,3,3,256,256]{4,3,2,1,0:T(8,128)(2,1)S(1)} copy-done((bf16[3,3,3,256,256]{4,3,2,1,0:T(8,128)(2,1)S(1)}, bf16[3,3,3,256,256]{4,3,2,1,0:T(8,128)(2,1)}, u32[]{:S(2)}) %copy-start.1) | copy-done | bytes 3538968
  27.0 0.0 copy-start.3
  27.1 0.7 copy-done.3
  27.7 0.7 copy-done.4
  28.4 3.4 %forward.1 = (f32[2,4,128,256]{3,2,1,0:T(8,128)S(1)}, bf16[4,128,256]{2,1,0:T(8,128)(2,1)S(1)}, bf16[4,128,256]{2,1,0:T(8,128)(2,1)S(1)}) custom-call(bf16[4,128,256]{2,1,0:T(8,128)(2,1)S(1)} %collective-permute-done.3.prev.c0, bf16[4,128,256]{2,1,0:T(8,128)(2,1)S(1)} %get-tuple-element.15.first.c1, bf16[4,128,256]{2,1,0:T(8,128)(2,1)S(1)} %get-tuple-element.14.second.c2, ...), custom_call_target="tpu_custom_call" | custom-call | flops 3623878656 | bytes 6291456 | tf_op jit(solution)/shard_map/forward/pallas_call | solution.py:178
  31.8 1.9 %collective-permute-start.5 = (bf16[4,128,256]{2,1,0:T(8,128)(2,1)S(1)}, bf16[4,128,256]{2,1,0:T(8,128)(2,1)S(1)}, u32[]{:S(2)}, u32[]{:S(2)}) collective-permute-start(bf16[4,128,256]{2,1,0:T(8,128)(2,1)S(1)} %get-tuple-element.16.second.s1), channel_id=1, source_target_pairs={{0,4},{4,8},{8,12},{12,16},{16,20},{20,24},{24,28},{28,32},{32,36}... | collective-permute-start | bytes 786440 | tf_op jit(solution)/shard_map/ppermute | solution.py:62
  33.7 2.4 %collective-permute-start.6 = (bf16[4,128,256]{2,1,0:T(8,128)(2,1)S(1)}, bf16[4,128,256]{2,1,0:T(8,128)(2,1)S(1)}, u32[]{:S(2)}, u32[]{:S(2)}) collective-permute-start(bf16[4,128,256]{2,1,0:T(8,128)(2,1)S(1)} %get-tuple-element.17.first.s0), channel_id=1, source_target_pairs={{4,0},{8,4},{12,8},{16,12},{20,16},{24,20},{28,24},{32,28},{36,32}... | collective-permute-start | bytes 786440 | tf_op jit(solution)/shard_map/ppermute | solution.py:62
  36.1 1.6 turn_weights.1
  37.7 0.0 collective-permute-done.5.prev
  37.7 4.8 %collective-permute-done.6.follow = bf16[4,128,256]{2,1,0:T(8,128)(2,1)S(1)} collective-permute-done((bf16[4,128,256]{2,1,0:T(8,128)(2,1)S(1)}, bf16[4,128,256]{2,1,0:T(8,128)(2,1)S(1)}, u32[]{:S(2)}, u32[]{:S(2)}) %collective-permute-start.6) | collective-permute-done | bytes 262176 | tf_op jit(solution)/shard_map/ppermute | solution.py:62
  42.5 0.0 copy-start.2
  42.5 3.2 %transposed.1 = (bf16[4,128,256]{2,1,0:T(8,128)(2,1)S(1)}, bf16[4,128,256]{2,1,0:T(8,128)(2,1)S(1)}) custom-call(bf16[4,128,256]{2,1,0:T(8,128)(2,1)S(1)} %collective-permute-done.5.prev, bf16[4,128,256]{2,1,0:T(8,128)(2,1)S(1)} %get-tuple-element.17.first.s0, bf16[4,128,256]{2,1,0:T(8,128)(2,1)S(1)} %get-tuple-element.16.second.s1, ...), custom_call_target="tpu_custom_call" | custom-call | flops 3623878656 | bytes 5242880 | tf_op jit(solution)/shard_map/transposed/pallas_call | solution.py:192
  45.7 1.9 %collective-permute-start.7 = (bf16[4,128,256]{2,1,0:T(8,128)(2,1)S(1)}, bf16[4,128,256]{2,1,0:T(8,128)(2,1)S(1)}, u32[]{:S(2)}, u32[]{:S(2)}) collective-permute-start(bf16[4,128,256]{2,1,0:T(8,128)(2,1)S(1)} %get-tuple-element.18.i2), channel_id=1, source_target_pairs={{0,4},{4,8},{8,12},{12,16},{16,20},{20,24},{24,28},{28,32},{32,36}... | collective-permute-start | bytes 786440 | tf_op jit(solution)/shard_map/ppermute | solution.py:62
  47.6 2.6 %collective-permute-start.8 = (bf16[4,128,256]{2,1,0:T(8,128)(2,1)S(1)}, bf16[4,128,256]{2,1,0:T(8,128)(2,1)S(1)}, u32[]{:S(2)}, u32[]{:S(2)}) collective-permute-start(bf16[4,128,256]{2,1,0:T(8,128)(2,1)S(1)} %get-tuple-element.19.i1), channel_id=1, source_target_pairs={{4,0},{8,4},{12,8},{16,12},{20,16},{24,20},{28,24},{32,28},{36,32}... | collective-permute-start | bytes 786440 | tf_op jit(solution)/shard_map/ppermute | solution.py:62
  50.3 0.7 collective-permute-done.7.i0
  50.9 5.3 %collective-permute-done.8.i3 = bf16[4,128,256]{2,1,0:T(8,128)(2,1)S(1)} collective-permute-done((bf16[4,128,256]{2,1,0:T(8,128)(2,1)S(1)}, bf16[4,128,256]{2,1,0:T(8,128)(2,1)S(1)}, u32[]{:S(2)}, u32[]{:S(2)}) %collective-permute-start.8) | collective-permute-done | bytes 262176 | tf_op jit(solution)/shard_map/ppermute | solution.py:62
  56.2 0.0 copy-done.2
  56.2 0.0 copy-done.5
  56.2 8.9 %backward.1 = (f32[224,8,128]{2,1,0:T(8,128)S(1)}, f32[224,8,128]{2,1,0:T(8,128)S(1)}) custom-call(s32[3]{0:T(128)S(1)} %pad_add_fusion.pos_ref.pos, bf16[4,128,256]{2,1,0:T(8,128)(2,1)S(1)} %collective-permute-done.7.i0, bf16[4,128,256]{2,1,0:T(8,128)(2,1)S(1)} %get-tuple-element.19.i1, bf16[4,128,256]{2,1,0:T(8,128)(2,1)S(1)} %get-tuple-element.18.i2, ...), custom_call_target="tpu_custom_call" | custom-call | flops 5798205952 | bytes 10485760 | tf_op jit(solution)/shard_map/backward/pallas_call | solution.py:295
  65.2 0.1 collective-permute-start.9
  65.3 2.5 %collective-permute-done.9 = f32[224,8,128]{2,1,0:T(8,128)S(1)} collective-permute-done((f32[224,8,128]{2,1,0:T(8,128)S(1)}, f32[224,8,128]{2,1,0:T(8,128)S(1)}, u32[]{:S(2)}, u32[]{:S(2)}) %collective-permute-start.9) | collective-permute-done | bytes 917536 | tf_op jit(solution)/shard_map/ppermute | solution.py:40
  67.7 0.1 add.7
  67.8 18.4 %all_to_all.15 = f32[4,8,7,8,128]{4,3,2,1,0:T(8,128)S(1)} all-to-all(f32[4,8,7,8,128]{4,3,2,1,0:T(8,128)S(1)} %bitcast.39), channel_id=1, replica_groups=mesh['yh'=2,'z'=8,'yl'=2,'c'=2,'x'=4] {'yh','yl'}, dimensions={0} | all-to-all | bytes 1835008 | tf_op jit(solution)/shard_map/all_to_all | solution.py:389
  86.3 0.1 reduce_sum.18
  86.3 19.5 %all_to_all.16 = f32[8,7,8,128]{3,2,1,0:T(8,128)S(1)} all-to-all(f32[8,7,8,128]{3,2,1,0:T(8,128)S(1)} %reduce_sum.18), channel_id=1, replica_groups=mesh['yh'=2,'z'=8,'yl'=2,'c'=2,'x'=4] {'z'}, dimensions={0} | all-to-all | bytes 458752 | tf_op jit(solution)/shard_map/all_to_all | solution.py:391
  105.9 11.6 %all_to_all.17 = f32[8,7,8,128]{3,2,1,0:T(8,128)S(1)} all-to-all(f32[8,7,8,128]{3,2,1,0:T(8,128)S(1)} %broadcast_in_dim.2), channel_id=1, replica_groups=mesh['yh'=2,'z'=8,'yl'=2,'c'=2,'x'=4] {'z'}, dimensions={0} | all-to-all | bytes 458752 | tf_op jit(solution)/shard_map/all_to_all | solution.py:394
  117.4 1.7 collective-permute-start.11
  119.1 0.0 collective-permute-start.10
  119.1 3.2 %collective-permute-done.11 = f32[8,7,8,128]{3,2,1,0:T(8,128)S(1)} collective-permute-done((f32[8,7,8,128]{3,2,1,0:T(8,128)S(1)}, f32[8,7,8,128]{3,2,1,0:T(8,128)S(1)}, u32[]{:S(2)}, u32[]{:S(2)}) %collective-permute-start.11) | collective-permute-done | bytes 229408 | tf_op jit(solution)/shard_map/ppermute | solution.py:40
  122.3 3.0 %collective-permute-start.13 = (f32[4,7,8,128]{3,2,1,0:T(8,128)S(1)}, f32[4,7,8,128]{3,2,1,0:T(8,128)S(1)}, u32[]{:S(2)}, u32[]{:S(2)}) collective-permute-start(f32[4,7,8,128]{3,2,1,0:T(8,128)S(1)} %slice.25), channel_id=1, source_target_pairs={{0,136},{1,137},{2,138},{3,139},{4,7},{5,4},{6,5},{7,6},{8,0},{9,1... | collective-permute-start | bytes 344072 | tf_op jit(solution)/shard_map/ppermute | solution.py:40
  125.3 0.0 collective-permute-done.10
  125.3 0.1 collective-permute-start.12
  125.4 1.7 collective-permute-done.13
  127.1 3.2 %collective-permute-done.12 = f32[4,7,8,128]{3,2,1,0:T(8,128)S(1)} collective-permute-done((f32[4,7,8,128]{3,2,1,0:T(8,128)S(1)}, f32[4,7,8,128]{3,2,1,0:T(8,128)S(1)}, u32[]{:S(2)}, u32[]{:S(2)}) %collective-permute-start.12) | collective-permute-done | bytes 114720 | tf_op jit(solution)/shard_map/ppermute | solution.py:40
  130.3 0.1 pad_maximum_fusion.1
  130.3 1.0 collective-permute-start.15
  131.3 0.6 collective-permute-start.14
  131.9 11.1 %collective-permute-done.15 = f32[32,7,8,128]{3,2,1,0:T(8,128)S(1)} collective-permute-done((f32[32,7,8,128]{3,2,1,0:T(8,128)S(1)}, f32[32,7,8,128]{3,2,1,0:T(8,128)S(1)}, u32[]{:S(2)}, u32[]{:S(2)}) %collective-permute-start.15) | collective-permute-done | bytes 917536 | tf_op jit(solution)/shard_map/ppermute | solution.py:40
  143.0 2.2 %collective-permute-start.17 = (f32[16,7,8,128]{3,2,1,0:T(8,128)S(1)}, f32[16,7,8,128]{3,2,1,0:T(8,128)S(1)}, u32[]{:S(2)}, u32[]{:S(2)}) collective-permute-start(f32[16,7,8,128]{3,2,1,0:T(8,128)S(1)} %slice.27), channel_id=1, source_target_pairs={{0,3},{1,0},{2,1},{3,2},{4,140},{5,141},{6,142},{7,143},{8,11},{9,... | collective-permute-start | bytes 1376264 | tf_op jit(solution)/shard_map/ppermute | solution.py:40
  145.2 0.2 collective-permute-done.14
  145.4 0.1 collective-permute-start.16
  145.5 5.2 %collective-permute-done.17 = f32[16,7,8,128]{3,2,1,0:T(8,128)S(1)} collective-permute-done((f32[16,7,8,128]{3,2,1,0:T(8,128)S(1)}, f32[16,7,8,128]{3,2,1,0:T(8,128)S(1)}, u32[]{:S(2)}, u32[]{:S(2)}) %collective-permute-start.17) | collective-permute-done | bytes 458784 | tf_op jit(solution)/shard_map/ppermute | solution.py:40
  150.7 3.3 %collective-permute-done.16 = f32[16,7,8,128]{3,2,1,0:T(8,128)S(1)} collective-permute-done((f32[16,7,8,128]{3,2,1,0:T(8,128)S(1)}, f32[16,7,8,128]{3,2,1,0:T(8,128)S(1)}, u32[]{:S(2)}, u32[]{:S(2)}) %collective-permute-start.16) | collective-permute-done | bytes 458784 | tf_op jit(solution)/shard_map/ppermute | solution.py:40
  154.0 0.1 maximum_bitcast_fusion
  154.1 0.2 pad_maximum_fusion
  154.3 9.9 %collective-permute-start.18 = (f32[16,8,7,8,128]{4,3,2,1,0:T(8,128)S(1)}, f32[16,8,7,8,128]{4,3,2,1,0:T(8,128)S(1)}, u32[]{:S(2)}, u32[]{:S(2)}) collective-permute-start(f32[16,8,7,8,128]{4,3,2,1,0:T(8,128)S(1)} %bitcast.24), channel_id=1, source_target_pairs={{0,4},{1,5},{2,6},{3,7},{4,0},{5,1},{6,2},{7,3},{8,12},{9,13},{10,... | collective-permute-start | bytes 11010056 | tf_op jit(solution)/shard_map/ppermute | solution.py:40
  164.2 6.0 %collective-permute-done.18.other = f32[16,8,7,8,128]{4,3,2,1,0:T(8,128)S(1)} collective-permute-done((f32[16,8,7,8,128]{4,3,2,1,0:T(8,128)S(1)}, f32[16,8,7,8,128]{4,3,2,1,0:T(8,128)S(1)}, u32[]{:S(2)}, u32[]{:S(2)}) %collective-permute-start.18) | collective-permute-done | bytes 3670048 | tf_op jit(solution)/shard_map/ppermute | solution.py:40
  170.2 3.9 %assemble.1 = (f32[27,4,8,8,256]{4,3,2,1,0:T(8,128)}, f32[8,256]{1,0:T(8,128)S(1)}) custom-call(s32[3]{0:T(128)S(1)} %pad_add_fusion.pos_ref.pos, f32[16,8,7,8,128]{4,3,2,1,0:T(8,128)S(1)} %bitcast.25, f32[16,8,7,8,128]{4,3,2,1,0:T(8,128)S(1)} %collective-permute-done.18.other), custom_call_target="tpu_custom_call" | custom-call | flops 1000000 | bytes 15728640 | tf_op jit(solution)/shard_map/assemble/pallas_call | solution.py:339
  174.1 0.6 fusion
  (9 shorter events, 0.1 us)
Async XLA Ops:
  0.6 6.2 %collective-permute-start.2 = (bf16[2,128,256]{2,1,0:T(8,128)(2,1)}, bf16[2,128,256]{2,1,0:T(8,128)(2,1)S(1)}, u32[]{:S(2)}, u32[]{:S(2)}) collective-permute-start(bf16[2,128,256]{2,1,0:T(8,128)(2,1)} %bitcast.26), channel_id=1, source_target_pairs={{0,2},{1,3},{2,0},{3,1},{4,6},{5,7},{6,4},{7,5},{8,10},{9,11},{10,... | collective-permute-start | bytes 393224 | tf_op jit(solution)/shard_map/ppermute | solution.py:40
  4.3 6.2 %collective-permute-start.1 = (bf16[2,128,256]{2,1,0:T(8,128)(2,1)}, bf16[2,128,256]{2,1,0:T(8,128)(2,1)S(1)}, u32[]{:S(2)}, u32[]{:S(2)}) collective-permute-start(bf16[2,128,256]{2,1,0:T(8,128)(2,1)} %bitcast.27), channel_id=1, source_target_pairs={{0,3},{1,0},{2,1},{3,2},{4,7},{5,4},{6,5},{7,6},{8,11},{9,8},{10,9... | collective-permute-start | bytes 393224 | tf_op jit(solution)/shard_map/ppermute | solution.py:40
  5.1 7.6 %collective-permute-start = (bf16[2,128,256]{2,1,0:T(8,128)(2,1)}, bf16[2,128,256]{2,1,0:T(8,128)(2,1)S(1)}, u32[]{:S(2)}, u32[]{:S(2)}) collective-permute-start(bf16[2,128,256]{2,1,0:T(8,128)(2,1)} %bitcast.28), channel_id=1, source_target_pairs={{0,1},{1,2},{2,3},{3,0},{4,5},{5,6},{6,7},{7,4},{8,9},{9,10},{10,1... | collective-permute-start | bytes 393224 | tf_op jit(solution)/shard_map/ppermute | solution.py:40
  12.7 0.9 copy-start
  14.2 6.4 %collective-permute-start.3 = (bf16[4,128,256]{2,1,0:T(8,128)(2,1)S(1)}, bf16[4,128,256]{2,1,0:T(8,128)(2,1)S(1)}, u32[]{:S(2)}, u32[]{:S(2)}) collective-permute-start(bf16[4,128,256]{2,1,0:T(8,128)(2,1)S(1)} %get-tuple-element.14.second.c2), channel_id=1, source_target_pairs={{0,4},{4,8},{8,12},{12,16},{16,20},{20,24},{24,28},{28,32},{32,36}... | collective-permute-start | bytes 786440 | tf_op jit(solution)/shard_map/ppermute | solution.py:62
  17.4 7.7 %collective-permute-start.4 = (bf16[4,128,256]{2,1,0:T(8,128)(2,1)S(1)}, bf16[4,128,256]{2,1,0:T(8,128)(2,1)S(1)}, u32[]{:S(2)}, u32[]{:S(2)}) collective-permute-start(bf16[4,128,256]{2,1,0:T(8,128)(2,1)S(1)} %get-tuple-element.15.first.c1), channel_id=1, source_target_pairs={{4,0},{8,4},{12,8},{16,12},{20,16},{24,20},{28,24},{32,28},{36,32}... | collective-permute-start | bytes 786440 | tf_op jit(solution)/shard_map/ppermute | solution.py:62
  25.0 2.0 %copy-start.1 = (bf16[3,3,3,256,256]{4,3,2,1,0:T(8,128)(2,1)S(1)}, bf16[3,3,3,256,256]{4,3,2,1,0:T(8,128)(2,1)}, u32[]{:S(2)}) copy-start(bf16[3,3,3,256,256]{4,3,2,1,0:T(8,128)(2,1)} %weight.1) | copy-start | bytes 10616836
  27.0 0.7 copy-start.3
  27.7 0.7 copy-start.4
  31.8 5.9 %collective-permute-start.5 = (bf16[4,128,256]{2,1,0:T(8,128)(2,1)S(1)}, bf16[4,128,256]{2,1,0:T(8,128)(2,1)S(1)}, u32[]{:S(2)}, u32[]{:S(2)}) collective-permute-start(bf16[4,128,256]{2,1,0:T(8,128)(2,1)S(1)} %get-tuple-element.16.second.s1), channel_id=1, source_target_pairs={{0,4},{4,8},{8,12},{12,16},{16,20},{20,24},{24,28},{28,32},{32,36}... | collective-permute-start | bytes 786440 | tf_op jit(solution)/shard_map/ppermute | solution.py:62
  33.7 8.8 %collective-permute-start.6 = (bf16[4,128,256]{2,1,0:T(8,128)(2,1)S(1)}, bf16[4,128,256]{2,1,0:T(8,128)(2,1)S(1)}, u32[]{:S(2)}, u32[]{:S(2)}) collective-permute-start(bf16[4,128,256]{2,1,0:T(8,128)(2,1)S(1)} %get-tuple-element.17.first.s0), channel_id=1, source_target_pairs={{4,0},{8,4},{12,8},{16,12},{20,16},{24,20},{28,24},{32,28},{36,32}... | collective-permute-start | bytes 786440 | tf_op jit(solution)/shard_map/ppermute | solution.py:62
  42.5 13.8 %copy-start.2 = (bf16[3,3,3,256,256]{4,3,2,1,0:T(8,128)(2,1)S(1)}, bf16[3,3,3,256,256]{4,3,2,1,0:T(8,128)(2,1)}, u32[]{:S(2)}) copy-start(bf16[3,3,3,256,256]{4,3,2,1,0:T(8,128)(2,1)} %weight.1) | copy-start | bytes 10616836
  42.5 13.8 %copy-start.5 = (f32[256]{0:T(256)S(1)}, f32[256]{0:T(256)}, u32[]{:S(2)}) copy-start(f32[256]{0:T(256)} %param.7) | copy-start | bytes 3076
  45.7 5.2 %collective-permute-start.7 = (bf16[4,128,256]{2,1,0:T(8,128)(2,1)S(1)}, bf16[4,128,256]{2,1,0:T(8,128)(2,1)S(1)}, u32[]{:S(2)}, u32[]{:S(2)}) collective-permute-start(bf16[4,128,256]{2,1,0:T(8,128)(2,1)S(1)} %get-tuple-element.18.i2), channel_id=1, source_target_pairs={{0,4},{4,8},{8,12},{12,16},{16,20},{20,24},{24,28},{28,32},{32,36}... | collective-permute-start | bytes 786440 | tf_op jit(solution)/shard_map/ppermute | solution.py:62
  47.6 8.6 %collective-permute-start.8 = (bf16[4,128,256]{2,1,0:T(8,128)(2,1)S(1)}, bf16[4,128,256]{2,1,0:T(8,128)(2,1)S(1)}, u32[]{:S(2)}, u32[]{:S(2)}) collective-permute-start(bf16[4,128,256]{2,1,0:T(8,128)(2,1)S(1)} %get-tuple-element.19.i1), channel_id=1, source_target_pairs={{4,0},{8,4},{12,8},{16,12},{20,16},{24,20},{28,24},{32,28},{36,32}... | collective-permute-start | bytes 786440 | tf_op jit(solution)/shard_map/ppermute | solution.py:62
  65.2 2.6 %collective-permute-start.9 = (f32[224,8,128]{2,1,0:T(8,128)S(1)}, f32[224,8,128]{2,1,0:T(8,128)S(1)}, u32[]{:S(2)}, u32[]{:S(2)}) collective-permute-start(f32[224,8,128]{2,1,0:T(8,128)S(1)} %get-tuple-element.22), channel_id=1, source_target_pairs={{0,4},{1,5},{2,6},{3,7},{4,0},{5,1},{6,2},{7,3},{8,12},{9,13},{10,... | collective-permute-start | bytes 2752520 | tf_op jit(solution)/shard_map/ppermute | solution.py:40
  117.4 4.9 %collective-permute-start.11 = (f32[8,7,8,128]{3,2,1,0:T(8,128)S(1)}, f32[8,7,8,128]{3,2,1,0:T(8,128)S(1)}, u32[]{:S(2)}, u32[]{:S(2)}) collective-permute-start(f32[8,7,8,128]{3,2,1,0:T(8,128)S(1)} %all_to_all.17), channel_id=1, source_target_pairs={{0,136},{1,137},{2,138},{3,139},{4,7},{5,4},{6,5},{7,6},{8,0},{9,1... | collective-permute-start | bytes 688136 | tf_op jit(solution)/shard_map/ppermute | solution.py:40
  119.1 6.2 %collective-permute-start.10 = (f32[8,7,8,128]{3,2,1,0:T(8,128)S(1)}, f32[8,7,8,128]{3,2,1,0:T(8,128)S(1)}, u32[]{:S(2)}, u32[]{:S(2)}) collective-permute-start(f32[8,7,8,128]{3,2,1,0:T(8,128)S(1)} %all_to_all.17), channel_id=1, source_target_pairs={{0,8},{1,9},{2,10},{3,11},{4,5},{5,6},{6,7},{7,4},{8,128},{9,129},... | collective-permute-start | bytes 688136 | tf_op jit(solution)/shard_map/ppermute | solution.py:40
  122.3 4.8 %collective-permute-start.13 = (f32[4,7,8,128]{3,2,1,0:T(8,128)S(1)}, f32[4,7,8,128]{3,2,1,0:T(8,128)S(1)}, u32[]{:S(2)}, u32[]{:S(2)}) collective-permute-start(f32[4,7,8,128]{3,2,1,0:T(8,128)S(1)} %slice.25), channel_id=1, source_target_pairs={{0,136},{1,137},{2,138},{3,139},{4,7},{5,4},{6,5},{7,6},{8,0},{9,1... | collective-permute-start | bytes 344072 | tf_op jit(solution)/shard_map/ppermute | solution.py:40
  125.3 4.9 %collective-permute-start.12 = (f32[4,7,8,128]{3,2,1,0:T(8,128)S(1)}, f32[4,7,8,128]{3,2,1,0:T(8,128)S(1)}, u32[]{:S(2)}, u32[]{:S(2)}) collective-permute-start(f32[4,7,8,128]{3,2,1,0:T(8,128)S(1)} %slice.24), channel_id=1, source_target_pairs={{0,8},{1,9},{2,10},{3,11},{4,5},{5,6},{6,7},{7,4},{8,128},{9,129},... | collective-permute-start | bytes 344072 | tf_op jit(solution)/shard_map/ppermute | solution.py:40
  130.3 12.6 %collective-permute-start.15 = (f32[32,7,8,128]{3,2,1,0:T(8,128)S(1)}, f32[32,7,8,128]{3,2,1,0:T(8,128)S(1)}, u32[]{:S(2)}, u32[]{:S(2)}) collective-permute-start(f32[32,7,8,128]{3,2,1,0:T(8,128)S(1)} %bitcast.36), channel_id=1, source_target_pairs={{0,3},{1,0},{2,1},{3,2},{4,140},{5,141},{6,142},{7,143},{8,11},{9,... | collective-permute-start | bytes 2752520 | tf_op jit(solution)/shard_map/ppermute | solution.py:40
  131.3 14.1 %collective-permute-start.14 = (f32[32,7,8,128]{3,2,1,0:T(8,128)S(1)}, f32[32,7,8,128]{3,2,1,0:T(8,128)S(1)}, u32[]{:S(2)}, u32[]{:S(2)}) collective-permute-start(f32[32,7,8,128]{3,2,1,0:T(8,128)S(1)} %bitcast.37), channel_id=1, source_target_pairs={{0,1},{1,2},{2,3},{3,0},{4,12},{5,13},{6,14},{7,15},{8,9},{9,10},{... | collective-permute-start | bytes 2752520 | tf_op jit(solution)/shard_map/ppermute | solution.py:40
  143.0 7.7 %collective-permute-start.17 = (f32[16,7,8,128]{3,2,1,0:T(8,128)S(1)}, f32[16,7,8,128]{3,2,1,0:T(8,128)S(1)}, u32[]{:S(2)}, u32[]{:S(2)}) collective-permute-start(f32[16,7,8,128]{3,2,1,0:T(8,128)S(1)} %slice.27), channel_id=1, source_target_pairs={{0,3},{1,0},{2,1},{3,2},{4,140},{5,141},{6,142},{7,143},{8,11},{9,... | collective-permute-start | bytes 1376264 | tf_op jit(solution)/shard_map/ppermute | solution.py:40
  145.4 8.6 %collective-permute-start.16 = (f32[16,7,8,128]{3,2,1,0:T(8,128)S(1)}, f32[16,7,8,128]{3,2,1,0:T(8,128)S(1)}, u32[]{:S(2)}, u32[]{:S(2)}) collective-permute-start(f32[16,7,8,128]{3,2,1,0:T(8,128)S(1)} %slice.26), channel_id=1, source_target_pairs={{0,1},{1,2},{2,3},{3,0},{4,12},{5,13},{6,14},{7,15},{8,9},{9,10},{... | collective-permute-start | bytes 1376264 | tf_op jit(solution)/shard_map/ppermute | solution.py:40
  154.3 15.9 %collective-permute-start.18 = (f32[16,8,7,8,128]{4,3,2,1,0:T(8,128)S(1)}, f32[16,8,7,8,128]{4,3,2,1,0:T(8,128)S(1)}, u32[]{:S(2)}, u32[]{:S(2)}) collective-permute-start(f32[16,8,7,8,128]{4,3,2,1,0:T(8,128)S(1)} %bitcast.24), channel_id=1, source_target_pairs={{0,4},{1,5},{2,6},{3,7},{4,0},{5,1},{6,2},{7,3},{8,12},{9,13},{10,... | collective-permute-start | bytes 11010056 | tf_op jit(solution)/shard_map/ppermute | solution.py:40

commit v3 on v2

--- a/solution.py
+++ b/solution.py
@@ -17,6 +17,8 @@
 TILES = 27 * PART // 8
 PIECE = 7
 PIECES = 32
+CODED = 64
+SPAN = 250.0
 ALL = ("yh", "z", "yl", "c", "x")
 CHAIN = ("z", "yl", "c")
 
@@ -151,22 +153,35 @@
     )
 
 
-def turn_kernel(weight, out):
+def turn_kernel(weight, bias, head, out, same, bias_out, head_out):
     for d in range(3):
-        out[0, 0, 2 - d] = weight[0, 0, d].T
-
-
-def turn_weights(weight):
+        tap = weight[0, 0, d]
+        same[0, 0, d] = tap
+        out[0, 0, 2 - d] = tap.T
+    bias_out[...] = bias[...]
+    head_out[...] = head[...]
+
+
+def turn_weights(weight, bias, head):
+    full = jax.ShapeDtypeStruct((3, 3, 3, CH, CH), BF16)
+    row = jax.ShapeDtypeStruct((1, CH), F32)
+    here = pl.BlockSpec((1, 1, 3, CH, CH), lambda n: (n // 3, n % 3, 0, 0, 0))
+    line = pl.BlockSpec((1, CH), lambda n: (0, 0))
     return pl.pallas_call(
         turn_kernel,
         grid=(9,),
-        out_shape=jax.ShapeDtypeStruct((3, 3, 3, CH, CH), BF16),
-        in_specs=[pl.BlockSpec((1, 1, 3, CH, CH), lambda n: (n // 3, n % 3, 0, 0, 0))],
-        out_specs=pl.BlockSpec((1, 1, 3, CH, CH), lambda n: (2 - n // 3, 2 - n % 3, 0, 0, 0)),
+        out_shape=(full, full, row, row),
+        in_specs=[here, line, line],
+        out_specs=(
+            pl.BlockSpec((1, 1, 3, CH, CH), lambda n: (2 - n // 3, 2 - n % 3, 0, 0, 0)),
+            here,
+            line,
+            line,
+        ),
         compiler_params=params(8 << 20),
-        cost_estimate=cost(2e9, 8 << 20),
+        cost_estimate=cost(2e9, 11 << 20),
         name="turn_weights",
-    )(weight)
+    )(weight, bias, head)
 
 
 FRAME = jax.ShapeDtypeStruct((ROWS, COLS, CH), BF16)
@@ -262,7 +277,8 @@
     total_bias = jnp.sum(sum_bias, axis=0, keepdims=True)
     total_head = jnp.sum(sum_head, axis=0, keepdims=True)
     row = lax.broadcasted_iota(jnp.int32, (8, CH), 0)
-    small = jnp.where(row == 0, total_bias, jnp.where(row == 1, total_head, 0.0))
+    small_bias = jnp.where(row == 0, total_bias, 0.0)
+    small_head = jnp.where(row == 0, total_head, 0.0)
     blocks = []
     for b in range(3):
         block = PENALTY * correlate(turn_i, (s0, s1), b) + correlate(turn_c, (pgb.at[0], pgb.at[1]), b)
@@ -276,8 +292,9 @@
             a, b, d = k // 9, (k // 3) % 3, k % 3
             at = ((b * 3 + a) * 3 + d) * PART
             out[k * 8 : (k + 1) * 8] = total[at : at + PART, lanes].reshape(PART // 8, 8, 128)
-        out[TILES] = small[:, lanes]
-        out[TILES + 1 :] = jnp.zeros((PIECE * PIECES - TILES - 1, 8, 128), F32)
+        out[TILES] = small_bias[:, lanes]
+        out[TILES + 1] = small_head[:, lanes]
+        out[TILES + 2 :] = jnp.zeros((PIECE * PIECES - TILES - 2, 8, 128), F32)
 
     @pl.when(core == 0)
     def _():
@@ -315,6 +332,44 @@
     return jnp.where(distance == 0, 0, jnp.where(distance == 3, 1, distance + 1))
 
 
+def encode_kernel(terms, out):
+    value = terms[0]
+    for n in range(1, 8):
+        value = value + terms[n]
+    most = jnp.max(jnp.abs(value), axis=1, keepdims=True)
+    scale = (most * 1.004).astype(BF16)
+    wide = scale.astype(F32)
+    inverse = jnp.where(wide > 1e-37, 1.0 / jnp.maximum(wide, 1e-37), 0.0)
+    code = jnp.exp2(jnp.abs(value) * inverse * SPAN - SPAN / 2)
+    code = jnp.where(value < 0, -code, code).reshape(PIECE * 8, 128)
+    pad = jnp.zeros((1, 128), F32)
+    tail = jnp.concatenate([wide.reshape(PIECE, 128), pad], axis=0)
+    line = jnp.concatenate([code, tail], axis=0).astype(BF16)
+    for n in range(8):
+        out[n] = line
+
+
+def encode(terms):
+    return pl.pallas_call(
+        encode_kernel,
+        out_shape=jax.ShapeDtypeStruct((8, CODED, 128), BF16),
+        in_specs=[VMEM],
+        out_specs=VMEM,
+        compiler_params=params(4 << 20),
+        cost_estimate=cost(1e6, 1 << 19),
+        name="encode",
+    )(terms)
+
+
+def decode(line):
+    wide = line.astype(F32)
+    level = jnp.log2(jnp.abs(wide[: PIECE * 8])) * (1.0 / SPAN) + 0.5
+    level = jnp.where(wide[: PIECE * 8] < 0, -level, level)
+    return [
+        level[8 * j : 8 * j + 8] * wide[PIECE * 8 + j : PIECE * 8 + j + 1] for j in range(PIECE)
+    ]
+
+
 def assemble_kernel(pos, mine, other, out, small):
     x, core, y = pos[0], pos[1], pos[2]
     part = pl.program_id(0)
@@ -326,27 +381,27 @@
             place = jnp.where(held == 0, at_x * 4 + at_y, at_y * 4 + at_x)
             for z in range(8):
                 piece = row * 8 + z
-                for j in range(PIECE):
+                for j, value in enumerate(decode(ref[place, z])):
                     tile = piece * PIECE + j
                     if tile < TILES:
-                        out[tile // 8, 0, tile % 8, :, lane] = ref[place, z, j]
-                    elif tile == TILES:
-                        small[:, lane] = ref[place, z, j]
+                        out[tile // 8, 0, tile % 8, :, lane] = value
+                    elif tile < TILES + 2:
+                        at = (tile - TILES) * 8
+                        small[at : at + 8, lane] = value
 
 
 def assemble(pos, mine, other):
-    whole = pl.BlockSpec((16, 8, PIECE, 8, 128), lambda i: (0, 0, 0, 0, 0))
     return pl.pallas_call(
         assemble_kernel,
         grid=(ROWS,),
         out_shape=(
             jax.ShapeDtypeStruct((27, ROWS, 8, 8, CH), F32),
-            jax.ShapeDtypeStruct((8, CH), F32),
+            jax.ShapeDtypeStruct((16, CH), F32),
         ),
         in_specs=[SMEM, VMEM, VMEM],
         out_specs=(
             pl.BlockSpec((27, 1, 8, 8, CH), lambda i: (0, i, 0, 0, 0)),
-            pl.BlockSpec((8, CH), lambda i: (0, 0)),
+            pl.BlockSpec((16, CH), lambda i: (0, 0)),
         ),
         compiler_params=params(),
         cost_estimate=cost(1e6, 15 << 20),
@@ -373,10 +428,9 @@
     below = permute(own, along_x(1))
     above = permute(own, along_x(-1))
     across = permute(own, along_x(2))
+    turned, weight, bias, head = turn_weights(weight, bias.reshape(1, CH), head.reshape(1, CH))
+    turned = turned.reshape(3, 3, 3 * CH, CH)
     w9 = weight.reshape(3, 3, 3 * CH, CH)
-    turned = turn_weights(weight).reshape(3, 3, 3 * CH, CH)
-    bias = bias.reshape(1, CH)
-    head = head.reshape(1, CH)
 
     def with_halo(first, second):
         return (chain(second, 1), first, second, chain(first, -1))
@@ -389,15 +443,13 @@
     lines = lax.all_to_all(half.reshape(4, 8, PIECE, 8, 128), ("yh", "yl"), 0, 0, tiled=True)
     line = jnp.sum(lines, axis=0)
     pieces = lax.all_to_all(line, "z", 0, 0, tiled=True)
-    piece = jnp.sum(pieces, axis=0)
-    line = jnp.broadcast_to(piece[None], (8, PIECE, 8, 128))
-    line = lax.all_to_all(line, "z", 0, 0, tiled=True)
+    line = lax.all_to_all(encode(pieces), "z", 0, 0, tiled=True)
     block = ring_gather(line, split_first)
-    mine = ring_gather(block.reshape(32, PIECE, 8, 128), split_second)
-    mine = mine.reshape(16, 8, PIECE, 8, 128)
+    mine = ring_gather(block.reshape(32, CODED, 128), split_second)
+    mine = mine.reshape(16, 8, CODED, 128)
     other = permute(mine, swap_core)
     grad_weight, small = assemble(pos, mine, other)
-    return grad_weight.reshape(3, 3, 3, CH, CH), small[0], small[1]
+    return grad_weight.reshape(3, 3, 3, CH, CH), small[0], small[8]
 
 
 def solution(mesh):

time: 175 us -> 162 us (0.926)
  waiting for transfers between devices: 59.7 us -> 46.6 us
    ppermute x13, waiting for transfers between devices: 43.2 us -> 33.1 us  [permute(): return lax.ppermute(value, ALL, moved(fn))]
    ppermute x6, waiting for transfers between devices: 16.5 us -> 13.5 us  [chain(): return lax.ppermute(value, CHAIN, pairs)]
    unnamed x12 -> x8, local copies, waits for them, and re-layouts: 4.27 us -> 4.26 us
where the time goes in v3:
time: 162 us; the launch traced here: 161 us
  blocking collectives  48.4 us (30%)
  waiting for transfers between devices  46.6 us (29%)
  starting transfers between devices  37.5 us (23%)
  Pallas kernels  22.6 us (14%)
  local copies, waits for them, and re-layouts  4.87 us (3%)
    ppermute x13, waiting for transfers between devices, permute(): return lax.ppermute(value, ALL, moved(fn))  33.1 us
    ppermute x13, starting transfers between devices, permute(): return lax.ppermute(value, ALL, moved(fn))  23 us
    all_to_all x1, blocking collectives, per_device(): pieces = lax.all_to_all(line, 'z', 0, 0, tiled=True)  19.5 us
    all_to_all x1, blocking collectives, per_device(): lax.all_to_all(half.reshape(4, 8, PIECE, 8, 128), ('yh', 'yl'), 0, 0, til...  18.4 us
    ppermute x6, starting transfers between devices, chain(): return lax.ppermute(value, CHAIN, pairs)  14.4 us
    ppermute x6, waiting for transfers between devices, chain(): return lax.ppermute(value, CHAIN, pairs)  13.5 us
    all_to_all x1, blocking collectives, per_device(): line = lax.all_to_all(encode(pieces), 'z', 0, 0, tiled=True)  10.5 us
    pallas_call x1, Pallas kernels, backward(): pl.pallas_call(backward_kernel, out_shape=(jax.ShapeDtypeStruct((PIECE *...  8.92 us
  transfers between devices with their start and end apart: 19, of which 17 were waited for; matrix products, arithmetic and copies ran while one was open for 0% of the time, Pallas kernels for 1%

profile of v3, /device:TPU:1, one launch (start us, length us, event | category | flops | bytes accessed | tf_op | source)
XLA Modules:
  0.0 161.5 jit_solution(16177651263487756742)
XLA Ops:
  0.6 3.6 %collective-permute-start.2 = (bf16[2,128,256]{2,1,0:T(8,128)(2,1)}, bf16[2,128,256]{2,1,0:T(8,128)(2,1)S(1)}, u32[]{:S(2)}, u32[]{:S(2)}) collective-permute-start(bf16[2,128,256]{2,1,0:T(8,128)(2,1)} %bitcast.26), channel_id=1, source_target_pairs={{0,2},{1,3},{2,0},{3,1},{4,6},{5,7},{6,4},{7,5},{8,10},{9,11},{10,... | collective-permute-start | bytes 393224 | tf_op jit(solution)/shard_map/ppermute | solution.py:42
  4.3 0.9 collective-permute-start.1
  5.1 0.6 collective-permute-start
  5.7 0.1 pad_add_fusion.pos_ref.pos
  5.8 1.0 collective-permute-done.2.across
  6.8 3.7 %collective-permute-done.1.above = bf16[2,128,256]{2,1,0:T(8,128)(2,1)S(1)} collective-permute-done((bf16[2,128,256]{2,1,0:T(8,128)(2,1)}, bf16[2,128,256]{2,1,0:T(8,128)(2,1)S(1)}, u32[]{:S(2)}, u32[]{:S(2)}) %collective-permute-start.1) | collective-permute-done | bytes 131104 | tf_op jit(solution)/shard_map/ppermute | solution.py:42
  10.5 2.2 %collective-permute-done.below = bf16[2,128,256]{2,1,0:T(8,128)(2,1)S(1)} collective-permute-done((bf16[2,128,256]{2,1,0:T(8,128)(2,1)}, bf16[2,128,256]{2,1,0:T(8,128)(2,1)S(1)}, u32[]{:S(2)}, u32[]{:S(2)}) %collective-permute-start) | collective-permute-done | bytes 131104 | tf_op jit(solution)/shard_map/ppermute | solution.py:42
  12.7 0.0 copy-start
  12.7 0.9 copy-done
  13.6 0.6 gather_rows.1
  14.2 3.1 %collective-permute-start.3 = (bf16[4,128,256]{2,1,0:T(8,128)(2,1)S(1)}, bf16[4,128,256]{2,1,0:T(8,128)(2,1)S(1)}, u32[]{:S(2)}, u32[]{:S(2)}) collective-permute-start(bf16[4,128,256]{2,1,0:T(8,128)(2,1)S(1)} %get-tuple-element.18.second.c2), channel_id=1, source_target_pairs={{0,4},{4,8},{8,12},{12,16},{16,20},{20,24},{24,28},{28,32},{32,36}... | collective-permute-start | bytes 786440 | tf_op jit(solution)/shard_map/ppermute | solution.py:64
  17.4 1.9 %collective-permute-start.4 = (bf16[4,128,256]{2,1,0:T(8,128)(2,1)S(1)}, bf16[4,128,256]{2,1,0:T(8,128)(2,1)S(1)}, u32[]{:S(2)}, u32[]{:S(2)}) collective-permute-start(bf16[4,128,256]{2,1,0:T(8,128)(2,1)S(1)} %get-tuple-element.19.first.c1), channel_id=1, source_target_pairs={{4,0},{8,4},{12,8},{16,12},{20,16},{24,20},{28,24},{32,28},{36,32}... | collective-permute-start | bytes 786440 | tf_op jit(solution)/shard_map/ppermute | solution.py:64
  19.3 0.0 copy-start.1
  19.3 2.0 %copy-done.1 = bf16[3,3,3,256,256]{4,3,2,1,0:T(8,128)(2,1)S(1)} copy-done((bf16[3,3,3,256,256]{4,3,2,1,0:T(8,128)(2,1)S(1)}, bf16[3,3,3,256,256]{4,3,2,1,0:T(8,128)(2,1)}, u32[]{:S(2)}) %copy-start.1) | copy-done | bytes 3538968
  21.3 0.0 copy-start.2
  21.3 0.7 copy-done.2
  22.0 0.0 copy-start.3
  22.0 0.7 copy-done.3
  22.6 1.7 %turn_weights.1 = (bf16[3,3,3,256,256]{4,3,2,1,0:T(8,128)(2,1)S(1)}, bf16[3,3,3,256,256]{4,3,2,1,0:T(8,128)(2,1)S(1)}, f32[1,256]{1,0:T(1,128)S(1)}, f32[1,256]{1,0:T(1,128)S(1)}) custom-call(bf16[3,3,3,256,256]{4,3,2,1,0:T(8,128)(2,1)S(1)} %copy-done.1, f32[1,256]{1,0:T(1,128)S(1)} %bitcast.30, f32[1,256]{1,0:T(1,128)S(1)} %bitcast.31), custom_call_target="tpu_custom_call" | custom-call | flops 2000000000 | bytes 11534336 | tf_op jit(solution)/shard_map/turn_weights/pallas_call | solution.py:170
  24.3 0.0 collective-permute-done.3.prev.c0
  24.3 0.7 collective-permute-done.4.follow.c3
  25.0 3.4 %forward.1 = (f32[2,4,128,256]{3,2,1,0:T(8,128)S(1)}, bf16[4,128,256]{2,1,0:T(8,128)(2,1)S(1)}, bf16[4,128,256]{2,1,0:T(8,128)(2,1)S(1)}) custom-call(bf16[4,128,256]{2,1,0:T(8,128)(2,1)S(1)} %collective-permute-done.3.prev.c0, bf16[4,128,256]{2,1,0:T(8,128)(2,1)S(1)} %get-tuple-element.19.first.c1, bf16[4,128,256]{2,1,0:T(8,128)(2,1)S(1)} %get-tuple-element.18.second.c2, ...), custom_call_target="tpu_custom_call" | custom-call | flops 3623878656 | bytes 6291456 | tf_op jit(solution)/shard_map/forward/pallas_call | solution.py:193
  28.4 2.9 %collective-permute-start.5 = (bf16[4,128,256]{2,1,0:T(8,128)(2,1)S(1)}, bf16[4,128,256]{2,1,0:T(8,128)(2,1)S(1)}, u32[]{:S(2)}, u32[]{:S(2)}) collective-permute-start(bf16[4,128,256]{2,1,0:T(8,128)(2,1)S(1)} %get-tuple-element.23.second.s1), channel_id=1, source_target_pairs={{0,4},{4,8},{8,12},{12,16},{16,20},{20,24},{24,28},{28,32},{32,36}... | collective-permute-start | bytes 786440 | tf_op jit(solution)/shard_map/ppermute | solution.py:64
  31.4 1.9 %collective-permute-start.6 = (bf16[4,128,256]{2,1,0:T(8,128)(2,1)S(1)}, bf16[4,128,256]{2,1,0:T(8,128)(2,1)S(1)}, u32[]{:S(2)}, u32[]{:S(2)}) collective-permute-start(bf16[4,128,256]{2,1,0:T(8,128)(2,1)S(1)} %get-tuple-element.24.first.s0), channel_id=1, source_target_pairs={{4,0},{8,4},{12,8},{16,12},{20,16},{24,20},{28,24},{32,28},{36,32}... | collective-permute-start | bytes 786440 | tf_op jit(solution)/shard_map/ppermute | solution.py:64
  33.3 1.4 collective-permute-done.5.prev
  34.7 4.5 %collective-permute-done.6.follow = bf16[4,128,256]{2,1,0:T(8,128)(2,1)S(1)} collective-permute-done((bf16[4,128,256]{2,1,0:T(8,128)(2,1)S(1)}, bf16[4,128,256]{2,1,0:T(8,128)(2,1)S(1)}, u32[]{:S(2)}, u32[]{:S(2)}) %collective-permute-start.6) | collective-permute-done | bytes 262176 | tf_op jit(solution)/shard_map/ppermute | solution.py:64
  39.1 3.2 %transposed.1 = (bf16[4,128,256]{2,1,0:T(8,128)(2,1)S(1)}, bf16[4,128,256]{2,1,0:T(8,128)(2,1)S(1)}) custom-call(bf16[4,128,256]{2,1,0:T(8,128)(2,1)S(1)} %collective-permute-done.5.prev, bf16[4,128,256]{2,1,0:T(8,128)(2,1)S(1)} %get-tuple-element.24.first.s0, bf16[4,128,256]{2,1,0:T(8,128)(2,1)S(1)} %get-tuple-element.23.second.s1, ...), custom_call_target="tpu_custom_call" | custom-call | flops 3623878656 | bytes 5242880 | tf_op jit(solution)/shard_map/transposed/pallas_call | solution.py:207
  42.3 1.9 %collective-permute-start.7 = (bf16[4,128,256]{2,1,0:T(8,128)(2,1)S(1)}, bf16[4,128,256]{2,1,0:T(8,128)(2,1)S(1)}, u32[]{:S(2)}, u32[]{:S(2)}) collective-permute-start(bf16[4,128,256]{2,1,0:T(8,128)(2,1)S(1)} %get-tuple-element.26.i2), channel_id=1, source_target_pairs={{0,4},{4,8},{8,12},{12,16},{16,20},{20,24},{24,28},{28,32},{32,36}... | collective-permute-start | bytes 786440 | tf_op jit(solution)/shard_map/ppermute | solution.py:64
  44.3 2.6 %collective-permute-start.8 = (bf16[4,128,256]{2,1,0:T(8,128)(2,1)S(1)}, bf16[4,128,256]{2,1,0:T(8,128)(2,1)S(1)}, u32[]{:S(2)}, u32[]{:S(2)}) collective-permute-start(bf16[4,128,256]{2,1,0:T(8,128)(2,1)S(1)} %get-tuple-element.27.i1), channel_id=1, source_target_pairs={{4,0},{8,4},{12,8},{16,12},{20,16},{24,20},{28,24},{32,28},{36,32}... | collective-permute-start | bytes 786440 | tf_op jit(solution)/shard_map/ppermute | solution.py:64
  46.9 0.7 collective-permute-done.7.i0
  47.6 6.3 %collective-permute-done.8.i3 = bf16[4,128,256]{2,1,0:T(8,128)(2,1)S(1)} collective-permute-done((bf16[4,128,256]{2,1,0:T(8,128)(2,1)S(1)}, bf16[4,128,256]{2,1,0:T(8,128)(2,1)S(1)}, u32[]{:S(2)}, u32[]{:S(2)}) %collective-permute-start.8) | collective-permute-done | bytes 262176 | tf_op jit(solution)/shard_map/ppermute | solution.py:64
  53.9 8.9 %backward.1 = (f32[224,8,128]{2,1,0:T(8,128)S(1)}, f32[224,8,128]{2,1,0:T(8,128)S(1)}) custom-call(s32[3]{0:T(128)S(1)} %pad_add_fusion.pos_ref.pos, bf16[4,128,256]{2,1,0:T(8,128)(2,1)S(1)} %collective-permute-done.7.i0, bf16[4,128,256]{2,1,0:T(8,128)(2,1)S(1)} %get-tuple-element.27.i1, bf16[4,128,256]{2,1,0:T(8,128)(2,1)S(1)} %get-tuple-element.26.i2, ...), custom_call_target="tpu_custom_call" | custom-call | flops 5798205952 | bytes 10485760 | tf_op jit(solution)/shard_map/backward/pallas_call | solution.py:312
  62.8 0.1 collective-permute-start.9
  62.9 2.5 %collective-permute-done.9 = f32[224,8,128]{2,1,0:T(8,128)S(1)} collective-permute-done((f32[224,8,128]{2,1,0:T(8,128)S(1)}, f32[224,8,128]{2,1,0:T(8,128)S(1)}, u32[]{:S(2)}, u32[]{:S(2)}) %collective-permute-start.9) | collective-permute-done | bytes 917536 | tf_op jit(solution)/shard_map/ppermute | solution.py:42
  65.4 0.1 add.7
  65.5 18.4 %all_to_all.15 = f32[4,8,7,8,128]{4,3,2,1,0:T(8,128)S(1)} all-to-all(f32[4,8,7,8,128]{4,3,2,1,0:T(8,128)S(1)} %bitcast.35), channel_id=1, replica_groups=mesh['yh'=2,'z'=8,'yl'=2,'c'=2,'x'=4] {'yh','yl'}, dimensions={0} | all-to-all | bytes 1835008 | tf_op jit(solution)/shard_map/all_to_all | solution.py:443
  83.9 0.1 reduce_sum.9
  84.0 19.5 %all_to_all.16.terms = f32[8,7,8,128]{3,2,1,0:T(8,128)S(1)} all-to-all(f32[8,7,8,128]{3,2,1,0:T(8,128)S(1)} %reduce_sum.9), channel_id=1, replica_groups=mesh['yh'=2,'z'=8,'yl'=2,'c'=2,'x'=4] {'z'}, dimensions={0} | all-to-all | bytes 458752 | tf_op jit(solution)/shard_map/all_to_all | solution.py:445
  103.5 0.1 encode.1
  103.5 10.5 %all_to_all.17 = bf16[8,64,128]{2,1,0:T(8,128)(2,1)S(1)} all-to-all(bf16[8,64,128]{2,1,0:T(8,128)(2,1)S(1)} %encode.1), channel_id=1, replica_groups=mesh['yh'=2,'z'=8,'yl'=2,'c'=2,'x'=4] {'z'}, dimensions={0} | all-to-all | bytes 262144 | tf_op jit(solution)/shard_map/all_to_all | solution.py:446
  114.0 1.7 %collective-permute-start.11 = (bf16[8,64,128]{2,1,0:T(8,128)(2,1)S(1)}, bf16[8,64,128]{2,1,0:T(8,128)(2,1)S(1)}, u32[]{:S(2)}, u32[]{:S(2)}) collective-permute-start(bf16[8,64,128]{2,1,0:T(8,128)(2,1)S(1)} %all_to_all.17), channel_id=1, source_target_pairs={{0,136},{1,137},{2,138},{3,139},{4,7},{5,4},{6,5},{7,6},{8,0},{9,1... | collective-permute-start | bytes 393224 | tf_op jit(solution)/shard_map/ppermute | solution.py:42
  115.7 0.0 collective-permute-start.10
  115.7 2.1 %collective-permute-done.11 = bf16[8,64,128]{2,1,0:T(8,128)(2,1)S(1)} collective-permute-done((bf16[8,64,128]{2,1,0:T(8,128)(2,1)S(1)}, bf16[8,64,128]{2,1,0:T(8,128)(2,1)S(1)}, u32[]{:S(2)}, u32[]{:S(2)}) %collective-permute-start.11) | collective-permute-done | bytes 131104 | tf_op jit(solution)/shard_map/ppermute | solution.py:42
  117.8 2.9 %collective-permute-start.13 = (bf16[4,64,128]{2,1,0:T(8,128)(2,1)S(1)}, bf16[4,64,128]{2,1,0:T(8,128)(2,1)S(1)}, u32[]{:S(2)}, u32[]{:S(2)}) collective-permute-start(bf16[4,64,128]{2,1,0:T(8,128)(2,1)S(1)} %slice.25), channel_id=1, source_target_pairs={{0,136},{1,137},{2,138},{3,139},{4,7},{5,4},{6,5},{7,6},{8,0},{9,1... | collective-permute-start | bytes 196616 | tf_op jit(solution)/shard_map/ppermute | solution.py:42
  120.7 0.0 collective-permute-done.10
  120.7 0.1 collective-permute-start.12
  120.8 1.2 collective-permute-done.13
  122.1 3.1 %collective-permute-done.12 = bf16[4,64,128]{2,1,0:T(8,128)(2,1)S(1)} collective-permute-done((bf16[4,64,128]{2,1,0:T(8,128)(2,1)S(1)}, bf16[4,64,128]{2,1,0:T(8,128)(2,1)S(1)}, u32[]{:S(2)}, u32[]{:S(2)}) %collective-permute-start.12) | collective-permute-done | bytes 65568 | tf_op jit(solution)/shard_map/ppermute | solution.py:42
  125.2 0.1 pad_maximum_fusion.1
  125.2 1.0 collective-permute-start.15
  126.2 0.6 collective-permute-start.14
  126.8 6.6 %collective-permute-done.15 = bf16[32,64,128]{2,1,0:T(8,128)(2,1)S(1)} collective-permute-done((bf16[32,64,128]{2,1,0:T(8,128)(2,1)S(1)}, bf16[32,64,128]{2,1,0:T(8,128)(2,1)S(1)}, u32[]{:S(2)}, u32[]{:S(2)}) %collective-permute-start.15) | collective-permute-done | bytes 524320 | tf_op jit(solution)/shard_map/ppermute | solution.py:42
  133.4 2.2 %collective-permute-start.17 = (bf16[16,64,128]{2,1,0:T(8,128)(2,1)S(1)}, bf16[16,64,128]{2,1,0:T(8,128)(2,1)S(1)}, u32[]{:S(2)}, u32[]{:S(2)}) collective-permute-start(bf16[16,64,128]{2,1,0:T(8,128)(2,1)S(1)} %slice.27), channel_id=1, source_target_pairs={{0,3},{1,0},{2,1},{3,2},{4,140},{5,141},{6,142},{7,143},{8,11},{9,... | collective-permute-start | bytes 786440 | tf_op jit(solution)/shard_map/ppermute | solution.py:42
  135.6 0.2 collective-permute-done.14
  135.8 0.1 collective-permute-start.16
  135.9 3.1 %collective-permute-done.17 = bf16[16,64,128]{2,1,0:T(8,128)(2,1)S(1)} collective-permute-done((bf16[16,64,128]{2,1,0:T(8,128)(2,1)S(1)}, bf16[16,64,128]{2,1,0:T(8,128)(2,1)S(1)}, u32[]{:S(2)}, u32[]{:S(2)}) %collective-permute-start.17) | collective-permute-done | bytes 262176 | tf_op jit(solution)/shard_map/ppermute | solution.py:42
  139.0 3.6 %collective-permute-done.16 = bf16[16,64,128]{2,1,0:T(8,128)(2,1)S(1)} collective-permute-done((bf16[16,64,128]{2,1,0:T(8,128)(2,1)S(1)}, bf16[16,64,128]{2,1,0:T(8,128)(2,1)S(1)}, u32[]{:S(2)}, u32[]{:S(2)}) %collective-permute-start.16) | collective-permute-done | bytes 262176 | tf_op jit(solution)/shard_map/ppermute | solution.py:42
  142.6 0.3 pad_maximum_fusion
  142.9 9.4 %collective-permute-start.18 = (bf16[16,8,64,128]{3,2,1,0:T(8,128)(2,1)S(1)}, bf16[16,8,64,128]{3,2,1,0:T(8,128)(2,1)S(1)}, u32[]{:S(2)}, u32[]{:S(2)}) collective-permute-start(bf16[16,8,64,128]{3,2,1,0:T(8,128)(2,1)S(1)} %bitcast.24), channel_id=1, source_target_pairs={{0,4},{1,5},{2,6},{3,7},{4,0},{5,1},{6,2},{7,3},{8,12},{9,13},{10,... | collective-permute-start | bytes 6291464 | tf_op jit(solution)/shard_map/ppermute | solution.py:42
  152.3 3.8 %collective-permute-done.18.other = bf16[16,8,64,128]{3,2,1,0:T(8,128)(2,1)S(1)} collective-permute-done((bf16[16,8,64,128]{3,2,1,0:T(8,128)(2,1)S(1)}, bf16[16,8,64,128]{3,2,1,0:T(8,128)(2,1)S(1)}, u32[]{:S(2)}, u32[]{:S(2)}) %collective-permute-start.18) | collective-permute-done | bytes 2097184 | tf_op jit(solution)/shard_map/ppermute | solution.py:42
  156.0 4.8 %assemble.1 = (f32[27,4,8,8,256]{4,3,2,1,0:T(8,128)}, f32[16,256]{1,0:T(8,128)S(1)}) custom-call(s32[3]{0:T(128)S(1)} %pad_add_fusion.pos_ref.pos, bf16[16,8,64,128]{3,2,1,0:T(8,128)(2,1)S(1)} %bitcast.25, bf16[16,8,64,128]{3,2,1,0:T(8,128)(2,1)S(1)} %collective-permute-done.18.other), custom_call_target="tpu_custom_call" | custom-call | flops 1000000 | bytes 15728640 | tf_op jit(solution)/shard_map/assemble/pallas_call | solution.py:394
  160.9 0.6 fusion
  (6 shorter events, 0.1 us)
Async XLA Ops:
  0.6 6.2 %collective-permute-start.2 = (bf16[2,128,256]{2,1,0:T(8,128)(2,1)}, bf16[2,128,256]{2,1,0:T(8,128)(2,1)S(1)}, u32[]{:S(2)}, u32[]{:S(2)}) collective-permute-start(bf16[2,128,256]{2,1,0:T(8,128)(2,1)} %bitcast.26), channel_id=1, source_target_pairs={{0,2},{1,3},{2,0},{3,1},{4,6},{5,7},{6,4},{7,5},{8,10},{9,11},{10,... | collective-permute-start | bytes 393224 | tf_op jit(solution)/shard_map/ppermute | solution.py:42
  4.3 6.2 %collective-permute-start.1 = (bf16[2,128,256]{2,1,0:T(8,128)(2,1)}, bf16[2,128,256]{2,1,0:T(8,128)(2,1)S(1)}, u32[]{:S(2)}, u32[]{:S(2)}) collective-permute-start(bf16[2,128,256]{2,1,0:T(8,128)(2,1)} %bitcast.27), channel_id=1, source_target_pairs={{0,3},{1,0},{2,1},{3,2},{4,7},{5,4},{6,5},{7,6},{8,11},{9,8},{10,9... | collective-permute-start | bytes 393224 | tf_op jit(solution)/shard_map/ppermute | solution.py:42
  5.1 7.6 %collective-permute-start = (bf16[2,128,256]{2,1,0:T(8,128)(2,1)}, bf16[2,128,256]{2,1,0:T(8,128)(2,1)S(1)}, u32[]{:S(2)}, u32[]{:S(2)}) collective-permute-start(bf16[2,128,256]{2,1,0:T(8,128)(2,1)} %bitcast.28), channel_id=1, source_target_pairs={{0,1},{1,2},{2,3},{3,0},{4,5},{5,6},{6,7},{7,4},{8,9},{9,10},{10,1... | collective-permute-start | bytes 393224 | tf_op jit(solution)/shard_map/ppermute | solution.py:42
  12.7 0.9 copy-start
  14.2 10.1 %collective-permute-start.3 = (bf16[4,128,256]{2,1,0:T(8,128)(2,1)S(1)}, bf16[4,128,256]{2,1,0:T(8,128)(2,1)S(1)}, u32[]{:S(2)}, u32[]{:S(2)}) collective-permute-start(bf16[4,128,256]{2,1,0:T(8,128)(2,1)S(1)} %get-tuple-element.18.second.c2), channel_id=1, source_target_pairs={{0,4},{4,8},{8,12},{12,16},{16,20},{20,24},{24,28},{28,32},{32,36}... | collective-permute-start | bytes 786440 | tf_op jit(solution)/shard_map/ppermute | solution.py:64
  17.4 7.7 %collective-permute-start.4 = (bf16[4,128,256]{2,1,0:T(8,128)(2,1)S(1)}, bf16[4,128,256]{2,1,0:T(8,128)(2,1)S(1)}, u32[]{:S(2)}, u32[]{:S(2)}) collective-permute-start(bf16[4,128,256]{2,1,0:T(8,128)(2,1)S(1)} %get-tuple-element.19.first.c1), channel_id=1, source_target_pairs={{4,0},{8,4},{12,8},{16,12},{20,16},{24,20},{28,24},{32,28},{36,32}... | collective-permute-start | bytes 786440 | tf_op jit(solution)/shard_map/ppermute | solution.py:64
  19.3 2.0 %copy-start.1 = (bf16[3,3,3,256,256]{4,3,2,1,0:T(8,128)(2,1)S(1)}, bf16[3,3,3,256,256]{4,3,2,1,0:T(8,128)(2,1)}, u32[]{:S(2)}) copy-start(bf16[3,3,3,256,256]{4,3,2,1,0:T(8,128)(2,1)} %weight.1) | copy-start | bytes 10616836
  21.3 0.7 copy-start.2
  22.0 0.7 copy-start.3
  28.4 6.2 %collective-permute-start.5 = (bf16[4,128,256]{2,1,0:T(8,128)(2,1)S(1)}, bf16[4,128,256]{2,1,0:T(8,128)(2,1)S(1)}, u32[]{:S(2)}, u32[]{:S(2)}) collective-permute-start(bf16[4,128,256]{2,1,0:T(8,128)(2,1)S(1)} %get-tuple-element.23.second.s1), channel_id=1, source_target_pairs={{0,4},{4,8},{8,12},{12,16},{16,20},{20,24},{24,28},{28,32},{32,36}... | collective-permute-start | bytes 786440 | tf_op jit(solution)/shard_map/ppermute | solution.py:64
  31.4 7.7 %collective-permute-start.6 = (bf16[4,128,256]{2,1,0:T(8,128)(2,1)S(1)}, bf16[4,128,256]{2,1,0:T(8,128)(2,1)S(1)}, u32[]{:S(2)}, u32[]{:S(2)}) collective-permute-start(bf16[4,128,256]{2,1,0:T(8,128)(2,1)S(1)} %get-tuple-element.24.first.s0), channel_id=1, source_target_pairs={{4,0},{8,4},{12,8},{16,12},{20,16},{24,20},{28,24},{32,28},{36,32}... | collective-permute-start | bytes 786440 | tf_op jit(solution)/shard_map/ppermute | solution.py:64
  42.3 5.2 %collective-permute-start.7 = (bf16[4,128,256]{2,1,0:T(8,128)(2,1)S(1)}, bf16[4,128,256]{2,1,0:T(8,128)(2,1)S(1)}, u32[]{:S(2)}, u32[]{:S(2)}) collective-permute-start(bf16[4,128,256]{2,1,0:T(8,128)(2,1)S(1)} %get-tuple-element.26.i2), channel_id=1, source_target_pairs={{0,4},{4,8},{8,12},{12,16},{16,20},{20,24},{24,28},{28,32},{32,36}... | collective-permute-start | bytes 786440 | tf_op jit(solution)/shard_map/ppermute | solution.py:64
  44.3 9.6 %collective-permute-start.8 = (bf16[4,128,256]{2,1,0:T(8,128)(2,1)S(1)}, bf16[4,128,256]{2,1,0:T(8,128)(2,1)S(1)}, u32[]{:S(2)}, u32[]{:S(2)}) collective-permute-start(bf16[4,128,256]{2,1,0:T(8,128)(2,1)S(1)} %get-tuple-element.27.i1), channel_id=1, source_target_pairs={{4,0},{8,4},{12,8},{16,12},{20,16},{24,20},{28,24},{32,28},{36,32}... | collective-permute-start | bytes 786440 | tf_op jit(solution)/shard_map/ppermute | solution.py:64
  62.8 2.6 %collective-permute-start.9 = (f32[224,8,128]{2,1,0:T(8,128)S(1)}, f32[224,8,128]{2,1,0:T(8,128)S(1)}, u32[]{:S(2)}, u32[]{:S(2)}) collective-permute-start(f32[224,8,128]{2,1,0:T(8,128)S(1)} %get-tuple-element.30), channel_id=1, source_target_pairs={{0,4},{1,5},{2,6},{3,7},{4,0},{5,1},{6,2},{7,3},{8,12},{9,13},{10,... | collective-permute-start | bytes 2752520 | tf_op jit(solution)/shard_map/ppermute | solution.py:42
  114.0 3.8 %collective-permute-start.11 = (bf16[8,64,128]{2,1,0:T(8,128)(2,1)S(1)}, bf16[8,64,128]{2,1,0:T(8,128)(2,1)S(1)}, u32[]{:S(2)}, u32[]{:S(2)}) collective-permute-start(bf16[8,64,128]{2,1,0:T(8,128)(2,1)S(1)} %all_to_all.17), channel_id=1, source_target_pairs={{0,136},{1,137},{2,138},{3,139},{4,7},{5,4},{6,5},{7,6},{8,0},{9,1... | collective-permute-start | bytes 393224 | tf_op jit(solution)/shard_map/ppermute | solution.py:42
  115.7 5.0 %collective-permute-start.10 = (bf16[8,64,128]{2,1,0:T(8,128)(2,1)S(1)}, bf16[8,64,128]{2,1,0:T(8,128)(2,1)S(1)}, u32[]{:S(2)}, u32[]{:S(2)}) collective-permute-start(bf16[8,64,128]{2,1,0:T(8,128)(2,1)S(1)} %all_to_all.17), channel_id=1, source_target_pairs={{0,8},{1,9},{2,10},{3,11},{4,5},{5,6},{6,7},{7,4},{8,128},{9,129},... | collective-permute-start | bytes 393224 | tf_op jit(solution)/shard_map/ppermute | solution.py:42
  117.8 4.2 %collective-permute-start.13 = (bf16[4,64,128]{2,1,0:T(8,128)(2,1)S(1)}, bf16[4,64,128]{2,1,0:T(8,128)(2,1)S(1)}, u32[]{:S(2)}, u32[]{:S(2)}) collective-permute-start(bf16[4,64,128]{2,1,0:T(8,128)(2,1)S(1)} %slice.25), channel_id=1, source_target_pairs={{0,136},{1,137},{2,138},{3,139},{4,7},{5,4},{6,5},{7,6},{8,0},{9,1... | collective-permute-start | bytes 196616 | tf_op jit(solution)/shard_map/ppermute | solution.py:42
  120.7 4.4 %collective-permute-start.12 = (bf16[4,64,128]{2,1,0:T(8,128)(2,1)S(1)}, bf16[4,64,128]{2,1,0:T(8,128)(2,1)S(1)}, u32[]{:S(2)}, u32[]{:S(2)}) collective-permute-start(bf16[4,64,128]{2,1,0:T(8,128)(2,1)S(1)} %slice.24), channel_id=1, source_target_pairs={{0,8},{1,9},{2,10},{3,11},{4,5},{5,6},{6,7},{7,4},{8,128},{9,129},... | collective-permute-start | bytes 196616 | tf_op jit(solution)/shard_map/ppermute | solution.py:42
  125.2 8.1 %collective-permute-start.15 = (bf16[32,64,128]{2,1,0:T(8,128)(2,1)S(1)}, bf16[32,64,128]{2,1,0:T(8,128)(2,1)S(1)}, u32[]{:S(2)}, u32[]{:S(2)}) collective-permute-start(bf16[32,64,128]{2,1,0:T(8,128)(2,1)S(1)} %bitcast.36), channel_id=1, source_target_pairs={{0,3},{1,0},{2,1},{3,2},{4,140},{5,141},{6,142},{7,143},{8,11},{9,... | collective-permute-start | bytes 1572872 | tf_op jit(solution)/shard_map/ppermute | solution.py:42
  126.2 9.5 %collective-permute-start.14 = (bf16[32,64,128]{2,1,0:T(8,128)(2,1)S(1)}, bf16[32,64,128]{2,1,0:T(8,128)(2,1)S(1)}, u32[]{:S(2)}, u32[]{:S(2)}) collective-permute-start(bf16[32,64,128]{2,1,0:T(8,128)(2,1)S(1)} %bitcast.37), channel_id=1, source_target_pairs={{0,1},{1,2},{2,3},{3,0},{4,12},{5,13},{6,14},{7,15},{8,9},{9,10},{... | collective-permute-start | bytes 1572872 | tf_op jit(solution)/shard_map/ppermute | solution.py:42
  133.4 5.6 %collective-permute-start.17 = (bf16[16,64,128]{2,1,0:T(8,128)(2,1)S(1)}, bf16[16,64,128]{2,1,0:T(8,128)(2,1)S(1)}, u32[]{:S(2)}, u32[]{:S(2)}) collective-permute-start(bf16[16,64,128]{2,1,0:T(8,128)(2,1)S(1)} %slice.27), channel_id=1, source_target_pairs={{0,3},{1,0},{2,1},{3,2},{4,140},{5,141},{6,142},{7,143},{8,11},{9,... | collective-permute-start | bytes 786440 | tf_op jit(solution)/shard_map/ppermute | solution.py:42
  135.8 6.8 %collective-permute-start.16 = (bf16[16,64,128]{2,1,0:T(8,128)(2,1)S(1)}, bf16[16,64,128]{2,1,0:T(8,128)(2,1)S(1)}, u32[]{:S(2)}, u32[]{:S(2)}) collective-permute-start(bf16[16,64,128]{2,1,0:T(8,128)(2,1)S(1)} %slice.26), channel_id=1, source_target_pairs={{0,1},{1,2},{2,3},{3,0},{4,12},{5,13},{6,14},{7,15},{8,9},{9,10},{... | collective-permute-start | bytes 786440 | tf_op jit(solution)/shard_map/ppermute | solution.py:42
  142.9 13.1 %collective-permute-start.18 = (bf16[16,8,64,128]{3,2,1,0:T(8,128)(2,1)S(1)}, bf16[16,8,64,128]{3,2,1,0:T(8,128)(2,1)S(1)}, u32[]{:S(2)}, u32[]{:S(2)}) collective-permute-start(bf16[16,8,64,128]{3,2,1,0:T(8,128)(2,1)S(1)} %bitcast.24), channel_id=1, source_target_pairs={{0,4},{1,5},{2,6},{3,7},{4,0},{5,1},{6,2},{7,3},{8,12},{9,13},{10,... | collective-permute-start | bytes 6291464 | tf_op jit(solution)/shard_map/ppermute | solution.py:42

commit v4 on v3

--- a/solution.py
+++ b/solution.py
@@ -20,6 +20,7 @@
 CODED = 64
 SPAN = 250.0
 ALL = ("yh", "z", "yl", "c", "x")
+PLANE = ("yh", "z", "yl")
 CHAIN = ("z", "yl", "c")
 
 
@@ -76,7 +77,8 @@
     return pl.CostEstimate(flops=int(flops), bytes_accessed=int(nbytes), transcendentals=0)
 
 
-def gather_rows_kernel(pos_ref, own, below, above, across, first, second):
+def gather_rows_kernel(pos_ref, own, below, above, across, ready, first, second):
+    del ready
     x = pos_ref[0]
     for shift, ref in ((0, own), (3, below), (1, above), (2, across)):
         row = lax.rem(x + shift, 4)
@@ -84,17 +86,17 @@
         second[row] = ref[1]
 
 
-def gather_rows(pos, own, below, above, across):
+def gather_rows(pos, own, below, above, across, ready):
     out = jax.ShapeDtypeStruct((ROWS, COLS, CH), BF16)
     return pl.pallas_call(
         gather_rows_kernel,
         out_shape=(out, out),
-        in_specs=[SMEM] + [VMEM] * 4,
+        in_specs=[SMEM] + [VMEM] * 5,
         out_specs=(VMEM, VMEM),
         compiler_params=params(),
         cost_estimate=cost(1e6, 1 << 20),
         name="gather_rows",
-    )(pos, own, below, above, across)
+    )(pos, own, below, above, across, ready)
 
 
 def spread_columns(frames, spread):
@@ -113,23 +115,41 @@
 TAPS = [(1, 1), (0, 1), (2, 1), (0, 0), (1, 0), (2, 0), (0, 2), (1, 2), (2, 2)]
 
 
-def convolve(spread, weight, acc):
-    for n, (a, b) in enumerate(TAPS):
-        rows = ROWS if b == 1 else ROWS - 1
-        src = 1 if b == 2 else 0
-        dst = 1 if b == 0 else 0
-        piece = spread[a : a + 2, src : src + rows].reshape(2 * rows * COLS, 3 * CH)
-        term = jnp.dot(piece, weight[a, b], preferred_element_type=F32)
-        term = term.reshape(2, rows, COLS, CH)
-        if n == 0:
-            acc[...] = term
+def row_range(b):
+    return (ROWS, 0, 0) if b == 1 else (ROWS - 1, 1 if b == 2 else 0, 1 if b == 0 else 0)
+
+
+def apply_tap(spread, weight, a, b, f0, count):
+    rows, src, _ = row_range(b)
+    piece = spread[f0 : f0 + count, src : src + rows].reshape(count * rows * COLS, 3 * CH)
+    term = jnp.dot(piece, weight[a, b], preferred_element_type=F32)
+    return term.reshape(count, rows, COLS, CH)
+
+
+def inner_kernel(first, second, weight, acc, spread):
+    spread_columns((first, second), spread)
+    acc[...] = apply_tap(spread, weight, 1, 1, 0, 2)
+    for a, b in TAPS[1:]:
+        rows, _, dst = row_range(b)
+        if a == 1:
+            acc[:, dst : dst + rows] += apply_tap(spread, weight, a, b, 0, 2)
+        elif a == 0:
+            acc[1:2, dst : dst + rows] += apply_tap(spread, weight, a, b, 0, 1)
         else:
-            acc[:, dst : dst + rows] += term
-
-
-def forward_kernel(prev, first, second, follow, weight, bias, head, pre, g0, g1, spread):
-    spread_columns((prev, first, second, follow), spread)
-    convolve(spread, weight, pre)
+            acc[0:1, dst : dst + rows] += apply_tap(spread, weight, a, b, 1, 1)
+
+
+def outer_taps(prev, follow, weight, acc, total, spread):
+    spread_columns((prev, follow), spread)
+    for f, a in ((0, 0), (1, 2)):
+        total[f : f + 1] = acc[f : f + 1] + apply_tap(spread, weight, a, 1, f, 1)
+        for b in (0, 2):
+            rows, _, dst = row_range(b)
+            total[f : f + 1, dst : dst + rows] += apply_tap(spread, weight, a, b, f, 1)
+
+
+def forward_kernel(prev, follow, acc, weight, bias, head, pre, g0, g1, spread):
+    outer_taps(prev, follow, weight, acc, pre, spread)
     for f, out in ((0, g0), (1, g1)):
         for r in range(ROWS):
             value = pre[f, r] + bias[...]
@@ -139,16 +159,15 @@
             out[r] = (head[...] * slope).astype(BF16)
 
 
-def transpose_kernel(prev, first, second, follow, weight, g0, g1, spread, acc):
-    spread_columns((prev, first, second, follow), spread)
-    convolve(spread, weight, acc)
+def transpose_kernel(prev, follow, acc, weight, g0, g1, spread, total):
+    outer_taps(prev, follow, weight, acc, total, spread)
     for f, out in ((0, g0), (1, g1)):
-        out[...] = acc[f].astype(BF16)
+        out[...] = total[f].astype(BF16)
 
 
 def conv_scratch():
     return dict(
-        spread=pltpu.VMEM((4, ROWS, COLS, 3 * CH), BF16),
+        spread=pltpu.VMEM((2, ROWS, COLS, 3 * CH), BF16),
         acc=pltpu.VMEM((2, ROWS, COLS, CH), F32),
     )
 
@@ -188,32 +207,44 @@
 CONV_FLOPS = 2 * 1024 * 27 * CH * CH
 
 
-def forward(frames, w9, bias, head):
-    s = conv_scratch()
+def inner(first, second, w9, name):
+    return pl.pallas_call(
+        inner_kernel,
+        out_shape=jax.ShapeDtypeStruct((2, ROWS, COLS, CH), F32),
+        in_specs=[VMEM] * 3,
+        out_specs=VMEM,
+        scratch_shapes=[conv_scratch()["spread"]],
+        compiler_params=params(),
+        cost_estimate=cost(CONV_FLOPS * 2 / 3, 6 << 20),
+        name=name,
+    )(first, second, w9)
+
+
+def forward(prev, follow, acc, w9, bias, head):
     return pl.pallas_call(
         forward_kernel,
         out_shape=(jax.ShapeDtypeStruct((2, ROWS, COLS, CH), F32), FRAME, FRAME),
-        in_specs=[VMEM] * 7,
+        in_specs=[VMEM] * 6,
         out_specs=(VMEM, VMEM, VMEM),
-        scratch_shapes=[s["spread"]],
-        compiler_params=params(),
-        cost_estimate=cost(CONV_FLOPS, 6 << 20),
+        scratch_shapes=[conv_scratch()["spread"]],
+        compiler_params=params(),
+        cost_estimate=cost(CONV_FLOPS / 3, 6 << 20),
         name="forward",
-    )(*frames, w9, bias, head)
-
-
-def transposed(frames, w9):
+    )(prev, follow, acc, w9, bias, head)
+
+
+def transposed(prev, follow, acc, w9):
     s = conv_scratch()
     return pl.pallas_call(
         transpose_kernel,
         out_shape=(FRAME, FRAME),
-        in_specs=[VMEM] * 5,
+        in_specs=[VMEM] * 4,
         out_specs=(VMEM, VMEM),
         scratch_shapes=[s["spread"], s["acc"]],
         compiler_params=params(),
-        cost_estimate=cost(CONV_FLOPS, 5 << 20),
+        cost_estimate=cost(CONV_FLOPS / 3, 5 << 20),
         name="transposed",
-    )(*frames, w9)
+    )(prev, follow, acc, w9)
 
 
 def part_transposed(frames, x, turned):
@@ -233,6 +264,22 @@
         turned[2 * PART : 3 * PART, at] = right.astype(BF16)
 
 
+def turn_clips_kernel(pos, c0, c1, c2, c3, turned):
+    part_transposed((c0, c1, c2, c3), pos[0], turned)
+
+
+def turn_clips(pos, clips):
+    return pl.pallas_call(
+        turn_clips_kernel,
+        out_shape=jax.ShapeDtypeStruct((3 * PART, 4 * ROWS * COLS), BF16),
+        in_specs=[SMEM] + [VMEM] * 4,
+        out_specs=VMEM,
+        compiler_params=params(),
+        cost_estimate=cost(1e9, 2 << 20),
+        name="turn_clips",
+    )(pos, *clips)
+
+
 def correlate(turned, grads, b):
     width = ROWS * COLS
     rows = ROWS if b == 1 else ROWS - 1
@@ -251,16 +298,14 @@
 
 
 def backward_kernel(
-    pos, i0, i1, i2, i3, c0, c1, c2, c3, s0, s1, pre, weight, head, sent, kept,
-    spread, acc, turn_i, turn_c, pgb, total,
+    pos, i0, i1, i2, i3, inside, turn_c, s0, s1, pre, weight, head, sent, kept,
+    spread, acc, turn_i, pgb, total,
 ):
     x = pos[0]
     core = pos[1]
     grads = (i0, i1, i2, i3)
-    spread_columns(grads, spread)
     part_transposed(grads, x, turn_i)
-    part_transposed((c0, c1, c2, c3), x, turn_c)
-    convolve(spread, weight, acc)
+    outer_taps(i0, i3, weight, inside, acc, spread)
     sum_bias = jnp.zeros((8, CH), F32)
     sum_head = jnp.zeros((8, CH), F32)
     for f in range(2):
@@ -307,58 +352,83 @@
         store(sent, 0)
 
 
-def backward(pos, grads, clips, score, pre, w9, head):
+def backward(pos, grads, inside, turn_c, score, pre, w9, head):
     s = conv_scratch()
     return pl.pallas_call(
         backward_kernel,
         out_shape=(jax.ShapeDtypeStruct((PIECE * PIECES, 8, 128), F32),) * 2,
-        in_specs=[SMEM] + [VMEM] * 13,
+        in_specs=[SMEM] + [VMEM] * 11,
         out_specs=(VMEM, VMEM),
         scratch_shapes=[
             s["spread"],
             s["acc"],
             pltpu.VMEM((3 * PART, 4 * ROWS * COLS), BF16),
-            pltpu.VMEM((3 * PART, 4 * ROWS * COLS), BF16),
             pltpu.VMEM((2, ROWS, COLS, CH), BF16),
             pltpu.VMEM((27 * PART, CH), F32),
         ],
         compiler_params=params(),
         cost_estimate=cost(CONV_FLOPS * 1.6, 10 << 20),
         name="backward",
-    )(pos, *grads, *clips, *score, pre, w9, head)
+    )(pos, *grads, inside, turn_c, *score, pre, w9, head)
 
 
 def relative(distance):
     return jnp.where(distance == 0, 0, jnp.where(distance == 3, 1, distance + 1))
 
 
-def encode_kernel(terms, out):
-    value = terms[0]
-    for n in range(1, 8):
-        value = value + terms[n]
+def encode(value):
     most = jnp.max(jnp.abs(value), axis=1, keepdims=True)
-    scale = (most * 1.004).astype(BF16)
-    wide = scale.astype(F32)
+    wide = (most * 1.004).astype(BF16).astype(F32)
     inverse = jnp.where(wide > 1e-37, 1.0 / jnp.maximum(wide, 1e-37), 0.0)
     code = jnp.exp2(jnp.abs(value) * inverse * SPAN - SPAN / 2)
     code = jnp.where(value < 0, -code, code).reshape(PIECE * 8, 128)
-    pad = jnp.zeros((1, 128), F32)
-    tail = jnp.concatenate([wide.reshape(PIECE, 128), pad], axis=0)
-    line = jnp.concatenate([code, tail], axis=0).astype(BF16)
+    tail = jnp.concatenate([wide.reshape(PIECE, 128), jnp.zeros((1, 128), F32)], axis=0)
+    return jnp.concatenate([code, tail], axis=0).astype(BF16)
+
+
+def encode_terms_kernel(kept, received, out):
+    def step(n, _):
+        at = pl.ds(n * PIECE, PIECE)
+        out[n] = encode(kept[at] + received[at])
+        return 0
+
+    lax.fori_loop(0, PIECES, step, 0, unroll=4)
+
+
+def encode_terms(kept, received):
+    return pl.pallas_call(
+        encode_terms_kernel,
+        out_shape=jax.ShapeDtypeStruct((PIECES, CODED, 128), BF16),
+        in_specs=[VMEM, VMEM],
+        out_specs=VMEM,
+        compiler_params=params(4 << 20),
+        cost_estimate=cost(1e6, 3 << 20),
+        name="encode_terms",
+    )(kept, received)
+
+
+def recode_kernel(pieces, out):
+    def step(n, total):
+        more = decode(pieces[n])
+        return tuple(t + m for t, m in zip(total, more))
+
+    zero = tuple(jnp.zeros((8, 128), F32) for _ in range(PIECE))
+    total = lax.fori_loop(0, PIECES, step, zero, unroll=4)
+    line = encode(jnp.stack(total))
     for n in range(8):
         out[n] = line
 
 
-def encode(terms):
-    return pl.pallas_call(
-        encode_kernel,
+def recode(pieces):
+    return pl.pallas_call(
+        recode_kernel,
         out_shape=jax.ShapeDtypeStruct((8, CODED, 128), BF16),
         in_specs=[VMEM],
         out_specs=VMEM,
         compiler_params=params(4 << 20),
         cost_estimate=cost(1e6, 1 << 19),
-        name="encode",
-    )(terms)
+        name="recode",
+    )(pieces)
 
 
 def decode(line):
@@ -380,7 +450,7 @@
             at_y = relative(lax.rem(row - y + 4, 4))
             place = jnp.where(held == 0, at_x * 4 + at_y, at_y * 4 + at_x)
             for z in range(8):
-                piece = row * 8 + z
+                piece = ((row // 2) * 8 + z) * 2 + row % 2
                 for j, value in enumerate(decode(ref[place, z])):
                     tile = piece * PIECE + j
                     if tile < TILES:
@@ -432,18 +502,18 @@
     turned = turned.reshape(3, 3, 3 * CH, CH)
     w9 = weight.reshape(3, 3, 3 * CH, CH)
 
-    def with_halo(first, second):
-        return (chain(second, 1), first, second, chain(first, -1))
-
-    clip_frames = with_halo(*gather_rows(pos, own, below, above, across))
-    pre, s0, s1 = forward(clip_frames, w9, bias, head)
-    grad_frames = with_halo(*transposed(with_halo(s0, s1), turned))
-    sent, kept = backward(pos, grad_frames, clip_frames, (s0, s1), pre, w9, head)
-    half = kept + permute(sent, swap_core)
-    lines = lax.all_to_all(half.reshape(4, 8, PIECE, 8, 128), ("yh", "yl"), 0, 0, tiled=True)
-    line = jnp.sum(lines, axis=0)
-    pieces = lax.all_to_all(line, "z", 0, 0, tiled=True)
-    line = lax.all_to_all(encode(pieces), "z", 0, 0, tiled=True)
+    c1, c2 = gather_rows(pos, own, below, above, across, bias)
+    c0, c3 = chain(c2, 1), chain(c1, -1)
+    pre, s0, s1 = forward(c0, c3, inner(c1, c2, w9, "forward_inner"), w9, bias, head)
+    before, after = chain(s1, 1), chain(s0, -1)
+    i1, i2 = transposed(before, after, inner(s0, s1, turned, "transposed_inner"), turned)
+    turn_c = turn_clips(pos, (c0, c1, c2, c3))
+    i0, i3 = chain(i2, 1), chain(i1, -1)
+    inside = inner(i1, i2, w9, "backward_inner")
+    sent, kept = backward(pos, (i0, i1, i2, i3), inside, turn_c, (s0, s1), pre, w9, head)
+    coded = encode_terms(kept, permute(sent, swap_core))
+    pieces = lax.all_to_all(coded, PLANE, 0, 0, tiled=True)
+    line = lax.all_to_all(recode(pieces), "z", 0, 0, tiled=True)
     block = ring_gather(line, split_first)
     mine = ring_gather(block.reshape(32, CODED, 128), split_second)
     mine = mine.reshape(16, 8, CODED, 128)

time: 162 us -> 149 us (0.920)
  waiting for transfers between devices: 46.6 us -> 34.7 us
  blocking collectives: 48.4 us -> 43 us
  local copies, waits for them, and re-layouts: 4.87 us -> 8.67 us
    pallas_call x1 -> x6, Pallas kernels: 0.05 us -> 9.06 us  [the longest x3 6.73 us: inner(): pl.pallas_call(inner_kernel, out_shape=jax.ShapeDtypeStruct((2, ROWS, COL...]
    ppermute x13, waiting for transfers between devices: 33.1 us -> 26.2 us  [permute(): return lax.ppermute(value, ALL, moved(fn))]
    all_to_all x3 -> x2, blocking collectives: 48.4 us -> 43 us  [the longest x1 32 us: per_device(): pieces = lax.all_to_all(coded, PLANE, 0, 0, tiled=True)]
    ppermute x6, waiting for transfers between devices: 13.5 us -> 8.45 us  [chain(): return lax.ppermute(value, CHAIN, pairs)]
    pallas_call x1, Pallas kernels: 8.92 us -> 4.31 us  [backward(): pl.pallas_call(backward_kernel, out_shape=(jax.ShapeDtypeStruct((PIECE *...]
    unnamed x8 -> x14, local copies, waits for them, and re-layouts: 4.26 us -> 8.05 us
    pallas_call x1, Pallas kernels: 3.21 us -> 1.19 us  [transposed(): pl.pallas_call(transpose_kernel, out_shape=(FRAME, FRAME), in_specs=[VMEM...]
    pallas_call x1, Pallas kernels: 3.38 us -> 1.36 us  [forward(): pl.pallas_call(forward_kernel, out_shape=(jax.ShapeDtypeStruct((2, ROWS,...]
  transfers between devices with their start and end apart: 19 -> 19, of which waited for: 17 -> 12; matrix products, arithmetic and copies ran while one was open for 0% -> 0% of each run, Pallas kernels for 1% -> 6%
where the time goes in v4:
time: 149 us
  blocking collectives  43 us (29%)
  starting transfers between devices  37.7 us (25%)
  waiting for transfers between devices  34.7 us (23%)
  Pallas kernels  23.5 us (16%)
  local copies, waits for them, and re-layouts  8.67 us (6%)
    all_to_all x1, blocking collectives, per_device(): pieces = lax.all_to_all(coded, PLANE, 0, 0, tiled=True)  32 us
    ppermute x13, waiting for transfers between devices, permute(): return lax.ppermute(value, ALL, moved(fn))  26.2 us
    ppermute x13, starting transfers between devices, permute(): return lax.ppermute(value, ALL, moved(fn))  22.3 us
    ppermute x6, starting transfers between devices, chain(): return lax.ppermute(value, CHAIN, pairs)  15.5 us
    all_to_all x1, blocking collectives, per_device(): line = lax.all_to_all(recode(pieces), 'z', 0, 0, tiled=True)  11 us
    ppermute x6, waiting for transfers between devices, chain(): return lax.ppermute(value, CHAIN, pairs)  8.45 us
    unnamed x14, local copies, waits for them, and re-layouts  8.05 us
    pallas_call x3, Pallas kernels, inner(): pl.pallas_call(inner_kernel, out_shape=jax.ShapeDtypeStruct((2, ROWS, COL...  6.73 us
  transfers between devices with their start and end apart: 19, of which 12 were waited for; matrix products, arithmetic and copies ran while one was open for 0% of the time, Pallas kernels for 6%

profile of v4, /device:TPU:1, one launch (start us, length us, event | category | flops | bytes accessed | tf_op | source)
XLA Modules:
  0.0 148.9 jit_solution(5388458802480070161)
XLA Ops:
  0.6 3.6 %collective-permute-start.2 = (bf16[2,128,256]{2,1,0:T(8,128)(2,1)}, bf16[2,128,256]{2,1,0:T(8,128)(2,1)}, u32[]{:S(2)}, u32[]{:S(2)}) collective-permute-start(bf16[2,128,256]{2,1,0:T(8,128)(2,1)} %bitcast.31), channel_id=1, source_target_pairs={{0,2},{1,3},{2,0},{3,1},{4,6},{5,7},{6,4},{7,5},{8,10},{9,11},{10,... | collective-permute-start | bytes 393224 | tf_op jit(solution)/shard_map/ppermute | solution.py:43
  4.3 0.9 collective-permute-start.1
  5.1 0.6 collective-permute-start
  5.7 2.0 %copy-done.4 = bf16[3,3,3,256,256]{4,3,2,1,0:T(8,128)(2,1)S(1)} copy-done((bf16[3,3,3,256,256]{4,3,2,1,0:T(8,128)(2,1)S(1)}, bf16[3,3,3,256,256]{4,3,2,1,0:T(8,128)(2,1)}, u32[]{:S(2)}) %copy-start.4) | copy-done | bytes 3538968
  7.8 0.7 copy-done.5
  8.4 0.7 copy-done.6
  9.1 1.7 %turn_weights.1 = (bf16[3,3,3,256,256]{4,3,2,1,0:T(8,128)(2,1)S(1)}, bf16[3,3,3,256,256]{4,3,2,1,0:T(8,128)(2,1)S(1)}, f32[1,256]{1,0:T(1,128)S(1)}, f32[1,256]{1,0:T(1,128)S(1)}) custom-call(bf16[3,3,3,256,256]{4,3,2,1,0:T(8,128)(2,1)S(1)} %copy-done.4, f32[1,256]{1,0:T(1,128)S(1)} %bitcast.35, f32[1,256]{1,0:T(1,128)S(1)} %bitcast.36), custom_call_target="tpu_custom_call" | custom-call | flops 2000000000 | bytes 11534336 | tf_op jit(solution)/shard_map/turn_weights/pallas_call | solution.py:189
  10.8 0.0 copy-start
  10.8 1.8 %copy-done = bf16[3,3,3,256,256]{4,3,2,1,0:T(8,128)(2,1)} copy-done((bf16[3,3,3,256,256]{4,3,2,1,0:T(8,128)(2,1)}, bf16[3,3,3,256,256]{4,3,2,1,0:T(8,128)(2,1)S(1)}, u32[]{:S(2)}) %copy-start) | copy-done | bytes 3538968
  12.6 0.1 pad_add_fusion.pos_ref.pos
  12.6 0.0 collective-permute-done.2.across
  12.7 0.0 collective-permute-done.1.above
  12.7 0.2 collective-permute-done.below
  12.8 0.9 copy-done.3
  13.7 1.1 gather_rows.1
  14.8 4.4 %collective-permute-start.3 = (bf16[4,128,256]{2,1,0:T(8,128)(2,1)S(1)}, bf16[4,128,256]{2,1,0:T(8,128)(2,1)S(1)}, u32[]{:S(2)}, u32[]{:S(2)}) collective-permute-start(bf16[4,128,256]{2,1,0:T(8,128)(2,1)S(1)} %get-tuple-element.19.second.c2), channel_id=1, source_target_pairs={{0,4},{4,8},{8,12},{12,16},{16,20},{20,24},{24,28},{28,32},{32,36}... | collective-permute-start | bytes 786440 | tf_op jit(solution)/shard_map/ppermute | solution.py:65
  19.3 1.9 %collective-permute-start.4 = (bf16[4,128,256]{2,1,0:T(8,128)(2,1)S(1)}, bf16[4,128,256]{2,1,0:T(8,128)(2,1)S(1)}, u32[]{:S(2)}, u32[]{:S(2)}) collective-permute-start(bf16[4,128,256]{2,1,0:T(8,128)(2,1)S(1)} %get-tuple-element.20.first.c1), channel_id=1, source_target_pairs={{4,0},{8,4},{12,8},{16,12},{20,16},{24,20},{28,24},{32,28},{36,32}... | collective-permute-start | bytes 786440 | tf_op jit(solution)/shard_map/ppermute | solution.py:65
  21.2 0.0 copy-start.1
  21.2 2.0 %copy-done.1 = bf16[3,3,3,256,256]{4,3,2,1,0:T(8,128)(2,1)S(1)} copy-done((bf16[3,3,3,256,256]{4,3,2,1,0:T(8,128)(2,1)S(1)}, bf16[3,3,3,256,256]{4,3,2,1,0:T(8,128)(2,1)}, u32[]{:S(2)}) %copy-start.1) | copy-done | bytes 3538968
  23.2 2.3 %forward_inner.1.acc = f32[2,4,128,256]{3,2,1,0:T(8,128)S(1)} custom-call(bf16[4,128,256]{2,1,0:T(8,128)(2,1)S(1)} %get-tuple-element.20.first.c1, bf16[4,128,256]{2,1,0:T(8,128)(2,1)S(1)} %get-tuple-element.19.second.c2, bf16[3,3,768,256]{3,2,1,0:T(8,128)(2,1)S(1)} %bitcast.27), custom_call_target="tpu_custom_call" | custom-call | flops 2415919104 | bytes 6291456 | tf_op jit(solution)/shard_map/forward_inner/pallas_call | solution.py:211
  25.5 0.0 collective-permute-done.3.prev.c0
  25.5 1.5 collective-permute-done.4.follow.c3
  27.0 1.4 forward.1
  28.3 2.2 %collective-permute-start.5 = (bf16[4,128,256]{2,1,0:T(8,128)(2,1)S(1)}, bf16[4,128,256]{2,1,0:T(8,128)(2,1)S(1)}, u32[]{:S(2)}, u32[]{:S(2)}) collective-permute-start(bf16[4,128,256]{2,1,0:T(8,128)(2,1)S(1)} %get-tuple-element.23.second.s1), channel_id=1, source_target_pairs={{0,4},{4,8},{8,12},{12,16},{16,20},{20,24},{24,28},{28,32},{32,36}... | collective-permute-start | bytes 786440 | tf_op jit(solution)/shard_map/ppermute | solution.py:65
  30.5 2.2 %collective-permute-start.6 = (bf16[4,128,256]{2,1,0:T(8,128)(2,1)S(1)}, bf16[4,128,256]{2,1,0:T(8,128)(2,1)S(1)}, u32[]{:S(2)}, u32[]{:S(2)}) collective-permute-start(bf16[4,128,256]{2,1,0:T(8,128)(2,1)S(1)} %get-tuple-element.24.first.s0), channel_id=1, source_target_pairs={{4,0},{8,4},{12,8},{16,12},{20,16},{24,20},{28,24},{32,28},{36,32}... | collective-permute-start | bytes 786440 | tf_op jit(solution)/shard_map/ppermute | solution.py:65
  32.7 2.2 %transposed_inner.1.acc = f32[2,4,128,256]{3,2,1,0:T(8,128)S(1)} custom-call(bf16[4,128,256]{2,1,0:T(8,128)(2,1)S(1)} %get-tuple-element.24.first.s0, bf16[4,128,256]{2,1,0:T(8,128)(2,1)S(1)} %get-tuple-element.23.second.s1, bf16[3,3,768,256]{3,2,1,0:T(8,128)(2,1)S(1)} %bitcast.25), custom_call_target="tpu_custom_call" | custom-call | flops 2415919104 | bytes 6291456 | tf_op jit(solution)/shard_map/transposed_inner/pallas_call | solution.py:211
  34.9 0.0 collective-permute-done.5.prev
  34.9 4.1 %collective-permute-done.6.follow = bf16[4,128,256]{2,1,0:T(8,128)(2,1)S(1)} collective-permute-done((bf16[4,128,256]{2,1,0:T(8,128)(2,1)S(1)}, bf16[4,128,256]{2,1,0:T(8,128)(2,1)S(1)}, u32[]{:S(2)}, u32[]{:S(2)}) %collective-permute-start.6) | collective-permute-done | bytes 262176 | tf_op jit(solution)/shard_map/ppermute | solution.py:65
  39.0 1.2 transposed.1
  40.2 0.0 copy-start.2
  40.2 2.2 %collective-permute-start.7 = (bf16[4,128,256]{2,1,0:T(8,128)(2,1)S(1)}, bf16[4,128,256]{2,1,0:T(8,128)(2,1)S(1)}, u32[]{:S(2)}, u32[]{:S(2)}) collective-permute-start(bf16[4,128,256]{2,1,0:T(8,128)(2,1)S(1)} %get-tuple-element.26.second.i2), channel_id=1, source_target_pairs={{0,4},{4,8},{8,12},{12,16},{16,20},{20,24},{24,28},{28,32},{32,36}... | collective-permute-start | bytes 786440 | tf_op jit(solution)/shard_map/ppermute | solution.py:65
  42.4 2.6 %collective-permute-start.8 = (bf16[4,128,256]{2,1,0:T(8,128)(2,1)S(1)}, bf16[4,128,256]{2,1,0:T(8,128)(2,1)S(1)}, u32[]{:S(2)}, u32[]{:S(2)}) collective-permute-start(bf16[4,128,256]{2,1,0:T(8,128)(2,1)S(1)} %get-tuple-element.27.first.i1), channel_id=1, source_target_pairs={{4,0},{8,4},{12,8},{16,12},{20,16},{24,20},{28,24},{32,28},{36,32}... | collective-permute-start | bytes 786440 | tf_op jit(solution)/shard_map/ppermute | solution.py:65
  45.0 1.1 turn_clips.1.turn_c
  46.1 2.3 %backward_inner.1.inside = f32[2,4,128,256]{3,2,1,0:T(8,128)S(1)} custom-call(bf16[4,128,256]{2,1,0:T(8,128)(2,1)S(1)} %get-tuple-element.27.first.i1, bf16[4,128,256]{2,1,0:T(8,128)(2,1)S(1)} %get-tuple-element.26.second.i2, bf16[3,3,768,256]{3,2,1,0:T(8,128)(2,1)S(1)} %bitcast.29), custom_call_target="tpu_custom_call" | custom-call | flops 2415919104 | bytes 6291456 | tf_op jit(solution)/shard_map/backward_inner/pallas_call | solution.py:211
  48.4 0.0 collective-permute-done.7.i0
  48.4 2.8 %collective-permute-done.8.i3 = bf16[4,128,256]{2,1,0:T(8,128)(2,1)S(1)} collective-permute-done((bf16[4,128,256]{2,1,0:T(8,128)(2,1)S(1)}, bf16[4,128,256]{2,1,0:T(8,128)(2,1)S(1)}, u32[]{:S(2)}, u32[]{:S(2)}) %collective-permute-start.8) | collective-permute-done | bytes 262176 | tf_op jit(solution)/shard_map/ppermute | solution.py:65
  51.2 4.3 %backward.1 = (f32[224,8,128]{2,1,0:T(8,128)S(1)}, f32[224,8,128]{2,1,0:T(8,128)S(1)}) custom-call(s32[3]{0:T(128)S(1)} %pad_add_fusion.pos_ref.pos, bf16[4,128,256]{2,1,0:T(8,128)(2,1)S(1)} %collective-permute-done.7.i0, bf16[4,128,256]{2,1,0:T(8,128)(2,1)S(1)} %get-tuple-element.27.first.i1, bf16[4,128,256]{2,1,0:T(8,128)(2,1)S(1)} %get-tuple-element.26.second.i2, ...), custom_call_target="tpu_custom_call" | custom-call | flops 5798205952 | bytes 10485760 | tf_op jit(solution)/shard_map/backward/pallas_call | solution.py:357
  55.6 0.1 collective-permute-start.9
  55.7 2.5 %collective-permute-done.9.received = f32[224,8,128]{2,1,0:T(8,128)S(1)} collective-permute-done((f32[224,8,128]{2,1,0:T(8,128)S(1)}, f32[224,8,128]{2,1,0:T(8,128)S(1)}, u32[]{:S(2)}, u32[]{:S(2)}) %collective-permute-start.9) | collective-permute-done | bytes 917536 | tf_op jit(solution)/shard_map/ppermute | solution.py:43
  58.1 0.9 encode_terms.1
  59.0 32.0 %all_to_all.10.pieces = bf16[32,64,128]{2,1,0:T(8,128)(2,1)S(1)} all-to-all(bf16[32,64,128]{2,1,0:T(8,128)(2,1)S(1)} %encode_terms.1), channel_id=1, replica_groups=mesh['yh'=2,'z'=8,'yl'=2,'c'=2,'x'=4] {'yh','z','yl'}, dimensions={0} | all-to-all | bytes 1048576 | tf_op jit(solution)/shard_map/all_to_all | solution.py:515
  91.0 0.4 recode.1
  91.4 11.0 %all_to_all.11 = bf16[8,64,128]{2,1,0:T(8,128)(2,1)S(1)} all-to-all(bf16[8,64,128]{2,1,0:T(8,128)(2,1)S(1)} %recode.1), channel_id=1, replica_groups=mesh['yh'=2,'z'=8,'yl'=2,'c'=2,'x'=4] {'z'}, dimensions={0} | all-to-all | bytes 262144 | tf_op jit(solution)/shard_map/all_to_all | solution.py:516
  102.4 2.1 %collective-permute-start.11 = (bf16[8,64,128]{2,1,0:T(8,128)(2,1)S(1)}, bf16[8,64,128]{2,1,0:T(8,128)(2,1)S(1)}, u32[]{:S(2)}, u32[]{:S(2)}) collective-permute-start(bf16[8,64,128]{2,1,0:T(8,128)(2,1)S(1)} %all_to_all.11), channel_id=1, source_target_pairs={{0,136},{1,137},{2,138},{3,139},{4,7},{5,4},{6,5},{7,6},{8,0},{9,1... | collective-permute-start | bytes 393224 | tf_op jit(solution)/shard_map/ppermute | solution.py:43
  104.4 0.0 collective-permute-start.10
  104.4 1.9 %collective-permute-done.11 = bf16[8,64,128]{2,1,0:T(8,128)(2,1)S(1)} collective-permute-done((bf16[8,64,128]{2,1,0:T(8,128)(2,1)S(1)}, bf16[8,64,128]{2,1,0:T(8,128)(2,1)S(1)}, u32[]{:S(2)}, u32[]{:S(2)}) %collective-permute-start.11) | collective-permute-done | bytes 131104 | tf_op jit(solution)/shard_map/ppermute | solution.py:43
  106.4 3.1 %collective-permute-start.13 = (bf16[4,64,128]{2,1,0:T(8,128)(2,1)S(1)}, bf16[4,64,128]{2,1,0:T(8,128)(2,1)S(1)}, u32[]{:S(2)}, u32[]{:S(2)}) collective-permute-start(bf16[4,64,128]{2,1,0:T(8,128)(2,1)S(1)} %slice.25), channel_id=1, source_target_pairs={{0,136},{1,137},{2,138},{3,139},{4,7},{5,4},{6,5},{7,6},{8,0},{9,1... | collective-permute-start | bytes 196616 | tf_op jit(solution)/shard_map/ppermute | solution.py:43
  109.5 0.1 collective-permute-start.12
  109.6 1.2 collective-permute-done.13
  110.8 3.1 %collective-permute-done.12 = bf16[4,64,128]{2,1,0:T(8,128)(2,1)S(1)} collective-permute-done((bf16[4,64,128]{2,1,0:T(8,128)(2,1)S(1)}, bf16[4,64,128]{2,1,0:T(8,128)(2,1)S(1)}, u32[]{:S(2)}, u32[]{:S(2)}) %collective-permute-start.12) | collective-permute-done | bytes 65568 | tf_op jit(solution)/shard_map/ppermute | solution.py:43
  113.9 0.1 pad_maximum_fusion.1
  114.0 0.6 collective-permute-start.15
  114.6 0.9 collective-permute-start.14
  115.5 6.9 %collective-permute-done.15 = bf16[32,64,128]{2,1,0:T(8,128)(2,1)S(1)} collective-permute-done((bf16[32,64,128]{2,1,0:T(8,128)(2,1)S(1)}, bf16[32,64,128]{2,1,0:T(8,128)(2,1)S(1)}, u32[]{:S(2)}, u32[]{:S(2)}) %collective-permute-start.15) | collective-permute-done | bytes 524320 | tf_op jit(solution)/shard_map/ppermute | solution.py:43
  122.4 1.5 %collective-permute-start.17 = (bf16[16,64,128]{2,1,0:T(8,128)(2,1)S(1)}, bf16[16,64,128]{2,1,0:T(8,128)(2,1)S(1)}, u32[]{:S(2)}, u32[]{:S(2)}) collective-permute-start(bf16[16,64,128]{2,1,0:T(8,128)(2,1)S(1)} %slice.27), channel_id=1, source_target_pairs={{0,3},{1,0},{2,1},{3,2},{4,140},{5,141},{6,142},{7,143},{8,11},{9,... | collective-permute-start | bytes 786440 | tf_op jit(solution)/shard_map/ppermute | solution.py:43
  123.9 0.0 collective-permute-done.14
  124.0 0.1 collective-permute-start.16
  124.1 3.9 %collective-permute-done.17 = bf16[16,64,128]{2,1,0:T(8,128)(2,1)S(1)} collective-permute-done((bf16[16,64,128]{2,1,0:T(8,128)(2,1)S(1)}, bf16[16,64,128]{2,1,0:T(8,128)(2,1)S(1)}, u32[]{:S(2)}, u32[]{:S(2)}) %collective-permute-start.17) | collective-permute-done | bytes 262176 | tf_op jit(solution)/shard_map/ppermute | solution.py:43
  128.0 2.8 %collective-permute-done.16 = bf16[16,64,128]{2,1,0:T(8,128)(2,1)S(1)} collective-permute-done((bf16[16,64,128]{2,1,0:T(8,128)(2,1)S(1)}, bf16[16,64,128]{2,1,0:T(8,128)(2,1)S(1)}, u32[]{:S(2)}, u32[]{:S(2)}) %collective-permute-start.16) | collective-permute-done | bytes 262176 | tf_op jit(solution)/shard_map/ppermute | solution.py:43
  130.8 0.3 pad_maximum_fusion
  131.1 8.7 %collective-permute-start.18 = (bf16[16,8,64,128]{3,2,1,0:T(8,128)(2,1)S(1)}, bf16[16,8,64,128]{3,2,1,0:T(8,128)(2,1)S(1)}, u32[]{:S(2)}, u32[]{:S(2)}) collective-permute-start(bf16[16,8,64,128]{3,2,1,0:T(8,128)(2,1)S(1)} %bitcast.23), channel_id=1, source_target_pairs={{0,4},{1,5},{2,6},{3,7},{4,0},{5,1},{6,2},{7,3},{8,12},{9,13},{10,... | collective-permute-start | bytes 6291464 | tf_op jit(solution)/shard_map/ppermute | solution.py:43
  139.7 3.8 %collective-permute-done.18.other = bf16[16,8,64,128]{3,2,1,0:T(8,128)(2,1)S(1)} collective-permute-done((bf16[16,8,64,128]{3,2,1,0:T(8,128)(2,1)S(1)}, bf16[16,8,64,128]{3,2,1,0:T(8,128)(2,1)S(1)}, u32[]{:S(2)}, u32[]{:S(2)}) %collective-permute-start.18) | collective-permute-done | bytes 2097184 | tf_op jit(solution)/shard_map/ppermute | solution.py:43
  143.5 4.8 %assemble.1 = (f32[27,4,8,8,256]{4,3,2,1,0:T(8,128)}, f32[16,256]{1,0:T(8,128)S(1)}) custom-call(s32[3]{0:T(128)S(1)} %pad_add_fusion.pos_ref.pos, bf16[16,8,64,128]{3,2,1,0:T(8,128)(2,1)S(1)} %bitcast.24, bf16[16,8,64,128]{3,2,1,0:T(8,128)(2,1)S(1)} %collective-permute-done.18.other), custom_call_target="tpu_custom_call" | custom-call | flops 1000000 | bytes 15728640 | tf_op jit(solution)/shard_map/assemble/pallas_call | solution.py:464
  148.4 0.6 fusion
  (12 shorter events, 0.1 us)
Async XLA Ops:
  0.6 12.0 %collective-permute-start.2 = (bf16[2,128,256]{2,1,0:T(8,128)(2,1)}, bf16[2,128,256]{2,1,0:T(8,128)(2,1)}, u32[]{:S(2)}, u32[]{:S(2)}) collective-permute-start(bf16[2,128,256]{2,1,0:T(8,128)(2,1)} %bitcast.31), channel_id=1, source_target_pairs={{0,2},{1,3},{2,0},{3,1},{4,6},{5,7},{6,4},{7,5},{8,10},{9,11},{10,... | collective-permute-start | bytes 393224 | tf_op jit(solution)/shard_map/ppermute | solution.py:43
  4.3 8.4 %collective-permute-start.1 = (bf16[2,128,256]{2,1,0:T(8,128)(2,1)}, bf16[2,128,256]{2,1,0:T(8,128)(2,1)}, u32[]{:S(2)}, u32[]{:S(2)}) collective-permute-start(bf16[2,128,256]{2,1,0:T(8,128)(2,1)} %bitcast.32), channel_id=1, source_target_pairs={{0,3},{1,0},{2,1},{3,2},{4,7},{5,4},{6,5},{7,6},{8,11},{9,8},{10,9... | collective-permute-start | bytes 393224 | tf_op jit(solution)/shard_map/ppermute | solution.py:43
  5.1 7.7 %collective-permute-start = (bf16[2,128,256]{2,1,0:T(8,128)(2,1)}, bf16[2,128,256]{2,1,0:T(8,128)(2,1)}, u32[]{:S(2)}, u32[]{:S(2)}) collective-permute-start(bf16[2,128,256]{2,1,0:T(8,128)(2,1)} %bitcast.33), channel_id=1, source_target_pairs={{0,1},{1,2},{2,3},{3,0},{4,5},{5,6},{6,7},{7,4},{8,9},{9,10},{10,1... | collective-permute-start | bytes 393224 | tf_op jit(solution)/shard_map/ppermute | solution.py:43
  5.7 2.0 %copy-start.4 = (bf16[3,3,3,256,256]{4,3,2,1,0:T(8,128)(2,1)S(1)}, bf16[3,3,3,256,256]{4,3,2,1,0:T(8,128)(2,1)}, u32[]{:S(2)}) copy-start(bf16[3,3,3,256,256]{4,3,2,1,0:T(8,128)(2,1)} %weight.1) | copy-start | bytes 10616836
  7.7 0.7 copy-start.5
  8.4 0.7 copy-start.6
  10.8 1.8 %copy-start = (bf16[3,3,3,256,256]{4,3,2,1,0:T(8,128)(2,1)}, bf16[3,3,3,256,256]{4,3,2,1,0:T(8,128)(2,1)S(1)}, u32[]{:S(2)}) copy-start(bf16[3,3,3,256,256]{4,3,2,1,0:T(8,128)(2,1)S(1)} %get-tuple-element.21) | copy-start | bytes 10616836
  12.8 0.9 copy-start.3
  14.8 10.6 %collective-permute-start.3 = (bf16[4,128,256]{2,1,0:T(8,128)(2,1)S(1)}, bf16[4,128,256]{2,1,0:T(8,128)(2,1)S(1)}, u32[]{:S(2)}, u32[]{:S(2)}) collective-permute-start(bf16[4,128,256]{2,1,0:T(8,128)(2,1)S(1)} %get-tuple-element.19.second.c2), channel_id=1, source_target_pairs={{0,4},{4,8},{8,12},{12,16},{16,20},{20,24},{24,28},{28,32},{32,36}... | collective-permute-start | bytes 786440 | tf_op jit(solution)/shard_map/ppermute | solution.py:65
  19.3 7.7 %collective-permute-start.4 = (bf16[4,128,256]{2,1,0:T(8,128)(2,1)S(1)}, bf16[4,128,256]{2,1,0:T(8,128)(2,1)S(1)}, u32[]{:S(2)}, u32[]{:S(2)}) collective-permute-start(bf16[4,128,256]{2,1,0:T(8,128)(2,1)S(1)} %get-tuple-element.20.first.c1), channel_id=1, source_target_pairs={{4,0},{8,4},{12,8},{16,12},{20,16},{24,20},{28,24},{32,28},{36,32}... | collective-permute-start | bytes 786440 | tf_op jit(solution)/shard_map/ppermute | solution.py:65
  21.2 2.0 %copy-start.1 = (bf16[3,3,3,256,256]{4,3,2,1,0:T(8,128)(2,1)S(1)}, bf16[3,3,3,256,256]{4,3,2,1,0:T(8,128)(2,1)}, u32[]{:S(2)}) copy-start(bf16[3,3,3,256,256]{4,3,2,1,0:T(8,128)(2,1)} %copy-done) | copy-start | bytes 10616836
  28.3 6.6 %collective-permute-start.5 = (bf16[4,128,256]{2,1,0:T(8,128)(2,1)S(1)}, bf16[4,128,256]{2,1,0:T(8,128)(2,1)S(1)}, u32[]{:S(2)}, u32[]{:S(2)}) collective-permute-start(bf16[4,128,256]{2,1,0:T(8,128)(2,1)S(1)} %get-tuple-element.23.second.s1), channel_id=1, source_target_pairs={{0,4},{4,8},{8,12},{12,16},{16,20},{20,24},{24,28},{28,32},{32,36}... | collective-permute-start | bytes 786440 | tf_op jit(solution)/shard_map/ppermute | solution.py:65
  30.5 8.5 %collective-permute-start.6 = (bf16[4,128,256]{2,1,0:T(8,128)(2,1)S(1)}, bf16[4,128,256]{2,1,0:T(8,128)(2,1)S(1)}, u32[]{:S(2)}, u32[]{:S(2)}) collective-permute-start(bf16[4,128,256]{2,1,0:T(8,128)(2,1)S(1)} %get-tuple-element.24.first.s0), channel_id=1, source_target_pairs={{4,0},{8,4},{12,8},{16,12},{20,16},{24,20},{28,24},{32,28},{36,32}... | collective-permute-start | bytes 786440 | tf_op jit(solution)/shard_map/ppermute | solution.py:65
  40.2 5.9 %copy-start.2 = (bf16[3,3,3,256,256]{4,3,2,1,0:T(8,128)(2,1)S(1)}, bf16[3,3,3,256,256]{4,3,2,1,0:T(8,128)(2,1)}, u32[]{:S(2)}) copy-start(bf16[3,3,3,256,256]{4,3,2,1,0:T(8,128)(2,1)} %copy-done) | copy-start | bytes 10616836
  40.2 8.2 %collective-permute-start.7 = (bf16[4,128,256]{2,1,0:T(8,128)(2,1)S(1)}, bf16[4,128,256]{2,1,0:T(8,128)(2,1)S(1)}, u32[]{:S(2)}, u32[]{:S(2)}) collective-permute-start(bf16[4,128,256]{2,1,0:T(8,128)(2,1)S(1)} %get-tuple-element.26.second.i2), channel_id=1, source_target_pairs={{0,4},{4,8},{8,12},{12,16},{16,20},{20,24},{24,28},{28,32},{32,36}... | collective-permute-start | bytes 786440 | tf_op jit(solution)/shard_map/ppermute | solution.py:65
  42.4 8.8 %collective-permute-start.8 = (bf16[4,128,256]{2,1,0:T(8,128)(2,1)S(1)}, bf16[4,128,256]{2,1,0:T(8,128)(2,1)S(1)}, u32[]{:S(2)}, u32[]{:S(2)}) collective-permute-start(bf16[4,128,256]{2,1,0:T(8,128)(2,1)S(1)} %get-tuple-element.27.first.i1), channel_id=1, source_target_pairs={{4,0},{8,4},{12,8},{16,12},{20,16},{24,20},{28,24},{32,28},{36,32}... | collective-permute-start | bytes 786440 | tf_op jit(solution)/shard_map/ppermute | solution.py:65
  55.6 2.6 %collective-permute-start.9 = (f32[224,8,128]{2,1,0:T(8,128)S(1)}, f32[224,8,128]{2,1,0:T(8,128)S(1)}, u32[]{:S(2)}, u32[]{:S(2)}) collective-permute-start(f32[224,8,128]{2,1,0:T(8,128)S(1)} %get-tuple-element.30), channel_id=1, source_target_pairs={{0,4},{1,5},{2,6},{3,7},{4,0},{5,1},{6,2},{7,3},{8,12},{9,13},{10,... | collective-permute-start | bytes 2752520 | tf_op jit(solution)/shard_map/ppermute | solution.py:43
  102.4 4.0 %collective-permute-start.11 = (bf16[8,64,128]{2,1,0:T(8,128)(2,1)S(1)}, bf16[8,64,128]{2,1,0:T(8,128)(2,1)S(1)}, u32[]{:S(2)}, u32[]{:S(2)}) collective-permute-start(bf16[8,64,128]{2,1,0:T(8,128)(2,1)S(1)} %all_to_all.11), channel_id=1, source_target_pairs={{0,136},{1,137},{2,138},{3,139},{4,7},{5,4},{6,5},{7,6},{8,0},{9,1... | collective-permute-start | bytes 393224 | tf_op jit(solution)/shard_map/ppermute | solution.py:43
  104.4 5.0 %collective-permute-start.10 = (bf16[8,64,128]{2,1,0:T(8,128)(2,1)S(1)}, bf16[8,64,128]{2,1,0:T(8,128)(2,1)S(1)}, u32[]{:S(2)}, u32[]{:S(2)}) collective-permute-start(bf16[8,64,128]{2,1,0:T(8,128)(2,1)S(1)} %all_to_all.11), channel_id=1, source_target_pairs={{0,8},{1,9},{2,10},{3,11},{4,5},{5,6},{6,7},{7,4},{8,128},{9,129},... | collective-permute-start | bytes 393224 | tf_op jit(solution)/shard_map/ppermute | solution.py:43
  106.4 4.4 %collective-permute-start.13 = (bf16[4,64,128]{2,1,0:T(8,128)(2,1)S(1)}, bf16[4,64,128]{2,1,0:T(8,128)(2,1)S(1)}, u32[]{:S(2)}, u32[]{:S(2)}) collective-permute-start(bf16[4,64,128]{2,1,0:T(8,128)(2,1)S(1)} %slice.25), channel_id=1, source_target_pairs={{0,136},{1,137},{2,138},{3,139},{4,7},{5,4},{6,5},{7,6},{8,0},{9,1... | collective-permute-start | bytes 196616 | tf_op jit(solution)/shard_map/ppermute | solution.py:43
  109.5 4.4 %collective-permute-start.12 = (bf16[4,64,128]{2,1,0:T(8,128)(2,1)S(1)}, bf16[4,64,128]{2,1,0:T(8,128)(2,1)S(1)}, u32[]{:S(2)}, u32[]{:S(2)}) collective-permute-start(bf16[4,64,128]{2,1,0:T(8,128)(2,1)S(1)} %slice.24), channel_id=1, source_target_pairs={{0,8},{1,9},{2,10},{3,11},{4,5},{5,6},{6,7},{7,4},{8,128},{9,129},... | collective-permute-start | bytes 196616 | tf_op jit(solution)/shard_map/ppermute | solution.py:43
  114.0 8.4 %collective-permute-start.15 = (bf16[32,64,128]{2,1,0:T(8,128)(2,1)S(1)}, bf16[32,64,128]{2,1,0:T(8,128)(2,1)S(1)}, u32[]{:S(2)}, u32[]{:S(2)}) collective-permute-start(bf16[32,64,128]{2,1,0:T(8,128)(2,1)S(1)} %bitcast.37), channel_id=1, source_target_pairs={{0,3},{1,0},{2,1},{3,2},{4,140},{5,141},{6,142},{7,143},{8,11},{9,... | collective-permute-start | bytes 1572872 | tf_op jit(solution)/shard_map/ppermute | solution.py:43
  114.6 9.3 %collective-permute-start.14 = (bf16[32,64,128]{2,1,0:T(8,128)(2,1)S(1)}, bf16[32,64,128]{2,1,0:T(8,128)(2,1)S(1)}, u32[]{:S(2)}, u32[]{:S(2)}) collective-permute-start(bf16[32,64,128]{2,1,0:T(8,128)(2,1)S(1)} %bitcast.38), channel_id=1, source_target_pairs={{0,1},{1,2},{2,3},{3,0},{4,12},{5,13},{6,14},{7,15},{8,9},{9,10},{... | collective-permute-start | bytes 1572872 | tf_op jit(solution)/shard_map/ppermute | solution.py:43
  122.4 5.6 %collective-permute-start.17 = (bf16[16,64,128]{2,1,0:T(8,128)(2,1)S(1)}, bf16[16,64,128]{2,1,0:T(8,128)(2,1)S(1)}, u32[]{:S(2)}, u32[]{:S(2)}) collective-permute-start(bf16[16,64,128]{2,1,0:T(8,128)(2,1)S(1)} %slice.27), channel_id=1, source_target_pairs={{0,3},{1,0},{2,1},{3,2},{4,140},{5,141},{6,142},{7,143},{8,11},{9,... | collective-permute-start | bytes 786440 | tf_op jit(solution)/shard_map/ppermute | solution.py:43
  124.0 6.8 %collective-permute-start.16 = (bf16[16,64,128]{2,1,0:T(8,128)(2,1)S(1)}, bf16[16,64,128]{2,1,0:T(8,128)(2,1)S(1)}, u32[]{:S(2)}, u32[]{:S(2)}) collective-permute-start(bf16[16,64,128]{2,1,0:T(8,128)(2,1)S(1)} %slice.26), channel_id=1, source_target_pairs={{0,1},{1,2},{2,3},{3,0},{4,12},{5,13},{6,14},{7,15},{8,9},{9,10},{... | collective-permute-start | bytes 786440 | tf_op jit(solution)/shard_map/ppermute | solution.py:43
  131.1 12.4 %collective-permute-start.18 = (bf16[16,8,64,128]{3,2,1,0:T(8,128)(2,1)S(1)}, bf16[16,8,64,128]{3,2,1,0:T(8,128)(2,1)S(1)}, u32[]{:S(2)}, u32[]{:S(2)}) collective-permute-start(bf16[16,8,64,128]{3,2,1,0:T(8,128)(2,1)S(1)} %bitcast.23), channel_id=1, source_target_pairs={{0,4},{1,5},{2,6},{3,7},{4,0},{5,1},{6,2},{7,3},{8,12},{9,13},{10,... | collective-permute-start | bytes 6291464 | tf_op jit(solution)/shard_map/ppermute | solution.py:43

commit v5 on v4

--- a/solution.py
+++ b/solution.py
@@ -59,10 +59,15 @@
     return lambda y, z, c, x: (y + step, z, c, x) if c else (y, z, c, x + step)
 
 
-def chain(value, step):
-    count = 32
-    pairs = [(i, i + step) for i in range(count) if 0 <= i + step < count]
+def trade_far(value):
+    pairs = []
+    for i in range(1, 31, 2):
+        pairs += [(i, i + 1), (i + 1, i)]
     return lax.ppermute(value, CHAIN, pairs)
+
+
+def trade(near, far):
+    return permute(near, swap_core), trade_far(far)
 
 
 VMEM = pl.BlockSpec(memory_space=pltpu.VMEM)
@@ -77,22 +82,35 @@
     return pl.CostEstimate(flops=int(flops), bytes_accessed=int(nbytes), transcendentals=0)
 
 
-def gather_rows_kernel(pos_ref, own, below, above, across, ready, first, second):
+def place_edges(core, first, second, near, far):
+    @pl.when(core == 0)
+    def _():
+        near[...] = second[...]
+        far[...] = first[...]
+
+    @pl.when(core == 1)
+    def _():
+        near[...] = first[...]
+        far[...] = second[...]
+
+
+def gather_rows_kernel(pos_ref, own, below, above, across, ready, first, second, near, far):
     del ready
     x = pos_ref[0]
     for shift, ref in ((0, own), (3, below), (1, above), (2, across)):
         row = lax.rem(x + shift, 4)
         first[row] = ref[0]
         second[row] = ref[1]
+    place_edges(pos_ref[1], first, second, near, far)
 
 
 def gather_rows(pos, own, below, above, across, ready):
     out = jax.ShapeDtypeStruct((ROWS, COLS, CH), BF16)
     return pl.pallas_call(
         gather_rows_kernel,
-        out_shape=(out, out),
+        out_shape=(out,) * 4,
         in_specs=[SMEM] + [VMEM] * 5,
-        out_specs=(VMEM, VMEM),
+        out_specs=(VMEM,) * 4,
         compiler_params=params(),
         cost_estimate=cost(1e6, 1 << 20),
         name="gather_rows",
@@ -139,17 +157,18 @@
             acc[0:1, dst : dst + rows] += apply_tap(spread, weight, a, b, 1, 1)
 
 
-def outer_taps(prev, follow, weight, acc, total, spread):
-    spread_columns((prev, follow), spread)
-    for f, a in ((0, 0), (1, 2)):
-        total[f : f + 1] = acc[f : f + 1] + apply_tap(spread, weight, a, 1, f, 1)
-        for b in (0, 2):
+def outer_taps(core, near, far, weight, acc, total, spread):
+    spread_columns((near, far), spread)
+    total[...] = acc[...]
+    for n, f in ((0, 1 - core), (1, core)):
+        at = pl.ds(f, 1)
+        for b in (1, 0, 2):
             rows, _, dst = row_range(b)
-            total[f : f + 1, dst : dst + rows] += apply_tap(spread, weight, a, b, f, 1)
-
-
-def forward_kernel(prev, follow, acc, weight, bias, head, pre, g0, g1, spread):
-    outer_taps(prev, follow, weight, acc, pre, spread)
+            total[at, dst : dst + rows] += apply_tap(spread, weight, 2 * f, b, n, 1)
+
+
+def forward_kernel(pos, near, far, acc, weight, bias, head, pre, g0, g1, near_out, far_out, spread):
+    outer_taps(pos[1], near, far, weight, acc, pre, spread)
     for f, out in ((0, g0), (1, g1)):
         for r in range(ROWS):
             value = pre[f, r] + bias[...]
@@ -157,12 +176,14 @@
             sig = jax.nn.sigmoid(value)
             slope = sig * (1.0 + value * (1.0 - sig))
             out[r] = (head[...] * slope).astype(BF16)
-
-
-def transpose_kernel(prev, follow, acc, weight, g0, g1, spread, total):
-    outer_taps(prev, follow, weight, acc, total, spread)
+    place_edges(pos[1], g0, g1, near_out, far_out)
+
+
+def transpose_kernel(pos, near, far, acc, weight, g0, g1, near_out, far_out, spread, total):
+    outer_taps(pos[1], near, far, weight, acc, total, spread)
     for f, out in ((0, g0), (1, g1)):
         out[...] = total[f].astype(BF16)
+    place_edges(pos[1], g0, g1, near_out, far_out)
 
 
 def conv_scratch():
@@ -220,52 +241,53 @@
     )(first, second, w9)
 
 
-def forward(prev, follow, acc, w9, bias, head):
+def forward(pos, near, far, acc, w9, bias, head):
     return pl.pallas_call(
         forward_kernel,
-        out_shape=(jax.ShapeDtypeStruct((2, ROWS, COLS, CH), F32), FRAME, FRAME),
-        in_specs=[VMEM] * 6,
-        out_specs=(VMEM, VMEM, VMEM),
+        out_shape=(jax.ShapeDtypeStruct((2, ROWS, COLS, CH), F32),) + (FRAME,) * 4,
+        in_specs=[SMEM] + [VMEM] * 6,
+        out_specs=(VMEM,) * 5,
         scratch_shapes=[conv_scratch()["spread"]],
         compiler_params=params(),
         cost_estimate=cost(CONV_FLOPS / 3, 6 << 20),
         name="forward",
-    )(prev, follow, acc, w9, bias, head)
-
-
-def transposed(prev, follow, acc, w9):
+    )(pos, near, far, acc, w9, bias, head)
+
+
+def transposed(pos, near, far, acc, w9):
     s = conv_scratch()
     return pl.pallas_call(
         transpose_kernel,
-        out_shape=(FRAME, FRAME),
-        in_specs=[VMEM] * 4,
-        out_specs=(VMEM, VMEM),
+        out_shape=(FRAME,) * 4,
+        in_specs=[SMEM] + [VMEM] * 4,
+        out_specs=(VMEM,) * 4,
         scratch_shapes=[s["spread"], s["acc"]],
         compiler_params=params(),
         cost_estimate=cost(CONV_FLOPS / 3, 5 << 20),
         name="transposed",
-    )(prev, follow, acc, w9)
-
-
-def part_transposed(frames, x, turned):
+    )(pos, near, far, acc, w9)
+
+
+def part_transposed(frames, pos, turned):
     chan = lax.broadcasted_iota(jnp.int32, (PART, CH), 1)
-    want = lax.broadcasted_iota(jnp.int32, (PART, CH), 0) + x * PART
+    want = lax.broadcasted_iota(jnp.int32, (PART, CH), 0) + pos[0] * PART
     pick = jnp.where(chan == want, 1.0, 0.0).astype(BF16)
     width = ROWS * COLS
     lane = lax.rem(lax.broadcasted_iota(jnp.int32, (PART, width), 1), COLS)
-    for f, ref in enumerate(frames):
+    core = pos[1]
+    for f, ref in zip((3 - 3 * core, 1, 2, 3 * core), frames):
         flat = ref[...].reshape(width, CH)
         mid = lax.dot_general(pick, flat, (((1,), (1,)), ((), ())), preferred_element_type=F32)
         left = jnp.where(lane == 0, 0.0, pltpu.roll(mid, 1, axis=1))
         right = jnp.where(lane == COLS - 1, 0.0, pltpu.roll(mid, width - 1, axis=1))
-        at = slice(f * width, (f + 1) * width)
+        at = pl.ds(pl.multiple_of(f * width, width), width)
         turned[0:PART, at] = left.astype(BF16)
         turned[PART : 2 * PART, at] = mid.astype(BF16)
         turned[2 * PART : 3 * PART, at] = right.astype(BF16)
 
 
 def turn_clips_kernel(pos, c0, c1, c2, c3, turned):
-    part_transposed((c0, c1, c2, c3), pos[0], turned)
+    part_transposed((c0, c1, c2, c3), pos, turned)
 
 
 def turn_clips(pos, clips):
@@ -301,11 +323,10 @@
     pos, i0, i1, i2, i3, inside, turn_c, s0, s1, pre, weight, head, sent, kept,
     spread, acc, turn_i, pgb, total,
 ):
-    x = pos[0]
     core = pos[1]
     grads = (i0, i1, i2, i3)
-    part_transposed(grads, x, turn_i)
-    outer_taps(i0, i3, weight, inside, acc, spread)
+    part_transposed(grads, pos, turn_i)
+    outer_taps(core, i0, i3, weight, inside, acc, spread)
     sum_bias = jnp.zeros((8, CH), F32)
     sum_head = jnp.zeros((8, CH), F32)
     for f in range(2):
@@ -479,9 +500,11 @@
     )(pos, mine, other)
 
 
-def ring_gather(value, plan):
+def ring_gather(value, plan, direct=False):
     below = permute(value, plan(1))
     above = permute(value, plan(-1))
+    if direct:
+        return jnp.stack([value, below, above, permute(value, plan(2))])
     half = value.shape[0] // 2
     across_low = permute(below[:half], plan(1))
     across_high = permute(above[half:], plan(-1))
@@ -502,19 +525,21 @@
     turned = turned.reshape(3, 3, 3 * CH, CH)
     w9 = weight.reshape(3, 3, 3 * CH, CH)
 
-    c1, c2 = gather_rows(pos, own, below, above, across, bias)
-    c0, c3 = chain(c2, 1), chain(c1, -1)
-    pre, s0, s1 = forward(c0, c3, inner(c1, c2, w9, "forward_inner"), w9, bias, head)
-    before, after = chain(s1, 1), chain(s0, -1)
-    i1, i2 = transposed(before, after, inner(s0, s1, turned, "transposed_inner"), turned)
+    c1, c2, near, far = gather_rows(pos, own, below, above, across, bias)
+    c0, c3 = trade(near, far)
+    acc = inner(c1, c2, w9, "forward_inner")
+    pre, s0, s1, near, far = forward(pos, c0, c3, acc, w9, bias, head)
+    near, far = trade(near, far)
+    acc = inner(s0, s1, turned, "transposed_inner")
+    i1, i2, edge, rim = transposed(pos, near, far, acc, turned)
     turn_c = turn_clips(pos, (c0, c1, c2, c3))
-    i0, i3 = chain(i2, 1), chain(i1, -1)
+    i0, i3 = trade(edge, rim)
     inside = inner(i1, i2, w9, "backward_inner")
     sent, kept = backward(pos, (i0, i1, i2, i3), inside, turn_c, (s0, s1), pre, w9, head)
     coded = encode_terms(kept, permute(sent, swap_core))
     pieces = lax.all_to_all(coded, PLANE, 0, 0, tiled=True)
     line = lax.all_to_all(recode(pieces), "z", 0, 0, tiled=True)
-    block = ring_gather(line, split_first)
+    block = ring_gather(line, split_first, direct=True)
     mine = ring_gather(block.reshape(32, CODED, 128), split_second)
     mine = mine.reshape(16, 8, CODED, 128)
     other = permute(mine, swap_core)

time: 149 us -> 144 us (0.966)
  starting transfers between devices: 37.7 us -> 33.6 us
  blocking collectives: 43 us -> 40.9 us
  local copies, waits for them, and re-layouts: 8.67 us -> 6.66 us
  Pallas kernels: 23.5 us -> 25.2 us
    ppermute x6 -> x3, starting transfers between devices: 15.5 us -> 12.1 us  [trade_far(): return lax.ppermute(value, CHAIN, pairs)]
    all_to_all x1, blocking collectives: 32 us -> 29.9 us  [per_device(): pieces = lax.all_to_all(coded, PLANE, 0, 0, tiled=True)]
    unnamed x14 -> x12, local copies, waits for them, and re-layouts: 8.05 us -> 6.05 us
    ppermute x6 -> x3, waiting for transfers between devices: 8.45 us -> 10.2 us  [trade_far(): return lax.ppermute(value, CHAIN, pairs)]
    ppermute x13 -> x15, waiting for transfers between devices: 26.2 us -> 25.3 us  [permute(): return lax.ppermute(value, ALL, moved(fn))]
    ppermute x13 -> x15, starting transfers between devices: 22.3 us -> 21.5 us  [permute(): return lax.ppermute(value, ALL, moved(fn))]
  transfers between devices with their start and end apart: 19 -> 18, of which waited for: 12 -> 12; matrix products, arithmetic and copies ran while one was open for 0% -> 0% of each run, Pallas kernels for 6% -> 7%
where the time goes in v5:
time: 144 us; the launch traced here: 143 us
  blocking collectives  40.9 us (28%)
  waiting for transfers between devices  35.6 us (25%)
  starting transfers between devices  33.6 us (23%)
  Pallas kernels  25.2 us (18%)
  local copies, waits for them, and re-layouts  6.66 us (5%)
    all_to_all x1, blocking collectives, per_device(): pieces = lax.all_to_all(coded, PLANE, 0, 0, tiled=True)  29.9 us
    ppermute x15, waiting for transfers between devices, permute(): return lax.ppermute(value, ALL, moved(fn))  25.3 us
    ppermute x15, starting transfers between devices, permute(): return lax.ppermute(value, ALL, moved(fn))  21.5 us
    ppermute x3, starting transfers between devices, trade_far(): return lax.ppermute(value, CHAIN, pairs)  12.1 us
    all_to_all x1, blocking collectives, per_device(): line = lax.all_to_all(recode(pieces), 'z', 0, 0, tiled=True)  11 us
    ppermute x3, waiting for transfers between devices, trade_far(): return lax.ppermute(value, CHAIN, pairs)  10.2 us
    pallas_call x3, Pallas kernels, inner(): pl.pallas_call(inner_kernel, out_shape=jax.ShapeDtypeStruct((2, ROWS, COL...  6.73 us
    unnamed x12, local copies, waits for them, and re-layouts  6.05 us
  transfers between devices with their start and end apart: 18, of which 12 were waited for; matrix products, arithmetic and copies ran while one was open for 0% of the time, Pallas kernels for 7%

profile of v5, /device:TPU:1, one launch (start us, length us, event | category | flops | bytes accessed | tf_op | source)
XLA Modules:
  0.0 143.2 jit_solution(2227138405252995985)
XLA Ops:
  0.6 3.6 %collective-permute-start.2 = (bf16[2,128,256]{2,1,0:T(8,128)(2,1)}, bf16[2,128,256]{2,1,0:T(8,128)(2,1)}, u32[]{:S(2)}, u32[]{:S(2)}) collective-permute-start(bf16[2,128,256]{2,1,0:T(8,128)(2,1)} %bitcast.30), channel_id=1, source_target_pairs={{0,2},{1,3},{2,0},{3,1},{4,6},{5,7},{6,4},{7,5},{8,10},{9,11},{10,... | collective-permute-start | bytes 393224 | tf_op jit(solution)/shard_map/ppermute | solution.py:43
  4.3 0.9 collective-permute-start.1
  5.1 0.6 collective-permute-start
  5.7 0.0 copy-start.3
  5.7 2.0 %copy-done.3 = bf16[3,3,3,256,256]{4,3,2,1,0:T(8,128)(2,1)S(1)} copy-done((bf16[3,3,3,256,256]{4,3,2,1,0:T(8,128)(2,1)S(1)}, bf16[3,3,3,256,256]{4,3,2,1,0:T(8,128)(2,1)}, u32[]{:S(2)}) %copy-start.3) | copy-done | bytes 3538968
  7.8 0.7 copy-done.4
  8.4 0.0 copy-start.5
  8.4 0.7 copy-done.5
  9.1 1.7 %turn_weights.1 = (bf16[3,3,3,256,256]{4,3,2,1,0:T(8,128)(2,1)S(1)}, bf16[3,3,3,256,256]{4,3,2,1,0:T(8,128)(2,1)S(1)}, f32[1,256]{1,0:T(1,128)S(1)}, f32[1,256]{1,0:T(1,128)S(1)}) custom-call(bf16[3,3,3,256,256]{4,3,2,1,0:T(8,128)(2,1)S(1)} %copy-done.3, f32[1,256]{1,0:T(1,128)S(1)} %bitcast.34, f32[1,256]{1,0:T(1,128)S(1)} %bitcast.35), custom_call_target="tpu_custom_call" | custom-call | flops 2000000000 | bytes 11534336 | tf_op jit(solution)/shard_map/turn_weights/pallas_call | solution.py:210
  10.8 0.0 copy-start
  10.8 1.8 %copy-done = bf16[3,3,3,256,256]{4,3,2,1,0:T(8,128)(2,1)} copy-done((bf16[3,3,3,256,256]{4,3,2,1,0:T(8,128)(2,1)}, bf16[3,3,3,256,256]{4,3,2,1,0:T(8,128)(2,1)S(1)}, u32[]{:S(2)}) %copy-start) | copy-done | bytes 3538968
  12.6 0.1 pad_add_fusion.pos_ref.pos
  12.6 0.0 collective-permute-done.2.across
  12.7 0.0 collective-permute-done.1.above
  12.7 0.2 collective-permute-done.below
  12.8 0.0 copy-start.2
  12.8 0.9 copy-done.2
  13.7 1.1 gather_rows.1
  14.9 1.4 %collective-permute-start.3 = (bf16[4,128,256]{2,1,0:T(8,128)(2,1)S(1)}, bf16[4,128,256]{2,1,0:T(8,128)(2,1)S(1)}, u32[]{:S(2)}, u32[]{:S(2)}) collective-permute-start(bf16[4,128,256]{2,1,0:T(8,128)(2,1)S(1)} %get-tuple-element.25), channel_id=1, source_target_pairs={{0,4},{1,5},{2,6},{3,7},{4,0},{5,1},{6,2},{7,3},{8,12},{9,13},{10,... | collective-permute-start | bytes 786440 | tf_op jit(solution)/shard_map/ppermute | solution.py:43
  16.3 3.1 %collective-permute-start.4 = (bf16[4,128,256]{2,1,0:T(8,128)(2,1)S(1)}, bf16[4,128,256]{2,1,0:T(8,128)(2,1)S(1)}, u32[]{:S(2)}, u32[]{:S(2)}) collective-permute-start(bf16[4,128,256]{2,1,0:T(8,128)(2,1)S(1)} %get-tuple-element.26), channel_id=1, source_target_pairs={{4,8},{8,4},{12,16},{16,12},{20,24},{24,20},{28,32},{32,28},{36,40... | collective-permute-start | bytes 786440 | tf_op jit(solution)/shard_map/ppermute | solution.py:66
  19.4 2.2 %forward_inner.1.acc = f32[2,4,128,256]{3,2,1,0:T(8,128)S(1)} custom-call(bf16[4,128,256]{2,1,0:T(8,128)(2,1)S(1)} %get-tuple-element.27.first.c1, bf16[4,128,256]{2,1,0:T(8,128)(2,1)S(1)} %get-tuple-element.28.second.c2, bf16[3,3,768,256]{3,2,1,0:T(8,128)(2,1)S(1)} %bitcast.24), custom_call_target="tpu_custom_call" | custom-call | flops 2415919104 | bytes 6291456 | tf_op jit(solution)/shard_map/forward_inner/pallas_call | solution.py:232
  21.6 0.0 collective-permute-done.3.near.c0
  21.6 3.9 %collective-permute-done.4.far.c3 = bf16[4,128,256]{2,1,0:T(8,128)(2,1)S(1)} collective-permute-done((bf16[4,128,256]{2,1,0:T(8,128)(2,1)S(1)}, bf16[4,128,256]{2,1,0:T(8,128)(2,1)S(1)}, u32[]{:S(2)}, u32[]{:S(2)}) %collective-permute-start.4) | collective-permute-done | bytes 262176 | tf_op jit(solution)/shard_map/ppermute | solution.py:66
  25.5 2.3 %forward.1 = (f32[2,4,128,256]{3,2,1,0:T(8,128)S(1)}, bf16[4,128,256]{2,1,0:T(8,128)(2,1)S(1)}, bf16[4,128,256]{2,1,0:T(8,128)(2,1)S(1)}, bf16[4,128,256]{2,1,0:T(8,128)(2,1)S(1)}, bf16[4,128,256]{2,1,0:T(8,128)(2,1)S(1)}) custom-call(s32[3]{0:T(128)S(1)} %pad_add_fusion.pos_ref.pos, bf16[4,128,256]{2,1,0:T(8,128)(2,1)S(1)} %collective-permute-done.3.near.c0, ...), custom_call_target="tpu_custom_call" | custom-call | flops 1207959552 | bytes 6291456 | tf_op jit(solution)/shard_map/forward/pallas_call | solution.py:245
  27.8 0.1 collective-permute-start.5
  27.9 4.4 %collective-permute-start.6 = (bf16[4,128,256]{2,1,0:T(8,128)(2,1)S(1)}, bf16[4,128,256]{2,1,0:T(8,128)(2,1)S(1)}, u32[]{:S(2)}, u32[]{:S(2)}) collective-permute-start(bf16[4,128,256]{2,1,0:T(8,128)(2,1)S(1)} %get-tuple-element.32), channel_id=1, source_target_pairs={{4,8},{8,4},{12,16},{16,12},{20,24},{24,20},{28,32},{32,28},{36,40... | collective-permute-start | bytes 786440 | tf_op jit(solution)/shard_map/ppermute | solution.py:66
  32.3 0.0 copy-done.1
  32.3 2.3 %transposed_inner.1.acc = f32[2,4,128,256]{3,2,1,0:T(8,128)S(1)} custom-call(bf16[4,128,256]{2,1,0:T(8,128)(2,1)S(1)} %get-tuple-element.33.first.s0, bf16[4,128,256]{2,1,0:T(8,128)(2,1)S(1)} %get-tuple-element.34.second.s1, bf16[3,3,768,256]{3,2,1,0:T(8,128)(2,1)S(1)} %bitcast.28), custom_call_target="tpu_custom_call" | custom-call | flops 2415919104 | bytes 6291456 | tf_op jit(solution)/shard_map/transposed_inner/pallas_call | solution.py:232
  34.6 0.0 collective-permute-done.5.near
  34.6 3.8 %collective-permute-done.6.far = bf16[4,128,256]{2,1,0:T(8,128)(2,1)S(1)} collective-permute-done((bf16[4,128,256]{2,1,0:T(8,128)(2,1)S(1)}, bf16[4,128,256]{2,1,0:T(8,128)(2,1)S(1)}, u32[]{:S(2)}, u32[]{:S(2)}) %collective-permute-start.6) | collective-permute-done | bytes 262176 | tf_op jit(solution)/shard_map/ppermute | solution.py:66
  38.4 1.9 %transposed.1 = (bf16[4,128,256]{2,1,0:T(8,128)(2,1)S(1)}, bf16[4,128,256]{2,1,0:T(8,128)(2,1)S(1)}, bf16[4,128,256]{2,1,0:T(8,128)(2,1)S(1)}, bf16[4,128,256]{2,1,0:T(8,128)(2,1)S(1)}) custom-call(s32[3]{0:T(128)S(1)} %pad_add_fusion.pos_ref.pos, bf16[4,128,256]{2,1,0:T(8,128)(2,1)S(1)} %collective-permute-done.5.near, ...), custom_call_target="tpu_custom_call" | custom-call | flops 1207959552 | bytes 5242880 | tf_op jit(solution)/shard_map/transposed/pallas_call | solution.py:259
  40.3 0.1 collective-permute-start.7
  40.4 4.6 %collective-permute-start.8 = (bf16[4,128,256]{2,1,0:T(8,128)(2,1)S(1)}, bf16[4,128,256]{2,1,0:T(8,128)(2,1)S(1)}, u32[]{:S(2)}, u32[]{:S(2)}) collective-permute-start(bf16[4,128,256]{2,1,0:T(8,128)(2,1)S(1)} %get-tuple-element.39), channel_id=1, source_target_pairs={{4,8},{8,4},{12,16},{16,12},{20,24},{24,20},{28,32},{32,28},{36,40... | collective-permute-start | bytes 786440 | tf_op jit(solution)/shard_map/ppermute | solution.py:66
  45.0 1.1 turn_clips.1.turn_c
  46.1 2.3 %backward_inner.1.inside = f32[2,4,128,256]{3,2,1,0:T(8,128)S(1)} custom-call(bf16[4,128,256]{2,1,0:T(8,128)(2,1)S(1)} %get-tuple-element.37.first.i1, bf16[4,128,256]{2,1,0:T(8,128)(2,1)S(1)} %get-tuple-element.38.second.i2, bf16[3,3,768,256]{3,2,1,0:T(8,128)(2,1)S(1)} %bitcast.26), custom_call_target="tpu_custom_call" | custom-call | flops 2415919104 | bytes 6291456 | tf_op jit(solution)/shard_map/backward_inner/pallas_call | solution.py:232
  48.4 0.0 collective-permute-done.7.i0
  48.4 2.6 %collective-permute-done.8.i3 = bf16[4,128,256]{2,1,0:T(8,128)(2,1)S(1)} collective-permute-done((bf16[4,128,256]{2,1,0:T(8,128)(2,1)S(1)}, bf16[4,128,256]{2,1,0:T(8,128)(2,1)S(1)}, u32[]{:S(2)}, u32[]{:S(2)}) %collective-permute-start.8) | collective-permute-done | bytes 262176 | tf_op jit(solution)/shard_map/ppermute | solution.py:66
  50.9 4.4 %backward.1 = (f32[224,8,128]{2,1,0:T(8,128)S(1)}, f32[224,8,128]{2,1,0:T(8,128)S(1)}) custom-call(s32[3]{0:T(128)S(1)} %pad_add_fusion.pos_ref.pos, bf16[4,128,256]{2,1,0:T(8,128)(2,1)S(1)} %collective-permute-done.7.i0, bf16[4,128,256]{2,1,0:T(8,128)(2,1)S(1)} %get-tuple-element.37.first.i1, bf16[4,128,256]{2,1,0:T(8,128)(2,1)S(1)} %get-tuple-element.38.second.i2, ...), custom_call_target="tpu_custom_call" | custom-call | flops 5798205952 | bytes 10485760 | tf_op jit(solution)/shard_map/backward/pallas_call | solution.py:378
  55.3 0.1 collective-permute-start.9
  55.4 2.5 %collective-permute-done.9.received = f32[224,8,128]{2,1,0:T(8,128)S(1)} collective-permute-done((f32[224,8,128]{2,1,0:T(8,128)S(1)}, f32[224,8,128]{2,1,0:T(8,128)S(1)}, u32[]{:S(2)}, u32[]{:S(2)}) %collective-permute-start.9) | collective-permute-done | bytes 917536 | tf_op jit(solution)/shard_map/ppermute | solution.py:43
  57.8 0.8 encode_terms.1
  58.7 29.9 %all_to_all.10.pieces = bf16[32,64,128]{2,1,0:T(8,128)(2,1)S(1)} all-to-all(bf16[32,64,128]{2,1,0:T(8,128)(2,1)S(1)} %encode_terms.1), channel_id=1, replica_groups=mesh['yh'=2,'z'=8,'yl'=2,'c'=2,'x'=4] {'yh','z','yl'}, dimensions={0} | all-to-all | bytes 1048576 | tf_op jit(solution)/shard_map/all_to_all | solution.py:540
  88.6 0.4 recode.1
  89.0 11.0 %all_to_all.11 = bf16[8,64,128]{2,1,0:T(8,128)(2,1)S(1)} all-to-all(bf16[8,64,128]{2,1,0:T(8,128)(2,1)S(1)} %recode.1), channel_id=1, replica_groups=mesh['yh'=2,'z'=8,'yl'=2,'c'=2,'x'=4] {'z'}, dimensions={0} | all-to-all | bytes 262144 | tf_op jit(solution)/shard_map/all_to_all | solution.py:541
  100.0 0.6 collective-permute-start.12
  100.6 2.1 %collective-permute-start.11 = (bf16[8,64,128]{2,1,0:T(8,128)(2,1)S(1)}, bf16[8,64,128]{2,1,0:T(8,128)(2,1)S(1)}, u32[]{:S(2)}, u32[]{:S(2)}) collective-permute-start(bf16[8,64,128]{2,1,0:T(8,128)(2,1)S(1)} %all_to_all.11), channel_id=1, source_target_pairs={{0,136},{1,137},{2,138},{3,139},{4,7},{5,4},{6,5},{7,6},{8,0},{9,1... | collective-permute-start | bytes 393224 | tf_op jit(solution)/shard_map/ppermute | solution.py:43
  102.7 0.0 collective-permute-start.10
  102.7 2.6 %collective-permute-done.12 = bf16[8,64,128]{2,1,0:T(8,128)(2,1)S(1)} collective-permute-done((bf16[8,64,128]{2,1,0:T(8,128)(2,1)S(1)}, bf16[8,64,128]{2,1,0:T(8,128)(2,1)S(1)}, u32[]{:S(2)}, u32[]{:S(2)}) %collective-permute-start.12) | collective-permute-done | bytes 131104 | tf_op jit(solution)/shard_map/ppermute | solution.py:43
  105.3 1.1 collective-permute-done.11
  106.4 1.6 %collective-permute-done.10 = bf16[8,64,128]{2,1,0:T(8,128)(2,1)S(1)} collective-permute-done((bf16[8,64,128]{2,1,0:T(8,128)(2,1)S(1)}, bf16[8,64,128]{2,1,0:T(8,128)(2,1)S(1)}, u32[]{:S(2)}, u32[]{:S(2)}) %collective-permute-start.10) | collective-permute-done | bytes 131104 | tf_op jit(solution)/shard_map/ppermute | solution.py:43
  108.0 0.1 pad_maximum_fusion.1
  108.1 0.6 collective-permute-start.14
  108.7 0.9 collective-permute-start.13
  109.6 6.9 %collective-permute-done.14 = bf16[32,64,128]{2,1,0:T(8,128)(2,1)S(1)} collective-permute-done((bf16[32,64,128]{2,1,0:T(8,128)(2,1)S(1)}, bf16[32,64,128]{2,1,0:T(8,128)(2,1)S(1)}, u32[]{:S(2)}, u32[]{:S(2)}) %collective-permute-start.14) | collective-permute-done | bytes 524320 | tf_op jit(solution)/shard_map/ppermute | solution.py:43
  116.5 1.5 %collective-permute-start.16 = (bf16[16,64,128]{2,1,0:T(8,128)(2,1)S(1)}, bf16[16,64,128]{2,1,0:T(8,128)(2,1)S(1)}, u32[]{:S(2)}, u32[]{:S(2)}) collective-permute-start(bf16[16,64,128]{2,1,0:T(8,128)(2,1)S(1)} %slice.17), channel_id=1, source_target_pairs={{0,3},{1,0},{2,1},{3,2},{4,140},{5,141},{6,142},{7,143},{8,11},{9,... | collective-permute-start | bytes 786440 | tf_op jit(solution)/shard_map/ppermute | solution.py:43
  118.0 0.0 collective-permute-done.13
  118.0 0.1 collective-permute-start.15
  118.1 3.9 %collective-permute-done.16 = bf16[16,64,128]{2,1,0:T(8,128)(2,1)S(1)} collective-permute-done((bf16[16,64,128]{2,1,0:T(8,128)(2,1)S(1)}, bf16[16,64,128]{2,1,0:T(8,128)(2,1)S(1)}, u32[]{:S(2)}, u32[]{:S(2)}) %collective-permute-start.16) | collective-permute-done | bytes 262176 | tf_op jit(solution)/shard_map/ppermute | solution.py:43
  122.1 2.8 %collective-permute-done.15 = bf16[16,64,128]{2,1,0:T(8,128)(2,1)S(1)} collective-permute-done((bf16[16,64,128]{2,1,0:T(8,128)(2,1)S(1)}, bf16[16,64,128]{2,1,0:T(8,128)(2,1)S(1)}, u32[]{:S(2)}, u32[]{:S(2)}) %collective-permute-start.15) | collective-permute-done | bytes 262176 | tf_op jit(solution)/shard_map/ppermute | solution.py:43
  124.9 0.3 pad_maximum_fusion
  125.2 8.8 %collective-permute-start.17 = (bf16[16,8,64,128]{3,2,1,0:T(8,128)(2,1)S(1)}, bf16[16,8,64,128]{3,2,1,0:T(8,128)(2,1)S(1)}, u32[]{:S(2)}, u32[]{:S(2)}) collective-permute-start(bf16[16,8,64,128]{3,2,1,0:T(8,128)(2,1)S(1)} %bitcast.22), channel_id=1, source_target_pairs={{0,4},{1,5},{2,6},{3,7},{4,0},{5,1},{6,2},{7,3},{8,12},{9,13},{10,... | collective-permute-start | bytes 6291464 | tf_op jit(solution)/shard_map/ppermute | solution.py:43
  134.0 3.8 %collective-permute-done.17.other = bf16[16,8,64,128]{3,2,1,0:T(8,128)(2,1)S(1)} collective-permute-done((bf16[16,8,64,128]{3,2,1,0:T(8,128)(2,1)S(1)}, bf16[16,8,64,128]{3,2,1,0:T(8,128)(2,1)S(1)}, u32[]{:S(2)}, u32[]{:S(2)}) %collective-permute-start.17) | collective-permute-done | bytes 2097184 | tf_op jit(solution)/shard_map/ppermute | solution.py:43
  137.8 4.8 %assemble.1 = (f32[27,4,8,8,256]{4,3,2,1,0:T(8,128)}, f32[16,256]{1,0:T(8,128)S(1)}) custom-call(s32[3]{0:T(128)S(1)} %pad_add_fusion.pos_ref.pos, bf16[16,8,64,128]{3,2,1,0:T(8,128)(2,1)S(1)} %bitcast.23, bf16[16,8,64,128]{3,2,1,0:T(8,128)(2,1)S(1)} %collective-permute-done.17.other), custom_call_target="tpu_custom_call" | custom-call | flops 1000000 | bytes 15728640 | tf_op jit(solution)/shard_map/assemble/pallas_call | solution.py:485
  142.6 0.6 fusion
  (5 shorter events, 0.1 us)
Async XLA Ops:
  0.6 12.0 %collective-permute-start.2 = (bf16[2,128,256]{2,1,0:T(8,128)(2,1)}, bf16[2,128,256]{2,1,0:T(8,128)(2,1)}, u32[]{:S(2)}, u32[]{:S(2)}) collective-permute-start(bf16[2,128,256]{2,1,0:T(8,128)(2,1)} %bitcast.30), channel_id=1, source_target_pairs={{0,2},{1,3},{2,0},{3,1},{4,6},{5,7},{6,4},{7,5},{8,10},{9,11},{10,... | collective-permute-start | bytes 393224 | tf_op jit(solution)/shard_map/ppermute | solution.py:43
  4.3 8.4 %collective-permute-start.1 = (bf16[2,128,256]{2,1,0:T(8,128)(2,1)}, bf16[2,128,256]{2,1,0:T(8,128)(2,1)}, u32[]{:S(2)}, u32[]{:S(2)}) collective-permute-start(bf16[2,128,256]{2,1,0:T(8,128)(2,1)} %bitcast.31), channel_id=1, source_target_pairs={{0,3},{1,0},{2,1},{3,2},{4,7},{5,4},{6,5},{7,6},{8,11},{9,8},{10,9... | collective-permute-start | bytes 393224 | tf_op jit(solution)/shard_map/ppermute | solution.py:43
  5.1 7.7 %collective-permute-start = (bf16[2,128,256]{2,1,0:T(8,128)(2,1)}, bf16[2,128,256]{2,1,0:T(8,128)(2,1)}, u32[]{:S(2)}, u32[]{:S(2)}) collective-permute-start(bf16[2,128,256]{2,1,0:T(8,128)(2,1)} %bitcast.32), channel_id=1, source_target_pairs={{0,1},{1,2},{2,3},{3,0},{4,5},{5,6},{6,7},{7,4},{8,9},{9,10},{10,1... | collective-permute-start | bytes 393224 | tf_op jit(solution)/shard_map/ppermute | solution.py:43
  5.7 2.0 %copy-start.3 = (bf16[3,3,3,256,256]{4,3,2,1,0:T(8,128)(2,1)S(1)}, bf16[3,3,3,256,256]{4,3,2,1,0:T(8,128)(2,1)}, u32[]{:S(2)}) copy-start(bf16[3,3,3,256,256]{4,3,2,1,0:T(8,128)(2,1)} %weight.1) | copy-start | bytes 10616836
  7.7 0.7 copy-start.4
  8.4 0.7 copy-start.5
  10.8 1.8 %copy-start = (bf16[3,3,3,256,256]{4,3,2,1,0:T(8,128)(2,1)}, bf16[3,3,3,256,256]{4,3,2,1,0:T(8,128)(2,1)S(1)}, u32[]{:S(2)}) copy-start(bf16[3,3,3,256,256]{4,3,2,1,0:T(8,128)(2,1)S(1)} %get-tuple-element.35) | copy-start | bytes 10616836
  12.8 0.9 copy-start.2
  14.9 6.8 %collective-permute-start.3 = (bf16[4,128,256]{2,1,0:T(8,128)(2,1)S(1)}, bf16[4,128,256]{2,1,0:T(8,128)(2,1)S(1)}, u32[]{:S(2)}, u32[]{:S(2)}) collective-permute-start(bf16[4,128,256]{2,1,0:T(8,128)(2,1)S(1)} %get-tuple-element.25), channel_id=1, source_target_pairs={{0,4},{1,5},{2,6},{3,7},{4,0},{5,1},{6,2},{7,3},{8,12},{9,13},{10,... | collective-permute-start | bytes 786440 | tf_op jit(solution)/shard_map/ppermute | solution.py:43
  16.3 9.2 %collective-permute-start.4 = (bf16[4,128,256]{2,1,0:T(8,128)(2,1)S(1)}, bf16[4,128,256]{2,1,0:T(8,128)(2,1)S(1)}, u32[]{:S(2)}, u32[]{:S(2)}) collective-permute-start(bf16[4,128,256]{2,1,0:T(8,128)(2,1)S(1)} %get-tuple-element.26), channel_id=1, source_target_pairs={{4,8},{8,4},{12,16},{16,12},{20,24},{24,20},{28,32},{32,28},{36,40... | collective-permute-start | bytes 786440 | tf_op jit(solution)/shard_map/ppermute | solution.py:66
  25.5 6.8 %copy-start.1 = (bf16[3,3,3,256,256]{4,3,2,1,0:T(8,128)(2,1)S(1)}, bf16[3,3,3,256,256]{4,3,2,1,0:T(8,128)(2,1)}, u32[]{:S(2)}) copy-start(bf16[3,3,3,256,256]{4,3,2,1,0:T(8,128)(2,1)} %copy-done) | copy-start | bytes 10616836
  27.8 6.8 %collective-permute-start.5 = (bf16[4,128,256]{2,1,0:T(8,128)(2,1)S(1)}, bf16[4,128,256]{2,1,0:T(8,128)(2,1)S(1)}, u32[]{:S(2)}, u32[]{:S(2)}) collective-permute-start(bf16[4,128,256]{2,1,0:T(8,128)(2,1)S(1)} %get-tuple-element.31), channel_id=1, source_target_pairs={{0,4},{1,5},{2,6},{3,7},{4,0},{5,1},{6,2},{7,3},{8,12},{9,13},{10,... | collective-permute-start | bytes 786440 | tf_op jit(solution)/shard_map/ppermute | solution.py:43
  27.9 10.5 %collective-permute-start.6 = (bf16[4,128,256]{2,1,0:T(8,128)(2,1)S(1)}, bf16[4,128,256]{2,1,0:T(8,128)(2,1)S(1)}, u32[]{:S(2)}, u32[]{:S(2)}) collective-permute-start(bf16[4,128,256]{2,1,0:T(8,128)(2,1)S(1)} %get-tuple-element.32), channel_id=1, source_target_pairs={{4,8},{8,4},{12,16},{16,12},{20,24},{24,20},{28,32},{32,28},{36,40... | collective-permute-start | bytes 786440 | tf_op jit(solution)/shard_map/ppermute | solution.py:66
  40.3 8.0 %collective-permute-start.7 = (bf16[4,128,256]{2,1,0:T(8,128)(2,1)S(1)}, bf16[4,128,256]{2,1,0:T(8,128)(2,1)S(1)}, u32[]{:S(2)}, u32[]{:S(2)}) collective-permute-start(bf16[4,128,256]{2,1,0:T(8,128)(2,1)S(1)} %get-tuple-element.36), channel_id=1, source_target_pairs={{0,4},{1,5},{2,6},{3,7},{4,0},{5,1},{6,2},{7,3},{8,12},{9,13},{10,... | collective-permute-start | bytes 786440 | tf_op jit(solution)/shard_map/ppermute | solution.py:43
  40.4 10.5 %collective-permute-start.8 = (bf16[4,128,256]{2,1,0:T(8,128)(2,1)S(1)}, bf16[4,128,256]{2,1,0:T(8,128)(2,1)S(1)}, u32[]{:S(2)}, u32[]{:S(2)}) collective-permute-start(bf16[4,128,256]{2,1,0:T(8,128)(2,1)S(1)} %get-tuple-element.39), channel_id=1, source_target_pairs={{4,8},{8,4},{12,16},{16,12},{20,24},{24,20},{28,32},{32,28},{36,40... | collective-permute-start | bytes 786440 | tf_op jit(solution)/shard_map/ppermute | solution.py:66
  55.3 2.6 %collective-permute-start.9 = (f32[224,8,128]{2,1,0:T(8,128)S(1)}, f32[224,8,128]{2,1,0:T(8,128)S(1)}, u32[]{:S(2)}, u32[]{:S(2)}) collective-permute-start(f32[224,8,128]{2,1,0:T(8,128)S(1)} %get-tuple-element.42), channel_id=1, source_target_pairs={{0,4},{1,5},{2,6},{3,7},{4,0},{5,1},{6,2},{7,3},{8,12},{9,13},{10,... | collective-permute-start | bytes 2752520 | tf_op jit(solution)/shard_map/ppermute | solution.py:43
  100.0 5.3 %collective-permute-start.12 = (bf16[8,64,128]{2,1,0:T(8,128)(2,1)S(1)}, bf16[8,64,128]{2,1,0:T(8,128)(2,1)S(1)}, u32[]{:S(2)}, u32[]{:S(2)}) collective-permute-start(bf16[8,64,128]{2,1,0:T(8,128)(2,1)S(1)} %all_to_all.11), channel_id=1, source_target_pairs={{0,128},{1,129},{2,130},{3,131},{4,6},{5,7},{6,4},{7,5},{8,136},{9... | collective-permute-start | bytes 393224 | tf_op jit(solution)/shard_map/ppermute | solution.py:43
  100.6 5.8 %collective-permute-start.11 = (bf16[8,64,128]{2,1,0:T(8,128)(2,1)S(1)}, bf16[8,64,128]{2,1,0:T(8,128)(2,1)S(1)}, u32[]{:S(2)}, u32[]{:S(2)}) collective-permute-start(bf16[8,64,128]{2,1,0:T(8,128)(2,1)S(1)} %all_to_all.11), channel_id=1, source_target_pairs={{0,136},{1,137},{2,138},{3,139},{4,7},{5,4},{6,5},{7,6},{8,0},{9,1... | collective-permute-start | bytes 393224 | tf_op jit(solution)/shard_map/ppermute | solution.py:43
  102.7 5.3 %collective-permute-start.10 = (bf16[8,64,128]{2,1,0:T(8,128)(2,1)S(1)}, bf16[8,64,128]{2,1,0:T(8,128)(2,1)S(1)}, u32[]{:S(2)}, u32[]{:S(2)}) collective-permute-start(bf16[8,64,128]{2,1,0:T(8,128)(2,1)S(1)} %all_to_all.11), channel_id=1, source_target_pairs={{0,8},{1,9},{2,10},{3,11},{4,5},{5,6},{6,7},{7,4},{8,128},{9,129},... | collective-permute-start | bytes 393224 | tf_op jit(solution)/shard_map/ppermute | solution.py:43
  108.1 8.4 %collective-permute-start.14 = (bf16[32,64,128]{2,1,0:T(8,128)(2,1)S(1)}, bf16[32,64,128]{2,1,0:T(8,128)(2,1)S(1)}, u32[]{:S(2)}, u32[]{:S(2)}) collective-permute-start(bf16[32,64,128]{2,1,0:T(8,128)(2,1)S(1)} %bitcast.36), channel_id=1, source_target_pairs={{0,3},{1,0},{2,1},{3,2},{4,140},{5,141},{6,142},{7,143},{8,11},{9,... | collective-permute-start | bytes 1572872 | tf_op jit(solution)/shard_map/ppermute | solution.py:43
  108.7 9.3 %collective-permute-start.13 = (bf16[32,64,128]{2,1,0:T(8,128)(2,1)S(1)}, bf16[32,64,128]{2,1,0:T(8,128)(2,1)S(1)}, u32[]{:S(2)}, u32[]{:S(2)}) collective-permute-start(bf16[32,64,128]{2,1,0:T(8,128)(2,1)S(1)} %bitcast.37), channel_id=1, source_target_pairs={{0,1},{1,2},{2,3},{3,0},{4,12},{5,13},{6,14},{7,15},{8,9},{9,10},{... | collective-permute-start | bytes 1572872 | tf_op jit(solution)/shard_map/ppermute | solution.py:43
  116.5 5.6 %collective-permute-start.16 = (bf16[16,64,128]{2,1,0:T(8,128)(2,1)S(1)}, bf16[16,64,128]{2,1,0:T(8,128)(2,1)S(1)}, u32[]{:S(2)}, u32[]{:S(2)}) collective-permute-start(bf16[16,64,128]{2,1,0:T(8,128)(2,1)S(1)} %slice.17), channel_id=1, source_target_pairs={{0,3},{1,0},{2,1},{3,2},{4,140},{5,141},{6,142},{7,143},{8,11},{9,... | collective-permute-start | bytes 786440 | tf_op jit(solution)/shard_map/ppermute | solution.py:43
  118.0 6.8 %collective-permute-start.15 = (bf16[16,64,128]{2,1,0:T(8,128)(2,1)S(1)}, bf16[16,64,128]{2,1,0:T(8,128)(2,1)S(1)}, u32[]{:S(2)}, u32[]{:S(2)}) collective-permute-start(bf16[16,64,128]{2,1,0:T(8,128)(2,1)S(1)} %slice.16), channel_id=1, source_target_pairs={{0,1},{1,2},{2,3},{3,0},{4,12},{5,13},{6,14},{7,15},{8,9},{9,10},{... | collective-permute-start | bytes 786440 | tf_op jit(solution)/shard_map/ppermute | solution.py:43
  125.2 12.6 %collective-permute-start.17 = (bf16[16,8,64,128]{3,2,1,0:T(8,128)(2,1)S(1)}, bf16[16,8,64,128]{3,2,1,0:T(8,128)(2,1)S(1)}, u32[]{:S(2)}, u32[]{:S(2)}) collective-permute-start(bf16[16,8,64,128]{3,2,1,0:T(8,128)(2,1)S(1)} %bitcast.22), channel_id=1, source_target_pairs={{0,4},{1,5},{2,6},{3,7},{4,0},{5,1},{6,2},{7,3},{8,12},{9,13},{10,... | collective-permute-start | bytes 6291464 | tf_op jit(solution)/shard_map/ppermute | solution.py:43

commit v6 on v5

--- a/solution.py
+++ b/solution.py
@@ -157,18 +157,23 @@
             acc[0:1, dst : dst + rows] += apply_tap(spread, weight, a, b, 1, 1)
 
 
-def outer_taps(core, near, far, weight, acc, total, spread):
-    spread_columns((near, far), spread)
-    total[...] = acc[...]
-    for n, f in ((0, 1 - core), (1, core)):
-        at = pl.ds(f, 1)
-        for b in (1, 0, 2):
-            rows, _, dst = row_range(b)
-            total[at, dst : dst + rows] += apply_tap(spread, weight, 2 * f, b, n, 1)
-
-
-def forward_kernel(pos, near, far, acc, weight, bias, head, pre, g0, g1, near_out, far_out, spread):
-    outer_taps(pos[1], near, far, weight, acc, pre, spread)
+def side_taps(f, halo, weight, acc, total, spread):
+    spread_columns((halo,), spread)
+    at = pl.ds(f, 1)
+    rest = pl.ds(1 - f, 1)
+    total[rest] = acc[rest]
+    total[at] = acc[at] + apply_tap(spread, weight, 2 * f, 1, 0, 1)
+    for b in (0, 2):
+        rows, _, dst = row_range(b)
+        total[at, dst : dst + rows] += apply_tap(spread, weight, 2 * f, b, 0, 1)
+
+
+def near_kernel(pos, near, acc, weight, total, spread):
+    side_taps(1 - pos[1], near, weight, acc, total, spread)
+
+
+def forward_kernel(pos, far, acc, weight, bias, head, pre, g0, g1, near_out, far_out, spread):
+    side_taps(pos[1], far, weight, acc, pre, spread)
     for f, out in ((0, g0), (1, g1)):
         for r in range(ROWS):
             value = pre[f, r] + bias[...]
@@ -179,8 +184,8 @@
     place_edges(pos[1], g0, g1, near_out, far_out)
 
 
-def transpose_kernel(pos, near, far, acc, weight, g0, g1, near_out, far_out, spread, total):
-    outer_taps(pos[1], near, far, weight, acc, total, spread)
+def transpose_kernel(pos, far, acc, weight, g0, g1, near_out, far_out, spread, total):
+    side_taps(pos[1], far, weight, acc, total, spread)
     for f, out in ((0, g0), (1, g1)):
         out[...] = total[f].astype(BF16)
     place_edges(pos[1], g0, g1, near_out, far_out)
@@ -241,31 +246,44 @@
     )(first, second, w9)
 
 
-def forward(pos, near, far, acc, w9, bias, head):
+def forward(pos, far, acc, w9, bias, head):
     return pl.pallas_call(
         forward_kernel,
         out_shape=(jax.ShapeDtypeStruct((2, ROWS, COLS, CH), F32),) + (FRAME,) * 4,
-        in_specs=[SMEM] + [VMEM] * 6,
+        in_specs=[SMEM] + [VMEM] * 5,
         out_specs=(VMEM,) * 5,
         scratch_shapes=[conv_scratch()["spread"]],
         compiler_params=params(),
         cost_estimate=cost(CONV_FLOPS / 3, 6 << 20),
         name="forward",
-    )(pos, near, far, acc, w9, bias, head)
-
-
-def transposed(pos, near, far, acc, w9):
+    )(pos, far, acc, w9, bias, head)
+
+
+def add_near(pos, near, acc, w9, name):
+    return pl.pallas_call(
+        near_kernel,
+        out_shape=jax.ShapeDtypeStruct((2, ROWS, COLS, CH), F32),
+        in_specs=[SMEM] + [VMEM] * 3,
+        out_specs=VMEM,
+        scratch_shapes=[conv_scratch()["spread"]],
+        compiler_params=params(),
+        cost_estimate=cost(CONV_FLOPS / 6, 4 << 20),
+        name=name,
+    )(pos, near, acc, w9)
+
+
+def transposed(pos, far, acc, w9):
     s = conv_scratch()
     return pl.pallas_call(
         transpose_kernel,
         out_shape=(FRAME,) * 4,
-        in_specs=[SMEM] + [VMEM] * 4,
+        in_specs=[SMEM] + [VMEM] * 3,
         out_specs=(VMEM,) * 4,
         scratch_shapes=[s["spread"], s["acc"]],
         compiler_params=params(),
         cost_estimate=cost(CONV_FLOPS / 3, 5 << 20),
         name="transposed",
-    )(pos, near, far, acc, w9)
+    )(pos, far, acc, w9)
 
 
 def part_transposed(frames, pos, turned):
@@ -286,20 +304,25 @@
         turned[2 * PART : 3 * PART, at] = right.astype(BF16)
 
 
-def turn_clips_kernel(pos, c0, c1, c2, c3, turned):
+def near_turn_kernel(pos, near, acc, weight, c0, c1, c2, c3, total, turned, spread):
+    side_taps(1 - pos[1], near, weight, acc, total, spread)
     part_transposed((c0, c1, c2, c3), pos, turned)
 
 
-def turn_clips(pos, clips):
-    return pl.pallas_call(
-        turn_clips_kernel,
-        out_shape=jax.ShapeDtypeStruct((3 * PART, 4 * ROWS * COLS), BF16),
-        in_specs=[SMEM] + [VMEM] * 4,
-        out_specs=VMEM,
-        compiler_params=params(),
-        cost_estimate=cost(1e9, 2 << 20),
-        name="turn_clips",
-    )(pos, *clips)
+def add_near_turn(pos, near, acc, w9, clips):
+    return pl.pallas_call(
+        near_turn_kernel,
+        out_shape=(
+            jax.ShapeDtypeStruct((2, ROWS, COLS, CH), F32),
+            jax.ShapeDtypeStruct((3 * PART, 4 * ROWS * COLS), BF16),
+        ),
+        in_specs=[SMEM] + [VMEM] * 7,
+        out_specs=(VMEM, VMEM),
+        scratch_shapes=[conv_scratch()["spread"]],
+        compiler_params=params(),
+        cost_estimate=cost(CONV_FLOPS / 4, 6 << 20),
+        name="transposed_near",
+    )(pos, near, acc, w9, *clips)
 
 
 def correlate(turned, grads, b):
@@ -326,7 +349,7 @@
     core = pos[1]
     grads = (i0, i1, i2, i3)
     part_transposed(grads, pos, turn_i)
-    outer_taps(core, i0, i3, weight, inside, acc, spread)
+    side_taps(core, i3, weight, inside, acc, spread)
     sum_bias = jnp.zeros((8, CH), F32)
     sum_head = jnp.zeros((8, CH), F32)
     for f in range(2):
@@ -527,14 +550,15 @@
 
     c1, c2, near, far = gather_rows(pos, own, below, above, across, bias)
     c0, c3 = trade(near, far)
-    acc = inner(c1, c2, w9, "forward_inner")
-    pre, s0, s1, near, far = forward(pos, c0, c3, acc, w9, bias, head)
+    acc = add_near(pos, c0, inner(c1, c2, w9, "forward_inner"), w9, "forward_near")
+    pre, s0, s1, near, far = forward(pos, c3, acc, w9, bias, head)
     near, far = trade(near, far)
     acc = inner(s0, s1, turned, "transposed_inner")
-    i1, i2, edge, rim = transposed(pos, near, far, acc, turned)
-    turn_c = turn_clips(pos, (c0, c1, c2, c3))
+    acc, turn_c = add_near_turn(pos, near, acc, turned, (c0, c1, c2, c3))
+    i1, i2, edge, rim = transposed(pos, far, acc, turned)
     i0, i3 = trade(edge, rim)
     inside = inner(i1, i2, w9, "backward_inner")
+    inside = add_near(pos, i0, inside, w9, "backward_near")
     sent, kept = backward(pos, (i0, i1, i2, i3), inside, turn_c, (s0, s1), pre, w9, head)
     coded = encode_terms(kept, permute(sent, swap_core))
     pieces = lax.all_to_all(coded, PLANE, 0, 0, tiled=True)

time: 144 us -> 142 us (0.986)
  waiting for transfers between devices: 35.6 us -> 32.6 us
  Pallas kernels: 25.2 us -> 26.9 us
    pallas_call x1 -> x3, Pallas kernels: 1.08 us -> 4.08 us  [the longest x2 2.46 us: add_near(): pl.pallas_call(near_kernel, out_shape=jax.ShapeDtypeStruct((2, ROWS, COLS...]
    ppermute x3, waiting for transfers between devices: 10.2 us -> 7.3 us  [trade_far(): return lax.ppermute(value, CHAIN, pairs)]
  transfers between devices with their start and end apart: 18 -> 18, of which waited for: 12 -> 12; matrix products, arithmetic and copies ran while one was open for 0% -> 0% of each run, Pallas kernels for 7% -> 9%
where the time goes in v6:
time: 142 us
  blocking collectives  40.9 us (29%)
  starting transfers between devices  33.6 us (24%)
  waiting for transfers between devices  32.6 us (23%)
  Pallas kernels  26.9 us (19%)
  local copies, waits for them, and re-layouts  6.66 us (5%)
    all_to_all x1, blocking collectives, per_device(): pieces = lax.all_to_all(coded, PLANE, 0, 0, tiled=True)  29.9 us
    ppermute x15, waiting for transfers between devices, permute(): return lax.ppermute(value, ALL, moved(fn))  25.3 us
    ppermute x15, starting transfers between devices, permute(): return lax.ppermute(value, ALL, moved(fn))  21.5 us
    ppermute x3, starting transfers between devices, trade_far(): return lax.ppermute(value, CHAIN, pairs)  12.1 us
    all_to_all x1, blocking collectives, per_device(): line = lax.all_to_all(recode(pieces), 'z', 0, 0, tiled=True)  11 us
    ppermute x3, waiting for transfers between devices, trade_far(): return lax.ppermute(value, CHAIN, pairs)  7.3 us
    pallas_call x3, Pallas kernels, inner(): pl.pallas_call(inner_kernel, out_shape=jax.ShapeDtypeStruct((2, ROWS, COL...  6.67 us
    unnamed x12, local copies, waits for them, and re-layouts  6.05 us
  transfers between devices with their start and end apart: 18, of which 12 were waited for; matrix products, arithmetic and copies ran while one was open for 0% of the time, Pallas kernels for 9%

profile of v6, /device:TPU:1, one launch (start us, length us, event | category | flops | bytes accessed | tf_op | source)
XLA Modules:
  0.0 141.9 jit_solution(16418139070029937328)
XLA Ops:
  0.6 3.6 %collective-permute-start.2 = (bf16[2,128,256]{2,1,0:T(8,128)(2,1)}, bf16[2,128,256]{2,1,0:T(8,128)(2,1)}, u32[]{:S(2)}, u32[]{:S(2)}) collective-permute-start(bf16[2,128,256]{2,1,0:T(8,128)(2,1)} %bitcast.33), channel_id=1, source_target_pairs={{0,2},{1,3},{2,0},{3,1},{4,6},{5,7},{6,4},{7,5},{8,10},{9,11},{10,... | collective-permute-start | bytes 393224 | tf_op jit(solution)/shard_map/ppermute | solution.py:43
  4.3 0.9 collective-permute-start.1
  5.1 0.6 collective-permute-start
  5.7 0.0 copy-start.3
  5.7 2.0 %copy-done.3 = bf16[3,3,3,256,256]{4,3,2,1,0:T(8,128)(2,1)S(1)} copy-done((bf16[3,3,3,256,256]{4,3,2,1,0:T(8,128)(2,1)S(1)}, bf16[3,3,3,256,256]{4,3,2,1,0:T(8,128)(2,1)}, u32[]{:S(2)}) %copy-start.3) | copy-done | bytes 3538968
  7.8 0.7 copy-done.4
  8.4 0.7 copy-done.5
  9.1 1.7 %turn_weights.1 = (bf16[3,3,3,256,256]{4,3,2,1,0:T(8,128)(2,1)S(1)}, bf16[3,3,3,256,256]{4,3,2,1,0:T(8,128)(2,1)S(1)}, f32[1,256]{1,0:T(1,128)S(1)}, f32[1,256]{1,0:T(1,128)S(1)}) custom-call(bf16[3,3,3,256,256]{4,3,2,1,0:T(8,128)(2,1)S(1)} %copy-done.3, f32[1,256]{1,0:T(1,128)S(1)} %bitcast.37, f32[1,256]{1,0:T(1,128)S(1)} %bitcast.38), custom_call_target="tpu_custom_call" | custom-call | flops 2000000000 | bytes 11534336 | tf_op jit(solution)/shard_map/turn_weights/pallas_call | solution.py:215
  10.8 0.0 copy-start
  10.8 1.8 %copy-done = bf16[3,3,3,256,256]{4,3,2,1,0:T(8,128)(2,1)} copy-done((bf16[3,3,3,256,256]{4,3,2,1,0:T(8,128)(2,1)}, bf16[3,3,3,256,256]{4,3,2,1,0:T(8,128)(2,1)S(1)}, u32[]{:S(2)}) %copy-start) | copy-done | bytes 3538968
  12.6 0.1 pad_add_fusion.pos_ref.pos
  12.6 0.0 collective-permute-done.2.across
  12.7 0.0 collective-permute-done.1.above
  12.7 0.2 collective-permute-done.below
  12.8 0.9 copy-done.2
  13.7 1.1 gather_rows.1
  14.9 1.4 %collective-permute-start.4 = (bf16[4,128,256]{2,1,0:T(8,128)(2,1)S(1)}, bf16[4,128,256]{2,1,0:T(8,128)(2,1)S(1)}, u32[]{:S(2)}, u32[]{:S(2)}) collective-permute-start(bf16[4,128,256]{2,1,0:T(8,128)(2,1)S(1)} %get-tuple-element.28), channel_id=1, source_target_pairs={{0,4},{1,5},{2,6},{3,7},{4,0},{5,1},{6,2},{7,3},{8,12},{9,13},{10,... | collective-permute-start | bytes 786440 | tf_op jit(solution)/shard_map/ppermute | solution.py:43
  16.3 3.1 %collective-permute-start.3 = (bf16[4,128,256]{2,1,0:T(8,128)(2,1)S(1)}, bf16[4,128,256]{2,1,0:T(8,128)(2,1)S(1)}, u32[]{:S(2)}, u32[]{:S(2)}) collective-permute-start(bf16[4,128,256]{2,1,0:T(8,128)(2,1)S(1)} %get-tuple-element.27), channel_id=1, source_target_pairs={{4,8},{8,4},{12,16},{16,12},{20,24},{24,20},{28,32},{32,28},{36,40... | collective-permute-start | bytes 786440 | tf_op jit(solution)/shard_map/ppermute | solution.py:66
  19.4 2.2 %forward_inner.1.acc = f32[2,4,128,256]{3,2,1,0:T(8,128)S(1)} custom-call(bf16[4,128,256]{2,1,0:T(8,128)(2,1)S(1)} %get-tuple-element.29.first.c1, bf16[4,128,256]{2,1,0:T(8,128)(2,1)S(1)} %get-tuple-element.30.second.c2, bf16[3,3,768,256]{3,2,1,0:T(8,128)(2,1)S(1)} %bitcast.22), custom_call_target="tpu_custom_call" | custom-call | flops 2415919104 | bytes 6291456 | tf_op jit(solution)/shard_map/forward_inner/pallas_call | solution.py:237
  21.6 0.0 collective-permute-done.4.near.c0
  21.6 1.2 forward_near.1.acc
  22.9 2.6 %collective-permute-done.3.far.c3 = bf16[4,128,256]{2,1,0:T(8,128)(2,1)S(1)} collective-permute-done((bf16[4,128,256]{2,1,0:T(8,128)(2,1)S(1)}, bf16[4,128,256]{2,1,0:T(8,128)(2,1)S(1)}, u32[]{:S(2)}, u32[]{:S(2)}) %collective-permute-start.3) | collective-permute-done | bytes 262176 | tf_op jit(solution)/shard_map/ppermute | solution.py:66
  25.5 1.7 %forward.1 = (f32[2,4,128,256]{3,2,1,0:T(8,128)S(1)}, bf16[4,128,256]{2,1,0:T(8,128)(2,1)S(1)}, bf16[4,128,256]{2,1,0:T(8,128)(2,1)S(1)}, bf16[4,128,256]{2,1,0:T(8,128)(2,1)S(1)}, bf16[4,128,256]{2,1,0:T(8,128)(2,1)S(1)}) custom-call(s32[3]{0:T(128)S(1)} %pad_add_fusion.pos_ref.pos, bf16[4,128,256]{2,1,0:T(8,128)(2,1)S(1)} %collective-permute-done.3.far.c3, ...), custom_call_target="tpu_custom_call" | custom-call | flops 1207959552 | bytes 6291456 | tf_op jit(solution)/shard_map/forward/pallas_call | solution.py:250
  27.2 0.1 collective-permute-start.6
  27.3 4.4 %collective-permute-start.5 = (bf16[4,128,256]{2,1,0:T(8,128)(2,1)S(1)}, bf16[4,128,256]{2,1,0:T(8,128)(2,1)S(1)}, u32[]{:S(2)}, u32[]{:S(2)}) collective-permute-start(bf16[4,128,256]{2,1,0:T(8,128)(2,1)S(1)} %get-tuple-element.33), channel_id=1, source_target_pairs={{4,8},{8,4},{12,16},{16,12},{20,24},{24,20},{28,32},{32,28},{36,40... | collective-permute-start | bytes 786440 | tf_op jit(solution)/shard_map/ppermute | solution.py:66
  31.7 0.0 copy-done.1
  31.7 2.2 %transposed_inner.1.acc = f32[2,4,128,256]{3,2,1,0:T(8,128)S(1)} custom-call(bf16[4,128,256]{2,1,0:T(8,128)(2,1)S(1)} %get-tuple-element.35.first.s0, bf16[4,128,256]{2,1,0:T(8,128)(2,1)S(1)} %get-tuple-element.36.second.s1, bf16[3,3,768,256]{3,2,1,0:T(8,128)(2,1)S(1)} %bitcast.28), custom_call_target="tpu_custom_call" | custom-call | flops 2415919104 | bytes 6291456 | tf_op jit(solution)/shard_map/transposed_inner/pallas_call | solution.py:237
  33.9 0.0 collective-permute-done.6.near
  33.9 1.6 %transposed_near.1 = (f32[2,4,128,256]{3,2,1,0:T(8,128)S(1)}, bf16[192,2048]{1,0:T(8,128)(2,1)S(1)}) custom-call(s32[3]{0:T(128)S(1)} %pad_add_fusion.pos_ref.pos, bf16[4,128,256]{2,1,0:T(8,128)(2,1)S(1)} %collective-permute-done.6.near, f32[2,4,128,256]{3,2,1,0:T(8,128)S(1)} %transposed_inner.1.acc, bf16[3,3,768,256]{3,2,1,0:T(8,128)(2,1)S(1)} %bitcast.29, ...), custom_call_target="tpu_custom_call" | custom-call | flops 905969664 | bytes 6291456 | tf_op jit(solution)/shard_map/transposed_near/pallas_call | solution.py:313
  35.6 2.2 %collective-permute-done.5.far = bf16[4,128,256]{2,1,0:T(8,128)(2,1)S(1)} collective-permute-done((bf16[4,128,256]{2,1,0:T(8,128)(2,1)S(1)}, bf16[4,128,256]{2,1,0:T(8,128)(2,1)S(1)}, u32[]{:S(2)}, u32[]{:S(2)}) %collective-permute-start.5) | collective-permute-done | bytes 262176 | tf_op jit(solution)/shard_map/ppermute | solution.py:66
  37.8 1.3 transposed.1
  39.1 0.1 collective-permute-start.7
  39.2 4.6 %collective-permute-start.8 = (bf16[4,128,256]{2,1,0:T(8,128)(2,1)S(1)}, bf16[4,128,256]{2,1,0:T(8,128)(2,1)S(1)}, u32[]{:S(2)}, u32[]{:S(2)}) collective-permute-start(bf16[4,128,256]{2,1,0:T(8,128)(2,1)S(1)} %get-tuple-element.42), channel_id=1, source_target_pairs={{4,8},{8,4},{12,16},{16,12},{20,24},{24,20},{28,32},{32,28},{36,40... | collective-permute-start | bytes 786440 | tf_op jit(solution)/shard_map/ppermute | solution.py:66
  43.8 2.2 %backward_inner.1.acc = f32[2,4,128,256]{3,2,1,0:T(8,128)S(1)} custom-call(bf16[4,128,256]{2,1,0:T(8,128)(2,1)S(1)} %get-tuple-element.40.first.i1, bf16[4,128,256]{2,1,0:T(8,128)(2,1)S(1)} %get-tuple-element.41.second.i2, bf16[3,3,768,256]{3,2,1,0:T(8,128)(2,1)S(1)} %bitcast.25), custom_call_target="tpu_custom_call" | custom-call | flops 2415919104 | bytes 6291456 | tf_op jit(solution)/shard_map/backward_inner/pallas_call | solution.py:237
  46.0 0.0 collective-permute-done.7.near.i0
  46.0 1.2 backward_near.1.inside
  47.3 2.4 %collective-permute-done.8.i3 = bf16[4,128,256]{2,1,0:T(8,128)(2,1)S(1)} collective-permute-done((bf16[4,128,256]{2,1,0:T(8,128)(2,1)S(1)}, bf16[4,128,256]{2,1,0:T(8,128)(2,1)S(1)}, u32[]{:S(2)}, u32[]{:S(2)}) %collective-permute-start.8) | collective-permute-done | bytes 262176 | tf_op jit(solution)/shard_map/ppermute | solution.py:66
  49.7 4.3 %backward.1 = (f32[224,8,128]{2,1,0:T(8,128)S(1)}, f32[224,8,128]{2,1,0:T(8,128)S(1)}) custom-call(s32[3]{0:T(128)S(1)} %pad_add_fusion.pos_ref.pos, bf16[4,128,256]{2,1,0:T(8,128)(2,1)S(1)} %collective-permute-done.7.near.i0, bf16[4,128,256]{2,1,0:T(8,128)(2,1)S(1)} %get-tuple-element.40.first.i1, bf16[4,128,256]{2,1,0:T(8,128)(2,1)S(1)} %get-tuple-element.41.second.i2, ...), custom_call_target="tpu_custom_call" | custom-call | flops 5798205952 | bytes 10485760 | tf_op jit(solution)/shard_map/backward/pallas_call | solution.py:401
  54.0 0.1 collective-permute-start.9
  54.1 2.5 %collective-permute-done.9.received = f32[224,8,128]{2,1,0:T(8,128)S(1)} collective-permute-done((f32[224,8,128]{2,1,0:T(8,128)S(1)}, f32[224,8,128]{2,1,0:T(8,128)S(1)}, u32[]{:S(2)}, u32[]{:S(2)}) %collective-permute-start.9) | collective-permute-done | bytes 917536 | tf_op jit(solution)/shard_map/ppermute | solution.py:43
  56.6 0.8 encode_terms.1
  57.4 29.9 %all_to_all.10.pieces = bf16[32,64,128]{2,1,0:T(8,128)(2,1)S(1)} all-to-all(bf16[32,64,128]{2,1,0:T(8,128)(2,1)S(1)} %encode_terms.1), channel_id=1, replica_groups=mesh['yh'=2,'z'=8,'yl'=2,'c'=2,'x'=4] {'yh','z','yl'}, dimensions={0} | all-to-all | bytes 1048576 | tf_op jit(solution)/shard_map/all_to_all | solution.py:564
  87.3 0.4 recode.1
  87.7 11.0 %all_to_all.11 = bf16[8,64,128]{2,1,0:T(8,128)(2,1)S(1)} all-to-all(bf16[8,64,128]{2,1,0:T(8,128)(2,1)S(1)} %recode.1), channel_id=1, replica_groups=mesh['yh'=2,'z'=8,'yl'=2,'c'=2,'x'=4] {'z'}, dimensions={0} | all-to-all | bytes 262144 | tf_op jit(solution)/shard_map/all_to_all | solution.py:565
  98.7 0.6 collective-permute-start.12
  99.3 2.1 %collective-permute-start.11 = (bf16[8,64,128]{2,1,0:T(8,128)(2,1)S(1)}, bf16[8,64,128]{2,1,0:T(8,128)(2,1)S(1)}, u32[]{:S(2)}, u32[]{:S(2)}) collective-permute-start(bf16[8,64,128]{2,1,0:T(8,128)(2,1)S(1)} %all_to_all.11), channel_id=1, source_target_pairs={{0,136},{1,137},{2,138},{3,139},{4,7},{5,4},{6,5},{7,6},{8,0},{9,1... | collective-permute-start | bytes 393224 | tf_op jit(solution)/shard_map/ppermute | solution.py:43
  101.4 0.0 collective-permute-start.10
  101.4 2.6 %collective-permute-done.12 = bf16[8,64,128]{2,1,0:T(8,128)(2,1)S(1)} collective-permute-done((bf16[8,64,128]{2,1,0:T(8,128)(2,1)S(1)}, bf16[8,64,128]{2,1,0:T(8,128)(2,1)S(1)}, u32[]{:S(2)}, u32[]{:S(2)}) %collective-permute-start.12) | collective-permute-done | bytes 131104 | tf_op jit(solution)/shard_map/ppermute | solution.py:43
  104.0 1.1 collective-permute-done.11
  105.1 1.6 %collective-permute-done.10 = bf16[8,64,128]{2,1,0:T(8,128)(2,1)S(1)} collective-permute-done((bf16[8,64,128]{2,1,0:T(8,128)(2,1)S(1)}, bf16[8,64,128]{2,1,0:T(8,128)(2,1)S(1)}, u32[]{:S(2)}, u32[]{:S(2)}) %collective-permute-start.10) | collective-permute-done | bytes 131104 | tf_op jit(solution)/shard_map/ppermute | solution.py:43
  106.7 0.1 pad_maximum_fusion.1
  106.8 0.6 collective-permute-start.14
  107.4 0.9 collective-permute-start.13
  108.3 6.9 %collective-permute-done.14 = bf16[32,64,128]{2,1,0:T(8,128)(2,1)S(1)} collective-permute-done((bf16[32,64,128]{2,1,0:T(8,128)(2,1)S(1)}, bf16[32,64,128]{2,1,0:T(8,128)(2,1)S(1)}, u32[]{:S(2)}, u32[]{:S(2)}) %collective-permute-start.14) | collective-permute-done | bytes 524320 | tf_op jit(solution)/shard_map/ppermute | solution.py:43
  115.2 1.5 %collective-permute-start.16 = (bf16[16,64,128]{2,1,0:T(8,128)(2,1)S(1)}, bf16[16,64,128]{2,1,0:T(8,128)(2,1)S(1)}, u32[]{:S(2)}, u32[]{:S(2)}) collective-permute-start(bf16[16,64,128]{2,1,0:T(8,128)(2,1)S(1)} %slice.17), channel_id=1, source_target_pairs={{0,3},{1,0},{2,1},{3,2},{4,140},{5,141},{6,142},{7,143},{8,11},{9,... | collective-permute-start | bytes 786440 | tf_op jit(solution)/shard_map/ppermute | solution.py:43
  116.7 0.0 collective-permute-done.13
  116.8 0.1 collective-permute-start.15
  116.9 3.9 %collective-permute-done.16 = bf16[16,64,128]{2,1,0:T(8,128)(2,1)S(1)} collective-permute-done((bf16[16,64,128]{2,1,0:T(8,128)(2,1)S(1)}, bf16[16,64,128]{2,1,0:T(8,128)(2,1)S(1)}, u32[]{:S(2)}, u32[]{:S(2)}) %collective-permute-start.16) | collective-permute-done | bytes 262176 | tf_op jit(solution)/shard_map/ppermute | solution.py:43
  120.8 2.8 %collective-permute-done.15 = bf16[16,64,128]{2,1,0:T(8,128)(2,1)S(1)} collective-permute-done((bf16[16,64,128]{2,1,0:T(8,128)(2,1)S(1)}, bf16[16,64,128]{2,1,0:T(8,128)(2,1)S(1)}, u32[]{:S(2)}, u32[]{:S(2)}) %collective-permute-start.15) | collective-permute-done | bytes 262176 | tf_op jit(solution)/shard_map/ppermute | solution.py:43
  123.6 0.3 pad_maximum_fusion
  123.9 8.8 %collective-permute-start.17 = (bf16[16,8,64,128]{3,2,1,0:T(8,128)(2,1)S(1)}, bf16[16,8,64,128]{3,2,1,0:T(8,128)(2,1)S(1)}, u32[]{:S(2)}, u32[]{:S(2)}) collective-permute-start(bf16[16,8,64,128]{3,2,1,0:T(8,128)(2,1)S(1)} %bitcast.31), channel_id=1, source_target_pairs={{0,4},{1,5},{2,6},{3,7},{4,0},{5,1},{6,2},{7,3},{8,12},{9,13},{10,... | collective-permute-start | bytes 6291464 | tf_op jit(solution)/shard_map/ppermute | solution.py:43
  132.7 3.8 %collective-permute-done.17.other = bf16[16,8,64,128]{3,2,1,0:T(8,128)(2,1)S(1)} collective-permute-done((bf16[16,8,64,128]{3,2,1,0:T(8,128)(2,1)S(1)}, bf16[16,8,64,128]{3,2,1,0:T(8,128)(2,1)S(1)}, u32[]{:S(2)}, u32[]{:S(2)}) %collective-permute-start.17) | collective-permute-done | bytes 2097184 | tf_op jit(solution)/shard_map/ppermute | solution.py:43
  136.5 4.8 %assemble.1 = (f32[27,4,8,8,256]{4,3,2,1,0:T(8,128)}, f32[16,256]{1,0:T(8,128)S(1)}) custom-call(s32[3]{0:T(128)S(1)} %pad_add_fusion.pos_ref.pos, bf16[16,8,64,128]{3,2,1,0:T(8,128)(2,1)S(1)} %bitcast.32, bf16[16,8,64,128]{3,2,1,0:T(8,128)(2,1)S(1)} %collective-permute-done.17.other), custom_call_target="tpu_custom_call" | custom-call | flops 1000000 | bytes 15728640 | tf_op jit(solution)/shard_map/assemble/pallas_call | solution.py:508
  141.3 0.6 fusion
  (7 shorter events, 0.1 us)
Async XLA Ops:
  0.6 12.0 %collective-permute-start.2 = (bf16[2,128,256]{2,1,0:T(8,128)(2,1)}, bf16[2,128,256]{2,1,0:T(8,128)(2,1)}, u32[]{:S(2)}, u32[]{:S(2)}) collective-permute-start(bf16[2,128,256]{2,1,0:T(8,128)(2,1)} %bitcast.33), channel_id=1, source_target_pairs={{0,2},{1,3},{2,0},{3,1},{4,6},{5,7},{6,4},{7,5},{8,10},{9,11},{10,... | collective-permute-start | bytes 393224 | tf_op jit(solution)/shard_map/ppermute | solution.py:43
  4.3 8.4 %collective-permute-start.1 = (bf16[2,128,256]{2,1,0:T(8,128)(2,1)}, bf16[2,128,256]{2,1,0:T(8,128)(2,1)}, u32[]{:S(2)}, u32[]{:S(2)}) collective-permute-start(bf16[2,128,256]{2,1,0:T(8,128)(2,1)} %bitcast.34), channel_id=1, source_target_pairs={{0,3},{1,0},{2,1},{3,2},{4,7},{5,4},{6,5},{7,6},{8,11},{9,8},{10,9... | collective-permute-start | bytes 393224 | tf_op jit(solution)/shard_map/ppermute | solution.py:43
  5.1 7.7 %collective-permute-start = (bf16[2,128,256]{2,1,0:T(8,128)(2,1)}, bf16[2,128,256]{2,1,0:T(8,128)(2,1)}, u32[]{:S(2)}, u32[]{:S(2)}) collective-permute-start(bf16[2,128,256]{2,1,0:T(8,128)(2,1)} %bitcast.35), channel_id=1, source_target_pairs={{0,1},{1,2},{2,3},{3,0},{4,5},{5,6},{6,7},{7,4},{8,9},{9,10},{10,1... | collective-permute-start | bytes 393224 | tf_op jit(solution)/shard_map/ppermute | solution.py:43
  5.7 2.0 %copy-start.3 = (bf16[3,3,3,256,256]{4,3,2,1,0:T(8,128)(2,1)S(1)}, bf16[3,3,3,256,256]{4,3,2,1,0:T(8,128)(2,1)}, u32[]{:S(2)}) copy-start(bf16[3,3,3,256,256]{4,3,2,1,0:T(8,128)(2,1)} %weight.1) | copy-start | bytes 10616836
  7.7 0.7 copy-start.4
  8.4 0.7 copy-start.5
  10.8 1.8 %copy-start = (bf16[3,3,3,256,256]{4,3,2,1,0:T(8,128)(2,1)}, bf16[3,3,3,256,256]{4,3,2,1,0:T(8,128)(2,1)S(1)}, u32[]{:S(2)}) copy-start(bf16[3,3,3,256,256]{4,3,2,1,0:T(8,128)(2,1)S(1)} %get-tuple-element.37) | copy-start | bytes 10616836
  12.8 0.9 copy-start.2
  14.9 6.8 %collective-permute-start.4 = (bf16[4,128,256]{2,1,0:T(8,128)(2,1)S(1)}, bf16[4,128,256]{2,1,0:T(8,128)(2,1)S(1)}, u32[]{:S(2)}, u32[]{:S(2)}) collective-permute-start(bf16[4,128,256]{2,1,0:T(8,128)(2,1)S(1)} %get-tuple-element.28), channel_id=1, source_target_pairs={{0,4},{1,5},{2,6},{3,7},{4,0},{5,1},{6,2},{7,3},{8,12},{9,13},{10,... | collective-permute-start | bytes 786440 | tf_op jit(solution)/shard_map/ppermute | solution.py:43
  16.3 9.2 %collective-permute-start.3 = (bf16[4,128,256]{2,1,0:T(8,128)(2,1)S(1)}, bf16[4,128,256]{2,1,0:T(8,128)(2,1)S(1)}, u32[]{:S(2)}, u32[]{:S(2)}) collective-permute-start(bf16[4,128,256]{2,1,0:T(8,128)(2,1)S(1)} %get-tuple-element.27), channel_id=1, source_target_pairs={{4,8},{8,4},{12,16},{16,12},{20,24},{24,20},{28,32},{32,28},{36,40... | collective-permute-start | bytes 786440 | tf_op jit(solution)/shard_map/ppermute | solution.py:66
  25.5 6.2 %copy-start.1 = (bf16[3,3,3,256,256]{4,3,2,1,0:T(8,128)(2,1)S(1)}, bf16[3,3,3,256,256]{4,3,2,1,0:T(8,128)(2,1)}, u32[]{:S(2)}) copy-start(bf16[3,3,3,256,256]{4,3,2,1,0:T(8,128)(2,1)} %copy-done) | copy-start | bytes 10616836
  27.2 6.8 %collective-permute-start.6 = (bf16[4,128,256]{2,1,0:T(8,128)(2,1)S(1)}, bf16[4,128,256]{2,1,0:T(8,128)(2,1)S(1)}, u32[]{:S(2)}, u32[]{:S(2)}) collective-permute-start(bf16[4,128,256]{2,1,0:T(8,128)(2,1)S(1)} %get-tuple-element.34), channel_id=1, source_target_pairs={{0,4},{1,5},{2,6},{3,7},{4,0},{5,1},{6,2},{7,3},{8,12},{9,13},{10,... | collective-permute-start | bytes 786440 | tf_op jit(solution)/shard_map/ppermute | solution.py:43
  27.3 10.5 %collective-permute-start.5 = (bf16[4,128,256]{2,1,0:T(8,128)(2,1)S(1)}, bf16[4,128,256]{2,1,0:T(8,128)(2,1)S(1)}, u32[]{:S(2)}, u32[]{:S(2)}) collective-permute-start(bf16[4,128,256]{2,1,0:T(8,128)(2,1)S(1)} %get-tuple-element.33), channel_id=1, source_target_pairs={{4,8},{8,4},{12,16},{16,12},{20,24},{24,20},{28,32},{32,28},{36,40... | collective-permute-start | bytes 786440 | tf_op jit(solution)/shard_map/ppermute | solution.py:66
  39.1 6.9 %collective-permute-start.7 = (bf16[4,128,256]{2,1,0:T(8,128)(2,1)S(1)}, bf16[4,128,256]{2,1,0:T(8,128)(2,1)S(1)}, u32[]{:S(2)}, u32[]{:S(2)}) collective-permute-start(bf16[4,128,256]{2,1,0:T(8,128)(2,1)S(1)} %get-tuple-element.39), channel_id=1, source_target_pairs={{0,4},{1,5},{2,6},{3,7},{4,0},{5,1},{6,2},{7,3},{8,12},{9,13},{10,... | collective-permute-start | bytes 786440 | tf_op jit(solution)/shard_map/ppermute | solution.py:43
  39.2 10.5 %collective-permute-start.8 = (bf16[4,128,256]{2,1,0:T(8,128)(2,1)S(1)}, bf16[4,128,256]{2,1,0:T(8,128)(2,1)S(1)}, u32[]{:S(2)}, u32[]{:S(2)}) collective-permute-start(bf16[4,128,256]{2,1,0:T(8,128)(2,1)S(1)} %get-tuple-element.42), channel_id=1, source_target_pairs={{4,8},{8,4},{12,16},{16,12},{20,24},{24,20},{28,32},{32,28},{36,40... | collective-permute-start | bytes 786440 | tf_op jit(solution)/shard_map/ppermute | solution.py:66
  54.0 2.6 %collective-permute-start.9 = (f32[224,8,128]{2,1,0:T(8,128)S(1)}, f32[224,8,128]{2,1,0:T(8,128)S(1)}, u32[]{:S(2)}, u32[]{:S(2)}) collective-permute-start(f32[224,8,128]{2,1,0:T(8,128)S(1)} %get-tuple-element.46), channel_id=1, source_target_pairs={{0,4},{1,5},{2,6},{3,7},{4,0},{5,1},{6,2},{7,3},{8,12},{9,13},{10,... | collective-permute-start | bytes 2752520 | tf_op jit(solution)/shard_map/ppermute | solution.py:43
  98.7 5.3 %collective-permute-start.12 = (bf16[8,64,128]{2,1,0:T(8,128)(2,1)S(1)}, bf16[8,64,128]{2,1,0:T(8,128)(2,1)S(1)}, u32[]{:S(2)}, u32[]{:S(2)}) collective-permute-start(bf16[8,64,128]{2,1,0:T(8,128)(2,1)S(1)} %all_to_all.11), channel_id=1, source_target_pairs={{0,128},{1,129},{2,130},{3,131},{4,6},{5,7},{6,4},{7,5},{8,136},{9... | collective-permute-start | bytes 393224 | tf_op jit(solution)/shard_map/ppermute | solution.py:43
  99.3 5.8 %collective-permute-start.11 = (bf16[8,64,128]{2,1,0:T(8,128)(2,1)S(1)}, bf16[8,64,128]{2,1,0:T(8,128)(2,1)S(1)}, u32[]{:S(2)}, u32[]{:S(2)}) collective-permute-start(bf16[8,64,128]{2,1,0:T(8,128)(2,1)S(1)} %all_to_all.11), channel_id=1, source_target_pairs={{0,136},{1,137},{2,138},{3,139},{4,7},{5,4},{6,5},{7,6},{8,0},{9,1... | collective-permute-start | bytes 393224 | tf_op jit(solution)/shard_map/ppermute | solution.py:43
  101.4 5.3 %collective-permute-start.10 = (bf16[8,64,128]{2,1,0:T(8,128)(2,1)S(1)}, bf16[8,64,128]{2,1,0:T(8,128)(2,1)S(1)}, u32[]{:S(2)}, u32[]{:S(2)}) collective-permute-start(bf16[8,64,128]{2,1,0:T(8,128)(2,1)S(1)} %all_to_all.11), channel_id=1, source_target_pairs={{0,8},{1,9},{2,10},{3,11},{4,5},{5,6},{6,7},{7,4},{8,128},{9,129},... | collective-permute-start | bytes 393224 | tf_op jit(solution)/shard_map/ppermute | solution.py:43
  106.8 8.4 %collective-permute-start.14 = (bf16[32,64,128]{2,1,0:T(8,128)(2,1)S(1)}, bf16[32,64,128]{2,1,0:T(8,128)(2,1)S(1)}, u32[]{:S(2)}, u32[]{:S(2)}) collective-permute-start(bf16[32,64,128]{2,1,0:T(8,128)(2,1)S(1)} %bitcast.39), channel_id=1, source_target_pairs={{0,3},{1,0},{2,1},{3,2},{4,140},{5,141},{6,142},{7,143},{8,11},{9,... | collective-permute-start | bytes 1572872 | tf_op jit(solution)/shard_map/ppermute | solution.py:43
  107.4 9.3 %collective-permute-start.13 = (bf16[32,64,128]{2,1,0:T(8,128)(2,1)S(1)}, bf16[32,64,128]{2,1,0:T(8,128)(2,1)S(1)}, u32[]{:S(2)}, u32[]{:S(2)}) collective-permute-start(bf16[32,64,128]{2,1,0:T(8,128)(2,1)S(1)} %bitcast.40), channel_id=1, source_target_pairs={{0,1},{1,2},{2,3},{3,0},{4,12},{5,13},{6,14},{7,15},{8,9},{9,10},{... | collective-permute-start | bytes 1572872 | tf_op jit(solution)/shard_map/ppermute | solution.py:43
  115.2 5.6 %collective-permute-start.16 = (bf16[16,64,128]{2,1,0:T(8,128)(2,1)S(1)}, bf16[16,64,128]{2,1,0:T(8,128)(2,1)S(1)}, u32[]{:S(2)}, u32[]{:S(2)}) collective-permute-start(bf16[16,64,128]{2,1,0:T(8,128)(2,1)S(1)} %slice.17), channel_id=1, source_target_pairs={{0,3},{1,0},{2,1},{3,2},{4,140},{5,141},{6,142},{7,143},{8,11},{9,... | collective-permute-start | bytes 786440 | tf_op jit(solution)/shard_map/ppermute | solution.py:43
  116.8 6.8 %collective-permute-start.15 = (bf16[16,64,128]{2,1,0:T(8,128)(2,1)S(1)}, bf16[16,64,128]{2,1,0:T(8,128)(2,1)S(1)}, u32[]{:S(2)}, u32[]{:S(2)}) collective-permute-start(bf16[16,64,128]{2,1,0:T(8,128)(2,1)S(1)} %slice.16), channel_id=1, source_target_pairs={{0,1},{1,2},{2,3},{3,0},{4,12},{5,13},{6,14},{7,15},{8,9},{9,10},{... | collective-permute-start | bytes 786440 | tf_op jit(solution)/shard_map/ppermute | solution.py:43
  123.9 12.6 %collective-permute-start.17 = (bf16[16,8,64,128]{3,2,1,0:T(8,128)(2,1)S(1)}, bf16[16,8,64,128]{3,2,1,0:T(8,128)(2,1)S(1)}, u32[]{:S(2)}, u32[]{:S(2)}) collective-permute-start(bf16[16,8,64,128]{3,2,1,0:T(8,128)(2,1)S(1)} %bitcast.31), channel_id=1, source_target_pairs={{0,4},{1,5},{2,6},{3,7},{4,0},{5,1},{6,2},{7,3},{8,12},{9,13},{10,... | collective-permute-start | bytes 6291464 | tf_op jit(solution)/shard_map/ppermute | solution.py:43

commit v7 on v6

--- a/solution.py
+++ b/solution.py
@@ -52,11 +52,11 @@
 
 
 def split_first(step):
+    return lambda y, z, c, x: (y + step, z, c, x) if c else (y, z, c, x + step)
+
+
+def split_second(step):
     return lambda y, z, c, x: (y, z, c, x + step) if c else (y + step, z, c, x)
-
-
-def split_second(step):
-    return lambda y, z, c, x: (y + step, z, c, x) if c else (y, z, c, x + step)
 
 
 def trade_far(value):
@@ -492,7 +492,7 @@
         lane = pl.ds(pl.multiple_of(held * 128, 128), 128)
         for row in range(4):
             at_y = relative(lax.rem(row - y + 4, 4))
-            place = jnp.where(held == 0, at_x * 4 + at_y, at_y * 4 + at_x)
+            place = jnp.where(held == 1, at_x * 4 + at_y, at_y * 4 + at_x)
             for z in range(8):
                 piece = ((row // 2) * 8 + z) * 2 + row % 2
                 for j, value in enumerate(decode(ref[place, z])):

time: 142 us -> 140 us (0.986)
  transfers between devices with their start and end apart: 18 -> 18, of which waited for: 12 -> 11; matrix products, arithmetic and copies ran while one was open for 0% -> 0% of each run, Pallas kernels for 9% -> 9%
where the time goes in v7:
time: 140 us
  blocking collectives  40.9 us (29%)
  starting transfers between devices  32.6 us (23%)
  waiting for transfers between devices  31.6 us (23%)
  Pallas kernels  26.9 us (19%)
  local copies, waits for them, and re-layouts  6.66 us (5%)
    all_to_all x1, blocking collectives, per_device(): pieces = lax.all_to_all(coded, PLANE, 0, 0, tiled=True)  29.9 us
    ppermute x15, waiting for transfers between devices, permute(): return lax.ppermute(value, ALL, moved(fn))  24.3 us
    ppermute x15, starting transfers between devices, permute(): return lax.ppermute(value, ALL, moved(fn))  20.5 us
    ppermute x3, starting transfers between devices, trade_far(): return lax.ppermute(value, CHAIN, pairs)  12.1 us
    all_to_all x1, blocking collectives, per_device(): line = lax.all_to_all(recode(pieces), 'z', 0, 0, tiled=True)  11 us
    ppermute x3, waiting for transfers between devices, trade_far(): return lax.ppermute(value, CHAIN, pairs)  7.3 us
    pallas_call x3, Pallas kernels, inner(): pl.pallas_call(inner_kernel, out_shape=jax.ShapeDtypeStruct((2, ROWS, COL...  6.67 us
    unnamed x12, local copies, waits for them, and re-layouts  6.05 us
  transfers between devices with their start and end apart: 18, of which 11 were waited for; matrix products, arithmetic and copies ran while one was open for 0% of the time, Pallas kernels for 9%

profile of v7, /device:TPU:1, one launch (start us, length us, event | category | flops | bytes accessed | tf_op | source)
XLA Modules:
  0.0 139.9 jit_solution(1329755707571798051)
XLA Ops:
  0.6 3.6 %collective-permute-start.2 = (bf16[2,128,256]{2,1,0:T(8,128)(2,1)}, bf16[2,128,256]{2,1,0:T(8,128)(2,1)}, u32[]{:S(2)}, u32[]{:S(2)}) collective-permute-start(bf16[2,128,256]{2,1,0:T(8,128)(2,1)} %bitcast.33), channel_id=1, source_target_pairs={{0,2},{1,3},{2,0},{3,1},{4,6},{5,7},{6,4},{7,5},{8,10},{9,11},{10,... | collective-permute-start | bytes 393224 | tf_op jit(solution)/shard_map/ppermute | solution.py:43
  4.3 0.9 collective-permute-start.1
  5.1 0.6 collective-permute-start
  5.7 0.0 copy-start.3
  5.7 2.0 %copy-done.3 = bf16[3,3,3,256,256]{4,3,2,1,0:T(8,128)(2,1)S(1)} copy-done((bf16[3,3,3,256,256]{4,3,2,1,0:T(8,128)(2,1)S(1)}, bf16[3,3,3,256,256]{4,3,2,1,0:T(8,128)(2,1)}, u32[]{:S(2)}) %copy-start.3) | copy-done | bytes 3538968
  7.8 0.7 copy-done.4
  8.4 0.7 copy-done.5
  9.1 1.7 %turn_weights.1 = (bf16[3,3,3,256,256]{4,3,2,1,0:T(8,128)(2,1)S(1)}, bf16[3,3,3,256,256]{4,3,2,1,0:T(8,128)(2,1)S(1)}, f32[1,256]{1,0:T(1,128)S(1)}, f32[1,256]{1,0:T(1,128)S(1)}) custom-call(bf16[3,3,3,256,256]{4,3,2,1,0:T(8,128)(2,1)S(1)} %copy-done.3, f32[1,256]{1,0:T(1,128)S(1)} %bitcast.37, f32[1,256]{1,0:T(1,128)S(1)} %bitcast.38), custom_call_target="tpu_custom_call" | custom-call | flops 2000000000 | bytes 11534336 | tf_op jit(solution)/shard_map/turn_weights/pallas_call | solution.py:215
  10.8 0.0 copy-start
  10.8 1.8 %copy-done = bf16[3,3,3,256,256]{4,3,2,1,0:T(8,128)(2,1)} copy-done((bf16[3,3,3,256,256]{4,3,2,1,0:T(8,128)(2,1)}, bf16[3,3,3,256,256]{4,3,2,1,0:T(8,128)(2,1)S(1)}, u32[]{:S(2)}) %copy-start) | copy-done | bytes 3538968
  12.6 0.1 pad_add_fusion.pos_ref.pos
  12.6 0.0 collective-permute-done.2.across
  12.7 0.0 collective-permute-done.1.above
  12.7 0.2 collective-permute-done.below
  12.8 0.9 copy-done.2
  13.7 1.1 gather_rows.1
  14.9 1.4 %collective-permute-start.4 = (bf16[4,128,256]{2,1,0:T(8,128)(2,1)S(1)}, bf16[4,128,256]{2,1,0:T(8,128)(2,1)S(1)}, u32[]{:S(2)}, u32[]{:S(2)}) collective-permute-start(bf16[4,128,256]{2,1,0:T(8,128)(2,1)S(1)} %get-tuple-element.28), channel_id=1, source_target_pairs={{0,4},{1,5},{2,6},{3,7},{4,0},{5,1},{6,2},{7,3},{8,12},{9,13},{10,... | collective-permute-start | bytes 786440 | tf_op jit(solution)/shard_map/ppermute | solution.py:43
  16.3 3.1 %collective-permute-start.3 = (bf16[4,128,256]{2,1,0:T(8,128)(2,1)S(1)}, bf16[4,128,256]{2,1,0:T(8,128)(2,1)S(1)}, u32[]{:S(2)}, u32[]{:S(2)}) collective-permute-start(bf16[4,128,256]{2,1,0:T(8,128)(2,1)S(1)} %get-tuple-element.27), channel_id=1, source_target_pairs={{4,8},{8,4},{12,16},{16,12},{20,24},{24,20},{28,32},{32,28},{36,40... | collective-permute-start | bytes 786440 | tf_op jit(solution)/shard_map/ppermute | solution.py:66
  19.4 2.2 %forward_inner.1.acc = f32[2,4,128,256]{3,2,1,0:T(8,128)S(1)} custom-call(bf16[4,128,256]{2,1,0:T(8,128)(2,1)S(1)} %get-tuple-element.29.first.c1, bf16[4,128,256]{2,1,0:T(8,128)(2,1)S(1)} %get-tuple-element.30.second.c2, bf16[3,3,768,256]{3,2,1,0:T(8,128)(2,1)S(1)} %bitcast.22), custom_call_target="tpu_custom_call" | custom-call | flops 2415919104 | bytes 6291456 | tf_op jit(solution)/shard_map/forward_inner/pallas_call | solution.py:237
  21.6 0.0 collective-permute-done.4.near.c0
  21.6 1.2 forward_near.1.acc
  22.9 2.6 %collective-permute-done.3.far.c3 = bf16[4,128,256]{2,1,0:T(8,128)(2,1)S(1)} collective-permute-done((bf16[4,128,256]{2,1,0:T(8,128)(2,1)S(1)}, bf16[4,128,256]{2,1,0:T(8,128)(2,1)S(1)}, u32[]{:S(2)}, u32[]{:S(2)}) %collective-permute-start.3) | collective-permute-done | bytes 262176 | tf_op jit(solution)/shard_map/ppermute | solution.py:66
  25.5 1.7 %forward.1 = (f32[2,4,128,256]{3,2,1,0:T(8,128)S(1)}, bf16[4,128,256]{2,1,0:T(8,128)(2,1)S(1)}, bf16[4,128,256]{2,1,0:T(8,128)(2,1)S(1)}, bf16[4,128,256]{2,1,0:T(8,128)(2,1)S(1)}, bf16[4,128,256]{2,1,0:T(8,128)(2,1)S(1)}) custom-call(s32[3]{0:T(128)S(1)} %pad_add_fusion.pos_ref.pos, bf16[4,128,256]{2,1,0:T(8,128)(2,1)S(1)} %collective-permute-done.3.far.c3, ...), custom_call_target="tpu_custom_call" | custom-call | flops 1207959552 | bytes 6291456 | tf_op jit(solution)/shard_map/forward/pallas_call | solution.py:250
  27.2 0.1 collective-permute-start.6
  27.3 4.4 %collective-permute-start.5 = (bf16[4,128,256]{2,1,0:T(8,128)(2,1)S(1)}, bf16[4,128,256]{2,1,0:T(8,128)(2,1)S(1)}, u32[]{:S(2)}, u32[]{:S(2)}) collective-permute-start(bf16[4,128,256]{2,1,0:T(8,128)(2,1)S(1)} %get-tuple-element.33), channel_id=1, source_target_pairs={{4,8},{8,4},{12,16},{16,12},{20,24},{24,20},{28,32},{32,28},{36,40... | collective-permute-start | bytes 786440 | tf_op jit(solution)/shard_map/ppermute | solution.py:66
  31.7 0.0 copy-done.1
  31.7 2.2 %transposed_inner.1.acc = f32[2,4,128,256]{3,2,1,0:T(8,128)S(1)} custom-call(bf16[4,128,256]{2,1,0:T(8,128)(2,1)S(1)} %get-tuple-element.35.first.s0, bf16[4,128,256]{2,1,0:T(8,128)(2,1)S(1)} %get-tuple-element.36.second.s1, bf16[3,3,768,256]{3,2,1,0:T(8,128)(2,1)S(1)} %bitcast.28), custom_call_target="tpu_custom_call" | custom-call | flops 2415919104 | bytes 6291456 | tf_op jit(solution)/shard_map/transposed_inner/pallas_call | solution.py:237
  33.9 0.0 collective-permute-done.6.near
  33.9 1.6 %transposed_near.1 = (f32[2,4,128,256]{3,2,1,0:T(8,128)S(1)}, bf16[192,2048]{1,0:T(8,128)(2,1)S(1)}) custom-call(s32[3]{0:T(128)S(1)} %pad_add_fusion.pos_ref.pos, bf16[4,128,256]{2,1,0:T(8,128)(2,1)S(1)} %collective-permute-done.6.near, f32[2,4,128,256]{3,2,1,0:T(8,128)S(1)} %transposed_inner.1.acc, bf16[3,3,768,256]{3,2,1,0:T(8,128)(2,1)S(1)} %bitcast.29, ...), custom_call_target="tpu_custom_call" | custom-call | flops 905969664 | bytes 6291456 | tf_op jit(solution)/shard_map/transposed_near/pallas_call | solution.py:313
  35.6 2.2 %collective-permute-done.5.far = bf16[4,128,256]{2,1,0:T(8,128)(2,1)S(1)} collective-permute-done((bf16[4,128,256]{2,1,0:T(8,128)(2,1)S(1)}, bf16[4,128,256]{2,1,0:T(8,128)(2,1)S(1)}, u32[]{:S(2)}, u32[]{:S(2)}) %collective-permute-start.5) | collective-permute-done | bytes 262176 | tf_op jit(solution)/shard_map/ppermute | solution.py:66
  37.8 1.3 transposed.1
  39.1 0.1 collective-permute-start.7
  39.2 4.6 %collective-permute-start.8 = (bf16[4,128,256]{2,1,0:T(8,128)(2,1)S(1)}, bf16[4,128,256]{2,1,0:T(8,128)(2,1)S(1)}, u32[]{:S(2)}, u32[]{:S(2)}) collective-permute-start(bf16[4,128,256]{2,1,0:T(8,128)(2,1)S(1)} %get-tuple-element.42), channel_id=1, source_target_pairs={{4,8},{8,4},{12,16},{16,12},{20,24},{24,20},{28,32},{32,28},{36,40... | collective-permute-start | bytes 786440 | tf_op jit(solution)/shard_map/ppermute | solution.py:66
  43.8 2.2 %backward_inner.1.acc = f32[2,4,128,256]{3,2,1,0:T(8,128)S(1)} custom-call(bf16[4,128,256]{2,1,0:T(8,128)(2,1)S(1)} %get-tuple-element.40.first.i1, bf16[4,128,256]{2,1,0:T(8,128)(2,1)S(1)} %get-tuple-element.41.second.i2, bf16[3,3,768,256]{3,2,1,0:T(8,128)(2,1)S(1)} %bitcast.25), custom_call_target="tpu_custom_call" | custom-call | flops 2415919104 | bytes 6291456 | tf_op jit(solution)/shard_map/backward_inner/pallas_call | solution.py:237
  46.0 0.0 collective-permute-done.7.near.i0
  46.0 1.2 backward_near.1.inside
  47.3 2.4 %collective-permute-done.8.i3 = bf16[4,128,256]{2,1,0:T(8,128)(2,1)S(1)} collective-permute-done((bf16[4,128,256]{2,1,0:T(8,128)(2,1)S(1)}, bf16[4,128,256]{2,1,0:T(8,128)(2,1)S(1)}, u32[]{:S(2)}, u32[]{:S(2)}) %collective-permute-start.8) | collective-permute-done | bytes 262176 | tf_op jit(solution)/shard_map/ppermute | solution.py:66
  49.7 4.3 %backward.1 = (f32[224,8,128]{2,1,0:T(8,128)S(1)}, f32[224,8,128]{2,1,0:T(8,128)S(1)}) custom-call(s32[3]{0:T(128)S(1)} %pad_add_fusion.pos_ref.pos, bf16[4,128,256]{2,1,0:T(8,128)(2,1)S(1)} %collective-permute-done.7.near.i0, bf16[4,128,256]{2,1,0:T(8,128)(2,1)S(1)} %get-tuple-element.40.first.i1, bf16[4,128,256]{2,1,0:T(8,128)(2,1)S(1)} %get-tuple-element.41.second.i2, ...), custom_call_target="tpu_custom_call" | custom-call | flops 5798205952 | bytes 10485760 | tf_op jit(solution)/shard_map/backward/pallas_call | solution.py:401
  54.0 0.1 collective-permute-start.9
  54.1 2.5 %collective-permute-done.9.received = f32[224,8,128]{2,1,0:T(8,128)S(1)} collective-permute-done((f32[224,8,128]{2,1,0:T(8,128)S(1)}, f32[224,8,128]{2,1,0:T(8,128)S(1)}, u32[]{:S(2)}, u32[]{:S(2)}) %collective-permute-start.9) | collective-permute-done | bytes 917536 | tf_op jit(solution)/shard_map/ppermute | solution.py:43
  56.6 0.8 encode_terms.1
  57.4 29.9 %all_to_all.10.pieces = bf16[32,64,128]{2,1,0:T(8,128)(2,1)S(1)} all-to-all(bf16[32,64,128]{2,1,0:T(8,128)(2,1)S(1)} %encode_terms.1), channel_id=1, replica_groups=mesh['yh'=2,'z'=8,'yl'=2,'c'=2,'x'=4] {'yh','z','yl'}, dimensions={0} | all-to-all | bytes 1048576 | tf_op jit(solution)/shard_map/all_to_all | solution.py:564
  87.3 0.4 recode.1
  87.7 11.0 %all_to_all.11 = bf16[8,64,128]{2,1,0:T(8,128)(2,1)S(1)} all-to-all(bf16[8,64,128]{2,1,0:T(8,128)(2,1)S(1)} %recode.1), channel_id=1, replica_groups=mesh['yh'=2,'z'=8,'yl'=2,'c'=2,'x'=4] {'z'}, dimensions={0} | all-to-all | bytes 262144 | tf_op jit(solution)/shard_map/all_to_all | solution.py:565
  98.7 1.2 collective-permute-start.12
  99.9 1.4 collective-permute-start.11
  101.3 0.1 collective-permute-start.10
  101.4 2.6 %collective-permute-done.12 = bf16[8,64,128]{2,1,0:T(8,128)(2,1)S(1)} collective-permute-done((bf16[8,64,128]{2,1,0:T(8,128)(2,1)S(1)}, bf16[8,64,128]{2,1,0:T(8,128)(2,1)S(1)}, u32[]{:S(2)}, u32[]{:S(2)}) %collective-permute-start.12) | collective-permute-done | bytes 131104 | tf_op jit(solution)/shard_map/ppermute | solution.py:43
  104.0 0.0 collective-permute-done.11
  104.0 2.6 %collective-permute-done.10 = bf16[8,64,128]{2,1,0:T(8,128)(2,1)S(1)} collective-permute-done((bf16[8,64,128]{2,1,0:T(8,128)(2,1)S(1)}, bf16[8,64,128]{2,1,0:T(8,128)(2,1)S(1)}, u32[]{:S(2)}, u32[]{:S(2)}) %collective-permute-start.10) | collective-permute-done | bytes 131104 | tf_op jit(solution)/shard_map/ppermute | solution.py:43
  106.6 0.1 pad_maximum_fusion.1
  106.6 2.2 %collective-permute-start.14 = (bf16[32,64,128]{2,1,0:T(8,128)(2,1)S(1)}, bf16[32,64,128]{2,1,0:T(8,128)(2,1)S(1)}, u32[]{:S(2)}, u32[]{:S(2)}) collective-permute-start(bf16[32,64,128]{2,1,0:T(8,128)(2,1)S(1)} %bitcast.39), channel_id=1, source_target_pairs={{0,136},{1,137},{2,138},{3,139},{4,7},{5,4},{6,5},{7,6},{8,0},{9,1... | collective-permute-start | bytes 1572872 | tf_op jit(solution)/shard_map/ppermute | solution.py:43
  108.8 0.0 collective-permute-start.13
  108.8 6.2 %collective-permute-done.14 = bf16[32,64,128]{2,1,0:T(8,128)(2,1)S(1)} collective-permute-done((bf16[32,64,128]{2,1,0:T(8,128)(2,1)S(1)}, bf16[32,64,128]{2,1,0:T(8,128)(2,1)S(1)}, u32[]{:S(2)}, u32[]{:S(2)}) %collective-permute-start.14) | collective-permute-done | bytes 524320 | tf_op jit(solution)/shard_map/ppermute | solution.py:43
  115.1 3.4 %collective-permute-start.16 = (bf16[16,64,128]{2,1,0:T(8,128)(2,1)S(1)}, bf16[16,64,128]{2,1,0:T(8,128)(2,1)S(1)}, u32[]{:S(2)}, u32[]{:S(2)}) collective-permute-start(bf16[16,64,128]{2,1,0:T(8,128)(2,1)S(1)} %slice.17), channel_id=1, source_target_pairs={{0,136},{1,137},{2,138},{3,139},{4,7},{5,4},{6,5},{7,6},{8,0},{9,1... | collective-permute-start | bytes 786440 | tf_op jit(solution)/shard_map/ppermute | solution.py:43
  118.4 0.0 collective-permute-done.13
  118.5 0.1 collective-permute-start.15
  118.6 3.2 %collective-permute-done.16 = bf16[16,64,128]{2,1,0:T(8,128)(2,1)S(1)} collective-permute-done((bf16[16,64,128]{2,1,0:T(8,128)(2,1)S(1)}, bf16[16,64,128]{2,1,0:T(8,128)(2,1)S(1)}, u32[]{:S(2)}, u32[]{:S(2)}) %collective-permute-start.16) | collective-permute-done | bytes 262176 | tf_op jit(solution)/shard_map/ppermute | solution.py:43
  121.8 3.2 %collective-permute-done.15 = bf16[16,64,128]{2,1,0:T(8,128)(2,1)S(1)} collective-permute-done((bf16[16,64,128]{2,1,0:T(8,128)(2,1)S(1)}, bf16[16,64,128]{2,1,0:T(8,128)(2,1)S(1)}, u32[]{:S(2)}, u32[]{:S(2)}) %collective-permute-start.15) | collective-permute-done | bytes 262176 | tf_op jit(solution)/shard_map/ppermute | solution.py:43
  125.0 0.3 pad_maximum_fusion
  125.3 5.4 %collective-permute-start.17 = (bf16[16,8,64,128]{3,2,1,0:T(8,128)(2,1)S(1)}, bf16[16,8,64,128]{3,2,1,0:T(8,128)(2,1)S(1)}, u32[]{:S(2)}, u32[]{:S(2)}) collective-permute-start(bf16[16,8,64,128]{3,2,1,0:T(8,128)(2,1)S(1)} %bitcast.31), channel_id=1, source_target_pairs={{0,4},{1,5},{2,6},{3,7},{4,0},{5,1},{6,2},{7,3},{8,12},{9,13},{10,... | collective-permute-start | bytes 6291464 | tf_op jit(solution)/shard_map/ppermute | solution.py:43
  130.7 3.8 %collective-permute-done.17.other = bf16[16,8,64,128]{3,2,1,0:T(8,128)(2,1)S(1)} collective-permute-done((bf16[16,8,64,128]{3,2,1,0:T(8,128)(2,1)S(1)}, bf16[16,8,64,128]{3,2,1,0:T(8,128)(2,1)S(1)}, u32[]{:S(2)}, u32[]{:S(2)}) %collective-permute-start.17) | collective-permute-done | bytes 2097184 | tf_op jit(solution)/shard_map/ppermute | solution.py:43
  134.5 4.8 %assemble.1 = (f32[27,4,8,8,256]{4,3,2,1,0:T(8,128)}, f32[16,256]{1,0:T(8,128)S(1)}) custom-call(s32[3]{0:T(128)S(1)} %pad_add_fusion.pos_ref.pos, bf16[16,8,64,128]{3,2,1,0:T(8,128)(2,1)S(1)} %bitcast.32, bf16[16,8,64,128]{3,2,1,0:T(8,128)(2,1)S(1)} %collective-permute-done.17.other), custom_call_target="tpu_custom_call" | custom-call | flops 1000000 | bytes 15728640 | tf_op jit(solution)/shard_map/assemble/pallas_call | solution.py:508
  139.3 0.6 fusion
  (7 shorter events, 0.1 us)
Async XLA Ops:
  0.6 12.0 %collective-permute-start.2 = (bf16[2,128,256]{2,1,0:T(8,128)(2,1)}, bf16[2,128,256]{2,1,0:T(8,128)(2,1)}, u32[]{:S(2)}, u32[]{:S(2)}) collective-permute-start(bf16[2,128,256]{2,1,0:T(8,128)(2,1)} %bitcast.33), channel_id=1, source_target_pairs={{0,2},{1,3},{2,0},{3,1},{4,6},{5,7},{6,4},{7,5},{8,10},{9,11},{10,... | collective-permute-start | bytes 393224 | tf_op jit(solution)/shard_map/ppermute | solution.py:43
  4.3 8.4 %collective-permute-start.1 = (bf16[2,128,256]{2,1,0:T(8,128)(2,1)}, bf16[2,128,256]{2,1,0:T(8,128)(2,1)}, u32[]{:S(2)}, u32[]{:S(2)}) collective-permute-start(bf16[2,128,256]{2,1,0:T(8,128)(2,1)} %bitcast.34), channel_id=1, source_target_pairs={{0,3},{1,0},{2,1},{3,2},{4,7},{5,4},{6,5},{7,6},{8,11},{9,8},{10,9... | collective-permute-start | bytes 393224 | tf_op jit(solution)/shard_map/ppermute | solution.py:43
  5.1 7.7 %collective-permute-start = (bf16[2,128,256]{2,1,0:T(8,128)(2,1)}, bf16[2,128,256]{2,1,0:T(8,128)(2,1)}, u32[]{:S(2)}, u32[]{:S(2)}) collective-permute-start(bf16[2,128,256]{2,1,0:T(8,128)(2,1)} %bitcast.35), channel_id=1, source_target_pairs={{0,1},{1,2},{2,3},{3,0},{4,5},{5,6},{6,7},{7,4},{8,9},{9,10},{10,1... | collective-permute-start | bytes 393224 | tf_op jit(solution)/shard_map/ppermute | solution.py:43
  5.7 2.0 %copy-start.3 = (bf16[3,3,3,256,256]{4,3,2,1,0:T(8,128)(2,1)S(1)}, bf16[3,3,3,256,256]{4,3,2,1,0:T(8,128)(2,1)}, u32[]{:S(2)}) copy-start(bf16[3,3,3,256,256]{4,3,2,1,0:T(8,128)(2,1)} %weight.1) | copy-start | bytes 10616836
  7.7 0.7 copy-start.4
  8.4 0.7 copy-start.5
  10.8 1.8 %copy-start = (bf16[3,3,3,256,256]{4,3,2,1,0:T(8,128)(2,1)}, bf16[3,3,3,256,256]{4,3,2,1,0:T(8,128)(2,1)S(1)}, u32[]{:S(2)}) copy-start(bf16[3,3,3,256,256]{4,3,2,1,0:T(8,128)(2,1)S(1)} %get-tuple-element.37) | copy-start | bytes 10616836
  12.8 0.9 copy-start.2
  14.9 6.8 %collective-permute-start.4 = (bf16[4,128,256]{2,1,0:T(8,128)(2,1)S(1)}, bf16[4,128,256]{2,1,0:T(8,128)(2,1)S(1)}, u32[]{:S(2)}, u32[]{:S(2)}) collective-permute-start(bf16[4,128,256]{2,1,0:T(8,128)(2,1)S(1)} %get-tuple-element.28), channel_id=1, source_target_pairs={{0,4},{1,5},{2,6},{3,7},{4,0},{5,1},{6,2},{7,3},{8,12},{9,13},{10,... | collective-permute-start | bytes 786440 | tf_op jit(solution)/shard_map/ppermute | solution.py:43
  16.3 9.2 %collective-permute-start.3 = (bf16[4,128,256]{2,1,0:T(8,128)(2,1)S(1)}, bf16[4,128,256]{2,1,0:T(8,128)(2,1)S(1)}, u32[]{:S(2)}, u32[]{:S(2)}) collective-permute-start(bf16[4,128,256]{2,1,0:T(8,128)(2,1)S(1)} %get-tuple-element.27), channel_id=1, source_target_pairs={{4,8},{8,4},{12,16},{16,12},{20,24},{24,20},{28,32},{32,28},{36,40... | collective-permute-start | bytes 786440 | tf_op jit(solution)/shard_map/ppermute | solution.py:66
  25.5 6.2 %copy-start.1 = (bf16[3,3,3,256,256]{4,3,2,1,0:T(8,128)(2,1)S(1)}, bf16[3,3,3,256,256]{4,3,2,1,0:T(8,128)(2,1)}, u32[]{:S(2)}) copy-start(bf16[3,3,3,256,256]{4,3,2,1,0:T(8,128)(2,1)} %copy-done) | copy-start | bytes 10616836
  27.2 6.8 %collective-permute-start.6 = (bf16[4,128,256]{2,1,0:T(8,128)(2,1)S(1)}, bf16[4,128,256]{2,1,0:T(8,128)(2,1)S(1)}, u32[]{:S(2)}, u32[]{:S(2)}) collective-permute-start(bf16[4,128,256]{2,1,0:T(8,128)(2,1)S(1)} %get-tuple-element.34), channel_id=1, source_target_pairs={{0,4},{1,5},{2,6},{3,7},{4,0},{5,1},{6,2},{7,3},{8,12},{9,13},{10,... | collective-permute-start | bytes 786440 | tf_op jit(solution)/shard_map/ppermute | solution.py:43
  27.3 10.5 %collective-permute-start.5 = (bf16[4,128,256]{2,1,0:T(8,128)(2,1)S(1)}, bf16[4,128,256]{2,1,0:T(8,128)(2,1)S(1)}, u32[]{:S(2)}, u32[]{:S(2)}) collective-permute-start(bf16[4,128,256]{2,1,0:T(8,128)(2,1)S(1)} %get-tuple-element.33), channel_id=1, source_target_pairs={{4,8},{8,4},{12,16},{16,12},{20,24},{24,20},{28,32},{32,28},{36,40... | collective-permute-start | bytes 786440 | tf_op jit(solution)/shard_map/ppermute | solution.py:66
  39.1 6.9 %collective-permute-start.7 = (bf16[4,128,256]{2,1,0:T(8,128)(2,1)S(1)}, bf16[4,128,256]{2,1,0:T(8,128)(2,1)S(1)}, u32[]{:S(2)}, u32[]{:S(2)}) collective-permute-start(bf16[4,128,256]{2,1,0:T(8,128)(2,1)S(1)} %get-tuple-element.39), channel_id=1, source_target_pairs={{0,4},{1,5},{2,6},{3,7},{4,0},{5,1},{6,2},{7,3},{8,12},{9,13},{10,... | collective-permute-start | bytes 786440 | tf_op jit(solution)/shard_map/ppermute | solution.py:43
  39.2 10.5 %collective-permute-start.8 = (bf16[4,128,256]{2,1,0:T(8,128)(2,1)S(1)}, bf16[4,128,256]{2,1,0:T(8,128)(2,1)S(1)}, u32[]{:S(2)}, u32[]{:S(2)}) collective-permute-start(bf16[4,128,256]{2,1,0:T(8,128)(2,1)S(1)} %get-tuple-element.42), channel_id=1, source_target_pairs={{4,8},{8,4},{12,16},{16,12},{20,24},{24,20},{28,32},{32,28},{36,40... | collective-permute-start | bytes 786440 | tf_op jit(solution)/shard_map/ppermute | solution.py:66
  54.0 2.6 %collective-permute-start.9 = (f32[224,8,128]{2,1,0:T(8,128)S(1)}, f32[224,8,128]{2,1,0:T(8,128)S(1)}, u32[]{:S(2)}, u32[]{:S(2)}) collective-permute-start(f32[224,8,128]{2,1,0:T(8,128)S(1)} %get-tuple-element.46), channel_id=1, source_target_pairs={{0,4},{1,5},{2,6},{3,7},{4,0},{5,1},{6,2},{7,3},{8,12},{9,13},{10,... | collective-permute-start | bytes 2752520 | tf_op jit(solution)/shard_map/ppermute | solution.py:43
  98.7 5.3 %collective-permute-start.12 = (bf16[8,64,128]{2,1,0:T(8,128)(2,1)S(1)}, bf16[8,64,128]{2,1,0:T(8,128)(2,1)S(1)}, u32[]{:S(2)}, u32[]{:S(2)}) collective-permute-start(bf16[8,64,128]{2,1,0:T(8,128)(2,1)S(1)} %all_to_all.11), channel_id=1, source_target_pairs={{0,2},{1,3},{2,0},{3,1},{4,132},{5,133},{6,134},{7,135},{8,10},{9,... | collective-permute-start | bytes 393224 | tf_op jit(solution)/shard_map/ppermute | solution.py:43
  99.9 4.1 %collective-permute-start.11 = (bf16[8,64,128]{2,1,0:T(8,128)(2,1)S(1)}, bf16[8,64,128]{2,1,0:T(8,128)(2,1)S(1)}, u32[]{:S(2)}, u32[]{:S(2)}) collective-permute-start(bf16[8,64,128]{2,1,0:T(8,128)(2,1)S(1)} %all_to_all.11), channel_id=1, source_target_pairs={{0,3},{1,0},{2,1},{3,2},{4,140},{5,141},{6,142},{7,143},{8,11},{9,... | collective-permute-start | bytes 393224 | tf_op jit(solution)/shard_map/ppermute | solution.py:43
  101.3 5.3 %collective-permute-start.10 = (bf16[8,64,128]{2,1,0:T(8,128)(2,1)S(1)}, bf16[8,64,128]{2,1,0:T(8,128)(2,1)S(1)}, u32[]{:S(2)}, u32[]{:S(2)}) collective-permute-start(bf16[8,64,128]{2,1,0:T(8,128)(2,1)S(1)} %all_to_all.11), channel_id=1, source_target_pairs={{0,1},{1,2},{2,3},{3,0},{4,12},{5,13},{6,14},{7,15},{8,9},{9,10},{... | collective-permute-start | bytes 393224 | tf_op jit(solution)/shard_map/ppermute | solution.py:43
  106.6 8.4 %collective-permute-start.14 = (bf16[32,64,128]{2,1,0:T(8,128)(2,1)S(1)}, bf16[32,64,128]{2,1,0:T(8,128)(2,1)S(1)}, u32[]{:S(2)}, u32[]{:S(2)}) collective-permute-start(bf16[32,64,128]{2,1,0:T(8,128)(2,1)S(1)} %bitcast.39), channel_id=1, source_target_pairs={{0,136},{1,137},{2,138},{3,139},{4,7},{5,4},{6,5},{7,6},{8,0},{9,1... | collective-permute-start | bytes 1572872 | tf_op jit(solution)/shard_map/ppermute | solution.py:43
  108.8 9.6 %collective-permute-start.13 = (bf16[32,64,128]{2,1,0:T(8,128)(2,1)S(1)}, bf16[32,64,128]{2,1,0:T(8,128)(2,1)S(1)}, u32[]{:S(2)}, u32[]{:S(2)}) collective-permute-start(bf16[32,64,128]{2,1,0:T(8,128)(2,1)S(1)} %bitcast.40), channel_id=1, source_target_pairs={{0,8},{1,9},{2,10},{3,11},{4,5},{5,6},{6,7},{7,4},{8,128},{9,129},... | collective-permute-start | bytes 1572872 | tf_op jit(solution)/shard_map/ppermute | solution.py:43
  115.1 6.7 %collective-permute-start.16 = (bf16[16,64,128]{2,1,0:T(8,128)(2,1)S(1)}, bf16[16,64,128]{2,1,0:T(8,128)(2,1)S(1)}, u32[]{:S(2)}, u32[]{:S(2)}) collective-permute-start(bf16[16,64,128]{2,1,0:T(8,128)(2,1)S(1)} %slice.17), channel_id=1, source_target_pairs={{0,136},{1,137},{2,138},{3,139},{4,7},{5,4},{6,5},{7,6},{8,0},{9,1... | collective-permute-start | bytes 786440 | tf_op jit(solution)/shard_map/ppermute | solution.py:43
  118.5 6.5 %collective-permute-start.15 = (bf16[16,64,128]{2,1,0:T(8,128)(2,1)S(1)}, bf16[16,64,128]{2,1,0:T(8,128)(2,1)S(1)}, u32[]{:S(2)}, u32[]{:S(2)}) collective-permute-start(bf16[16,64,128]{2,1,0:T(8,128)(2,1)S(1)} %slice.16), channel_id=1, source_target_pairs={{0,8},{1,9},{2,10},{3,11},{4,5},{5,6},{6,7},{7,4},{8,128},{9,129},... | collective-permute-start | bytes 786440 | tf_op jit(solution)/shard_map/ppermute | solution.py:43
  125.3 9.2 %collective-permute-start.17 = (bf16[16,8,64,128]{3,2,1,0:T(8,128)(2,1)S(1)}, bf16[16,8,64,128]{3,2,1,0:T(8,128)(2,1)S(1)}, u32[]{:S(2)}, u32[]{:S(2)}) collective-permute-start(bf16[16,8,64,128]{3,2,1,0:T(8,128)(2,1)S(1)} %bitcast.31), channel_id=1, source_target_pairs={{0,4},{1,5},{2,6},{3,7},{4,0},{5,1},{6,2},{7,3},{8,12},{9,13},{10,... | collective-permute-start | bytes 6291464 | tf_op jit(solution)/shard_map/ppermute | solution.py:43
